TPU v7x, 128 devices: a whole 4x4x4 slice. The times are simulated.
128 devices in a mesh: col: 16 (over x, z), row: 8 (over y, core).
Axes of the slice: x: 4, y: 4, z: 4, core: 2. Of those that a mesh axis runs over, the one named last changes fastest.
Arguments:
- position: float32 [128, 65536], P(None, ('col', 'row')), may hold values from -6 to 6
- momentum: float32 [128, 65536], P(None, ('col', 'row')), may hold values from -6 to 6
- row_factors: bfloat16 [65536, 64, 128], P(('col', 'row')), may hold values from -1 to 1
- col_factors: bfloat16 [65536, 64, 128], P(('col', 'row')), may hold values from -1 to 1
- tile_ranks: int32 [64, 64], replicated, may hold values from 16 to 128, as said below
- log_mean: float32 [65536], P(('col', 'row')), may hold values from -0.5 to 0.5
- counts: int32 [65536], P(('col', 'row')), may hold values from 0 to 11
- step_size: float32 [128], replicated, may hold values from 0.1 to 0.3
Outputs:
- new_position: float32 [128, 65536], P(None, ('col', 'row'))
- new_momentum: float32 [128, 65536], P(None, ('col', 'row'))
- energy_change: float32 [128], replicated
Inputs may be any that keep to these rules, and one draw needn't show every extreme that they name: `tile_ranks`: every entry is a multiple of 16; in every draw some tile has rank 16 and some tile has rank 128.
All inputs are finite; a program needn't handle non-finite values.
Results may differ from a plain program's by a relative error of at most 0.004.
Values may be sent and summed in bfloat16 or wider, within the bound.
No kernel may reach another device: no remote copies, remote signals or barrier semaphores. Data moves between devices by JAX's collectives and lax.ppermute only.
A program may use at most 128 MiB of HBM per device.

v0:
```python
import functools

import jax
import jax.numpy as jnp
from jax import lax
from jax.sharding import Mesh
from jax.sharding import PartitionSpec as P

COL_ROW = ("col_0", "col_1", "row_0", "row_1")
ROW = ("row_0", "row_1")


def partner_2(value, axis, stride):
    mask = 2**stride
    pairs = [(source, source ^ mask) for source in range(lax.axis_size(axis))]
    return lax.ppermute(value, axis, pairs)


def over_axes(value, axes):
    return functools.reduce(lax.psum, axes, value)


def on_device(
    position, momentum, row_factors, col_factors, tile_ranks, log_mean, counts, step_size
):
    chains = position.shape[0]
    tile_count = tile_ranks.shape[0]
    ranked = row_factors.shape[2]
    device = lax.axis_index(COL_ROW)
    own_tile = device // 2
    own_half = device % 2
    levels = jnp.arange(ranked, dtype=jnp.int32)
    col_ranks = lax.dynamic_slice_in_dim(tile_ranks, own_tile, 1, 1)[:, 0]
    row_ranks = lax.dynamic_slice_in_dim(tile_ranks, own_tile, 1, 0)[0]
    col_live = (levels[None, :] < col_ranks[:, None]).astype(jnp.float32)[:, :, None]
    row_live = (levels[None, :] < row_ranks[:, None]).astype(jnp.float32)[:, :, None]
    rate_base = counts.astype(jnp.float32)[None, :]

    def deliver(partial_value):
        halved = partial_value.reshape(2 * tile_count, ranked // 2, chains)
        arrived = lax.all_to_all(halved, COL_ROW, split_axis=0, concat_axis=0, tiled=True)
        summed = arrived.reshape(tile_count, 2, ranked // 2, chains).astype(jnp.float32).sum(axis=1)
        summed = summed.astype(jnp.bfloat16)
        partner = partner_2(summed, ROW, 0)
        lower_first = jnp.concatenate([summed, partner], axis=1)
        upper_first = jnp.concatenate([partner, summed], axis=1)
        return jnp.where(own_half == 0, lower_first, upper_first)

    def gradient(values):
        rounded = values.astype(jnp.bfloat16)
        partial_value = jnp.einsum(
            "yik,hy->ikh", col_factors, rounded, preferred_element_type=jnp.float32
        )
        partial_value = (partial_value * col_live).astype(jnp.bfloat16)
        coefficient = deliver(partial_value)
        latent_field = jnp.einsum(
            "xjk,jkh->hx", row_factors, coefficient, preferred_element_type=jnp.float32
        )
        exponent = log_mean[None, :] + latent_field
        intensity = jnp.exp(exponent)
        residual = rate_base - intensity
        adjoint = jnp.einsum(
            "xjk,hx->jkh",
            row_factors,
            residual.astype(jnp.bfloat16),
            preferred_element_type=jnp.float32,
        )
        adjoint = (adjoint * row_live).astype(jnp.bfloat16)
        returned = deliver(adjoint)
        pulled = jnp.einsum(
            "yik,ikh->hy", col_factors, returned, preferred_element_type=jnp.float32
        )
        energy = jnp.sum(intensity - rate_base * exponent + 0.5 * values * values, axis=1)
        return (values - pulled, energy)

    full_step = step_size[:, None]

    def leapfrog(section, carry):
        shifted, moment, start_energy, end_energy = carry
        forces, energy = gradient(shifted)
        weight = jnp.where(section == 1, 1.0, 0.5).astype(jnp.float32)
        moment = moment - weight * full_step * forces
        advance = jnp.where(section < 2, full_step * moment, jnp.zeros_like(moment))
        shifted = shifted + advance
        start_energy = jnp.where(section == 0, energy, start_energy)
        end_energy = jnp.where(section == 2, energy, end_energy)
        return (shifted, moment, start_energy, end_energy)

    empty = jnp.zeros((chains,), jnp.float32)
    shifted, moment, start_energy, end_energy = lax.fori_loop(
        0, 3, leapfrog, (position, momentum, empty, empty)
    )
    kinetic = 0.5 * jnp.sum(moment * moment - momentum * momentum, axis=1)
    change = over_axes(end_energy - start_energy + kinetic, COL_ROW)
    return (shifted, moment, change)


def solution(mesh):
    split = Mesh(mesh.devices.reshape(4, 4, 4, 2), ("col_0", "col_1", "row_0", "row_1"))
    return jax.shard_map(
        on_device,
        mesh=split,
        in_specs=(
            P(None, COL_ROW),
            P(None, COL_ROW),
            P(COL_ROW, None, None),
            P(COL_ROW, None, None),
            P(),
            P(COL_ROW),
            P(COL_ROW),
            P(),
        ),
        out_specs=(P(None, COL_ROW), P(None, COL_ROW), P()),
        check_vma=False,
    )
```

profile of v0, /device:TPU:1, one launch (start us, length us, event | category | flops | bytes accessed | tf_op | source)
XLA Modules:
  0.0 342.8 jit_solution(5153014258483212270)
XLA Ops:
  0.7 0.7 copy-done
  1.4 0.2 dynamic-slice_reduce_fusion
  1.6 12.0 %copy.23 = bf16[512,64,128]{2,0,1:T(8,128)(2,1)} copy(bf16[512,64,128]{2,1,0:T(8,128)(2,1)} %param.13) | data formatting | bytes 16777216
  13.6 13.0 %copy.24 = bf16[512,64,128]{0,2,1:T(8,128)(2,1)} copy(bf16[512,64,128]{2,1,0:T(8,128)(2,1)} %param.12) | data formatting | bytes 16777216
  26.7 287.1 %while.23 = (s32[]{:T(128)}, f32[128,512]{1,0:T(8,128)S(1)}, f32[128,512]{1,0:T(8,128)S(1)}, f32[128]{0:T(128)S(1)}, f32[128]{0:T(128)S(1)}, /*index=5*/f32[128,...) while((s32[]{:T(128)}, f32[128,512]{1,0:T(8,128)S(1)}, ...), condition=%wide.region_4.5_spmd.clone, body=%wide.region_0.4_spmd.clone.sunk | while | flops 4320166400 | bytes 109195080 | solution.py:90
  26.8 5.8 %multiply_convert_fusion.4 = bf16[64,128,128]{2,1,0:T(8,128)(2,1)S(1)} fusion(bf16[512,64,128]{2,0,1:T(8,128)(2,1)} %get-tuple-element.606, f32[64,128]{1,0:T(8,128)S(1)} %convert_bitcast_fusion.4, f32[128,512]{1,0:T(8,128)S(1)} %get-tuple-element.580), kind=kOutput, calls=%fused_computation.3.clone.1 | convolution fusion | flops 1075904512 | bytes 10780672 | tf_op jit(solution)/shard_map/while/body/eval_jaxpr/yik,hy->ikh/dot_general | solution.py:51
  32.6 41.5 %all_to_all.30 = bf16[128,64,128]{2,1,0:T(8,128)(2,1)S(1)} all-to-all(bf16[128,64,128]{2,1,0:T(8,128)(2,1)S(1)} %bitcast.74), channel_id=1, replica_groups=mesh['col_0'=4,'col_1'=4,'row_0'=4,'row_1'=2] {'col_0','col_1','row_0','..., dimensions={0} | all-to-all | bytes 4194304 | tf_op jit(solution)/shard_map/while/body/eval_jaxpr/all_to_all | solution.py:41
  74.1 0.5 bitcast_reduce_fusion.4
  74.6 1.3 collective-permute-start
  76.0 2.2 collective-permute-done
  78.2 1.3 fusion.49
  79.5 2.4 fusion.50
  81.9 1.5 multiply_convert_fusion.5
  83.4 33.7 %all_to_all.31 = bf16[128,64,128]{2,1,0:T(8,128)(2,1)S(1)} all-to-all(bf16[128,64,128]{2,1,0:T(8,128)(2,1)S(1)} %bitcast.77), channel_id=1, replica_groups=mesh['col_0'=4,'col_1'=4,'row_0'=4,'row_1'=2] {'col_0','col_1','row_0','..., dimensions={0} | all-to-all | bytes 4194304 | tf_op jit(solution)/shard_map/while/body/eval_jaxpr/all_to_all | solution.py:41
  117.1 0.5 bitcast_reduce_fusion.5
  117.6 1.3 collective-permute-start.1
  118.9 2.3 collective-permute-done.1
  121.2 6.4 %fusion.51 = (f32[128]{0:T(128)S(1)}, f32[128,512]{1,0:T(8,128)S(1)}, f32[128,512]{1,0:T(8,128)S(1)}) fusion(f32[128,512]{1,0:T(8,128)S(1)} %get-tuple-element.580, f32[128,512]{1,0:T(8,128)S(1)} %fusion.49, f32[512]{0:T(512)S(1)} %bitcast.80, f32[128]{0:T(128)S(1)} %bitcast.82, pred[]{:T(512)S(6)} %lt.137, f32[128,512]{1,0:T(8,128)S(1)} %get-tuple-element.581, ...), kind=kOutput, calls=%fused_computation.30.clone.1 | convolution fusion | flops 1083965312 | bytes 11800066 | tf_op jit(solution)/shard_map/while/body/eval_jaxpr/yik,ikh->hy/dot_general | solution.py:70
  127.7 5.8 %multiply_convert_fusion.4 = bf16[64,128,128]{2,1,0:T(8,128)(2,1)S(1)} fusion(bf16[512,64,128]{2,0,1:T(8,128)(2,1)} %get-tuple-element.606, f32[64,128]{1,0:T(8,128)S(1)} %convert_bitcast_fusion.4, f32[128,512]{1,0:T(8,128)S(1)} %get-tuple-element.580), kind=kOutput, calls=%fused_computation.3.clone.1 | convolution fusion | flops 1075904512 | bytes 10780672 | tf_op jit(solution)/shard_map/while/body/eval_jaxpr/yik,hy->ikh/dot_general | solution.py:51
  133.5 33.7 %all_to_all.30 = bf16[128,64,128]{2,1,0:T(8,128)(2,1)S(1)} all-to-all(bf16[128,64,128]{2,1,0:T(8,128)(2,1)S(1)} %bitcast.74), channel_id=1, replica_groups=mesh['col_0'=4,'col_1'=4,'row_0'=4,'row_1'=2] {'col_0','col_1','row_0','..., dimensions={0} | all-to-all | bytes 4194304 | tf_op jit(solution)/shard_map/while/body/eval_jaxpr/all_to_all | solution.py:41
  167.2 0.5 bitcast_reduce_fusion.4
  167.7 1.3 collective-permute-start
  169.1 2.2 collective-permute-done
  171.3 1.3 fusion.49
  172.6 2.4 fusion.50
  175.0 1.5 multiply_convert_fusion.5
  176.5 33.7 %all_to_all.31 = bf16[128,64,128]{2,1,0:T(8,128)(2,1)S(1)} all-to-all(bf16[128,64,128]{2,1,0:T(8,128)(2,1)S(1)} %bitcast.77), channel_id=1, replica_groups=mesh['col_0'=4,'col_1'=4,'row_0'=4,'row_1'=2] {'col_0','col_1','row_0','..., dimensions={0} | all-to-all | bytes 4194304 | tf_op jit(solution)/shard_map/while/body/eval_jaxpr/all_to_all | solution.py:41
  210.2 0.5 bitcast_reduce_fusion.5
  210.7 1.3 collective-permute-start.1
  212.0 2.3 collective-permute-done.1
  214.3 6.4 %fusion.51 = (f32[128]{0:T(128)S(1)}, f32[128,512]{1,0:T(8,128)S(1)}, f32[128,512]{1,0:T(8,128)S(1)}) fusion(f32[128,512]{1,0:T(8,128)S(1)} %get-tuple-element.580, f32[128,512]{1,0:T(8,128)S(1)} %fusion.49, f32[512]{0:T(512)S(1)} %bitcast.80, f32[128]{0:T(128)S(1)} %bitcast.82, pred[]{:T(512)S(6)} %lt.137, f32[128,512]{1,0:T(8,128)S(1)} %get-tuple-element.581, ...), kind=kOutput, calls=%fused_computation.30.clone.1 | convolution fusion | flops 1083965312 | bytes 11800066 | tf_op jit(solution)/shard_map/while/body/eval_jaxpr/yik,ikh->hy/dot_general | solution.py:70
  220.8 5.8 %multiply_convert_fusion.4 = bf16[64,128,128]{2,1,0:T(8,128)(2,1)S(1)} fusion(bf16[512,64,128]{2,0,1:T(8,128)(2,1)} %get-tuple-element.606, f32[64,128]{1,0:T(8,128)S(1)} %convert_bitcast_fusion.4, f32[128,512]{1,0:T(8,128)S(1)} %get-tuple-element.580), kind=kOutput, calls=%fused_computation.3.clone.1 | convolution fusion | flops 1075904512 | bytes 10780672 | tf_op jit(solution)/shard_map/while/body/eval_jaxpr/yik,hy->ikh/dot_general | solution.py:51
  226.6 33.7 %all_to_all.30 = bf16[128,64,128]{2,1,0:T(8,128)(2,1)S(1)} all-to-all(bf16[128,64,128]{2,1,0:T(8,128)(2,1)S(1)} %bitcast.74), channel_id=1, replica_groups=mesh['col_0'=4,'col_1'=4,'row_0'=4,'row_1'=2] {'col_0','col_1','row_0','..., dimensions={0} | all-to-all | bytes 4194304 | tf_op jit(solution)/shard_map/while/body/eval_jaxpr/all_to_all | solution.py:41
  260.3 0.5 bitcast_reduce_fusion.4
  260.8 1.3 collective-permute-start
  262.2 2.2 collective-permute-done
  264.4 1.3 fusion.49
  265.8 2.4 fusion.50
  268.1 1.5 multiply_convert_fusion.5
  269.6 33.7 %all_to_all.31 = bf16[128,64,128]{2,1,0:T(8,128)(2,1)S(1)} all-to-all(bf16[128,64,128]{2,1,0:T(8,128)(2,1)S(1)} %bitcast.77), channel_id=1, replica_groups=mesh['col_0'=4,'col_1'=4,'row_0'=4,'row_1'=2] {'col_0','col_1','row_0','..., dimensions={0} | all-to-all | bytes 4194304 | tf_op jit(solution)/shard_map/while/body/eval_jaxpr/all_to_all | solution.py:41
  303.3 0.5 bitcast_reduce_fusion.5
  303.8 1.3 collective-permute-start.1
  305.2 2.3 collective-permute-done.1
  307.4 6.4 %fusion.51 = (f32[128]{0:T(128)S(1)}, f32[128,512]{1,0:T(8,128)S(1)}, f32[128,512]{1,0:T(8,128)S(1)}) fusion(f32[128,512]{1,0:T(8,128)S(1)} %get-tuple-element.580, f32[128,512]{1,0:T(8,128)S(1)} %fusion.49, f32[512]{0:T(512)S(1)} %bitcast.80, f32[128]{0:T(128)S(1)} %bitcast.82, pred[]{:T(512)S(6)} %lt.137, f32[128,512]{1,0:T(8,128)S(1)} %get-tuple-element.581, ...), kind=kOutput, calls=%fused_computation.30.clone.1 | convolution fusion | flops 1083965312 | bytes 11800066 | tf_op jit(solution)/shard_map/while/body/eval_jaxpr/yik,ikh->hy/dot_general | solution.py:70
  314.0 6.9 %psum.28 = f32[128]{0:T(128)S(1)} all-reduce(f32[128]{0:T(128)S(1)} %multiply_add_fusion), channel_id=1, replica_groups=mesh['col_0'=4,'col_1'=4,'row_0'=4,'row_1'=2] {'col_0'}, use_global_device_ids=true, to_apply=%region_6.7 | all-reduce | flops 128 | bytes 1024 | tf_op jit(solution)/shard_map/psum | solution.py:20
  320.9 6.5 %psum.29 = f32[128]{0:T(128)S(1)} all-reduce(f32[128]{0:T(128)S(1)} %psum.28), channel_id=1, replica_groups=mesh['col_0'=4,'col_1'=4,'row_0'=4,'row_1'=2] {'col_1'}, use_global_device_ids=true, to_apply=%region_7.8 | all-reduce | flops 128 | bytes 1024 | tf_op jit(solution)/shard_map/psum | solution.py:20
  327.4 6.4 %psum.30 = f32[128]{0:T(128)S(1)} all-reduce(f32[128]{0:T(128)S(1)} %psum.29), channel_id=1, replica_groups=mesh['col_0'=4,'col_1'=4,'row_0'=4,'row_1'=2] {'row_0'}, use_global_device_ids=true, to_apply=%region_8.9 | all-reduce | flops 128 | bytes 1024 | tf_op jit(solution)/shard_map/psum | solution.py:20
  333.8 9.0 %psum.31 = f32[128]{0:T(128)} all-reduce(f32[128]{0:T(128)S(1)} %psum.30), channel_id=1, replica_groups=mesh['col_0'=4,'col_1'=4,'row_0'=4,'row_1'=2] {'row_1'}, use_global_device_ids=true, to_apply=%region_9.10 | all-reduce | flops 128 | bytes 1024 | tf_op jit(solution)/shard_map/psum | solution.py:20
  (41 shorter events, 0.7 us)
Async XLA Ops:
  0.6 0.8 copy-start
  13.6 13.1 %copy-start.7 = (s32[512]{0:T(512)S(1)}, s32[512]{0:T(512)}, u32[]{:S(2)}) copy-start(s32[512]{0:T(512)} %param.16) | copy-start | bytes 6148
  13.6 13.1 %copy-start.3 = (f32[128,512]{1,0:T(8,128)S(1)}, f32[128,512]{1,0:T(8,128)}, u32[]{:S(2)}) copy-start(f32[128,512]{1,0:T(8,128)} %param.10) | copy-start | bytes 786436
  13.6 13.1 %copy-start.6 = (f32[128,512]{1,0:T(8,128)S(1)}, f32[128,512]{1,0:T(8,128)}, u32[]{:S(2)}) copy-start(f32[128,512]{1,0:T(8,128)} %param.11) | copy-start | bytes 786436
  13.6 13.1 %copy-start.8 = (f32[512]{0:T(512)S(1)}, f32[512]{0:T(512)}, u32[]{:S(2)}) copy-start(f32[512]{0:T(512)} %param.15) | copy-start | bytes 6148
  13.6 13.1 %copy-start.9 = (f32[128]{0:T(128)S(1)}, f32[128]{0:T(128)}, u32[]{:S(2)}) copy-start(f32[128]{0:T(128)} %param.17) | copy-start | bytes 1540
  26.7 287.2 %copy-start.4 = (f32[128,512]{1,0:T(8,128)S(1)}, f32[128,512]{1,0:T(8,128)}, u32[]{:S(2)}) copy-start(f32[128,512]{1,0:T(8,128)} %param.11) | copy-start | bytes 786436
  26.8 51.4 %copy-start.1 = (bf16[512,64,128]{0,2,1:T(8,128)(2,1)S(1)}, bf16[512,64,128]{0,2,1:T(8,128)(2,1)}, u32[]{:S(2)}) copy-start(bf16[512,64,128]{0,2,1:T(8,128)(2,1)} %get-tuple-element.607) | copy-start | bytes 25165828 | tf_op jit(solution)/shard_map/while
  74.6 3.6 %collective-permute-start = (bf16[64,64,128]{2,1,0:T(8,128)(2,1)S(1)}, bf16[64,64,128]{2,1,0:T(8,128)(2,1)S(1)}, u32[]{:S(2)}, u32[]{:S(2)}) collective-permute-start(bf16[64,64,128]{2,1,0:T(8,128)(2,1)S(1)} %bitcast_reduce_fusion.4), channel_id=1, source_target_pairs={{0,1},{1,0},{2,3},{3,2},{4,5},{5,4},{6,7},{7,6},{8,9},{9,8},{10,11... | collective-permute-start | bytes 3145736 | tf_op jit(solution)/shard_map/while/body/eval_jaxpr/ppermute | solution.py:16
  117.6 3.6 %collective-permute-start.1 = (bf16[64,64,128]{2,1,0:T(8,128)(2,1)S(1)}, bf16[64,64,128]{2,1,0:T(8,128)(2,1)S(1)}, u32[]{:S(2)}, u32[]{:S(2)}) collective-permute-start(bf16[64,64,128]{2,1,0:T(8,128)(2,1)S(1)} %bitcast_reduce_fusion.5), channel_id=1, source_target_pairs={{0,1},{1,0},{2,3},{3,2},{4,5},{5,4},{6,7},{7,6},{8,9},{9,8},{10,11... | collective-permute-start | bytes 3145736 | tf_op jit(solution)/shard_map/while/body/eval_jaxpr/ppermute | solution.py:16
  127.7 43.6 %copy-start.1 = (bf16[512,64,128]{0,2,1:T(8,128)(2,1)S(1)}, bf16[512,64,128]{0,2,1:T(8,128)(2,1)}, u32[]{:S(2)}) copy-start(bf16[512,64,128]{0,2,1:T(8,128)(2,1)} %get-tuple-element.607) | copy-start | bytes 25165828 | tf_op jit(solution)/shard_map/while
  167.7 3.6 %collective-permute-start = (bf16[64,64,128]{2,1,0:T(8,128)(2,1)S(1)}, bf16[64,64,128]{2,1,0:T(8,128)(2,1)S(1)}, u32[]{:S(2)}, u32[]{:S(2)}) collective-permute-start(bf16[64,64,128]{2,1,0:T(8,128)(2,1)S(1)} %bitcast_reduce_fusion.4), channel_id=1, source_target_pairs={{0,1},{1,0},{2,3},{3,2},{4,5},{5,4},{6,7},{7,6},{8,9},{9,8},{10,11... | collective-permute-start | bytes 3145736 | tf_op jit(solution)/shard_map/while/body/eval_jaxpr/ppermute | solution.py:16
  210.7 3.6 %collective-permute-start.1 = (bf16[64,64,128]{2,1,0:T(8,128)(2,1)S(1)}, bf16[64,64,128]{2,1,0:T(8,128)(2,1)S(1)}, u32[]{:S(2)}, u32[]{:S(2)}) collective-permute-start(bf16[64,64,128]{2,1,0:T(8,128)(2,1)S(1)} %bitcast_reduce_fusion.5), channel_id=1, source_target_pairs={{0,1},{1,0},{2,3},{3,2},{4,5},{5,4},{6,7},{7,6},{8,9},{9,8},{10,11... | collective-permute-start | bytes 3145736 | tf_op jit(solution)/shard_map/while/body/eval_jaxpr/ppermute | solution.py:16
  220.8 43.6 %copy-start.1 = (bf16[512,64,128]{0,2,1:T(8,128)(2,1)S(1)}, bf16[512,64,128]{0,2,1:T(8,128)(2,1)}, u32[]{:S(2)}) copy-start(bf16[512,64,128]{0,2,1:T(8,128)(2,1)} %get-tuple-element.607) | copy-start | bytes 25165828 | tf_op jit(solution)/shard_map/while
  260.8 3.6 %collective-permute-start = (bf16[64,64,128]{2,1,0:T(8,128)(2,1)S(1)}, bf16[64,64,128]{2,1,0:T(8,128)(2,1)S(1)}, u32[]{:S(2)}, u32[]{:S(2)}) collective-permute-start(bf16[64,64,128]{2,1,0:T(8,128)(2,1)S(1)} %bitcast_reduce_fusion.4), channel_id=1, source_target_pairs={{0,1},{1,0},{2,3},{3,2},{4,5},{5,4},{6,7},{7,6},{8,9},{9,8},{10,11... | collective-permute-start | bytes 3145736 | tf_op jit(solution)/shard_map/while/body/eval_jaxpr/ppermute | solution.py:16
  303.8 3.6 %collective-permute-start.1 = (bf16[64,64,128]{2,1,0:T(8,128)(2,1)S(1)}, bf16[64,64,128]{2,1,0:T(8,128)(2,1)S(1)}, u32[]{:S(2)}, u32[]{:S(2)}) collective-permute-start(bf16[64,64,128]{2,1,0:T(8,128)(2,1)S(1)} %bitcast_reduce_fusion.5), channel_id=1, source_target_pairs={{0,1},{1,0},{2,3},{3,2},{4,5},{5,4},{6,7},{7,6},{8,9},{9,8},{10,11... | collective-permute-start | bytes 3145736 | tf_op jit(solution)/shard_map/while/body/eval_jaxpr/ppermute | solution.py:16
  313.9 29.0 %copy-start.2 = (f32[128,512]{1,0:T(8,128)}, f32[128,512]{1,0:T(8,128)S(1)}, u32[]{:S(2)}) copy-start(f32[128,512]{1,0:T(8,128)S(1)} %get-tuple-element.347) | copy-start | bytes 786436
  313.9 29.0 %copy-start.5 = (f32[128,512]{1,0:T(8,128)}, f32[128,512]{1,0:T(8,128)S(1)}, u32[]{:S(2)}) copy-start(f32[128,512]{1,0:T(8,128)S(1)} %get-tuple-element.348) | copy-start | bytes 786436
where the time goes:
time: 344 us; the launch traced here: 343 us
  blocking collectives  239 us (69%)
  matrix products  47.6 us (14%)
  local copies, waits for them, and re-layouts  26 us (8%)
  waiting for transfers between devices  13.5 us (4%)
  starting transfers between devices  8.01 us (2%)
  other arithmetic  7.85 us (2%)
    all_to_all x6, blocking collectives, deliver(): lax.all_to_all(halved, COL_ROW, split_axis=0, concat_axis=0, tiled=True)  210 us
    psum x4, blocking collectives, over_axes(): return functools.reduce(lax.psum, axes, value)  28.8 us
    unnamed x20, local copies, waits for them, and re-layouts  25.8 us
    dot_general x3, matrix products, gradient(): jnp.einsum('yik,ikh->hy', col_factors, returned, preferred_element_type=j...  19.1 us
    dot_general x3, matrix products, gradient(): jnp.einsum('yik,hy->ikh', col_factors, rounded, preferred_element_type=jn...  17.4 us
    ppermute x6, waiting for transfers between devices, partner_2(): return lax.ppermute(value, axis, pairs)  13.5 us
    ppermute x6, starting transfers between devices, partner_2(): return lax.ppermute(value, axis, pairs)  8.01 us
    while x3, matrix products  7.07 us
  transfers between devices with their start and end apart: 6, of which 6 were waited for; matrix products, arithmetic and copies ran while one was open for 0% of the time, Pallas kernels for 0%

commit v1 on v0

v1 whole, which is shorter than its diff:
```python
import functools

import jax
import jax.numpy as jnp
from jax import lax
from jax.experimental import pallas as pl
from jax.experimental.pallas import tpu as pltpu
from jax.sharding import Mesh
from jax.sharding import PartitionSpec as P

COL_ROW = ("col_0", "col_1", "row_0", "row_1")
CHIPS = ("col_0", "col_1", "row_0")
CORE = "row_1"
BF16 = jnp.bfloat16
F32 = jnp.float32
LIMIT = 8 << 20
NT = (((1,), (1,)), ((), ()))
VMEM = pl.BlockSpec(memory_space=pltpu.VMEM)
SMEM = pl.BlockSpec(memory_space=pltpu.SMEM)
ANY = pl.BlockSpec(memory_space=pl.ANY)


def swap(value):
    return lax.ppermute(value, CORE, [(0, 1), (1, 0)])


def spread(value):
    return lax.all_to_all(value, CHIPS, split_axis=0, concat_axis=0, tiled=True)


def other_half(value):
    lanes = value.shape[1] // 2
    return jnp.concatenate([value[:, lanes:], value[:, :lanes]], axis=1)


def low_lanes(value):
    return lax.broadcasted_iota(jnp.int32, value.shape, 1) < value.shape[1] // 2


def regroup_kernel(tiles, core_ref, raw_ref, own_ref, send_ref):
    to = lax.broadcasted_iota(jnp.int32, (256, 256), 0)
    at = lax.broadcasted_iota(jnp.int32, (256, 256), 1)
    order = (at == (to % 16) * 16 + to // 16).astype(F32).astype(BF16)
    first_core = core_ref[0] == 0
    cells = raw_ref.shape[0] // tiles

    def group(index, carry):
        first = index * 16
        at_cell = pl.ds(pl.multiple_of(first, 16), 16)
        for block in range(2):
            sides = []
            for side in range(2):
                rows = [
                    raw_ref[pl.ds(pl.multiple_of((first + y) * tiles, 16) + (2 * block + side) * 16, 16), :]
                    for y in range(16)
                ]
                sides.append(jnp.concatenate(rows, axis=0))
            low = low_lanes(sides[0])
            halves = [
                jnp.where(low, sides[0], other_half(sides[1])),
                jnp.where(low, other_half(sides[0]), sides[1]),
            ]
            own = jnp.where(first_core, halves[0], halves[1])
            send = jnp.where(first_core, halves[1], halves[0])
            moved = jnp.dot(
                order, jnp.concatenate([own, send], axis=1), preferred_element_type=F32
            ).astype(BF16)
            lanes = slice(block * 128, block * 128 + 128)
            for q in range(16):
                own_ref[q, at_cell, lanes] = moved[q * 16 : (q + 1) * 16, :128]
                send_ref[q, at_cell, lanes] = moved[q * 16 : (q + 1) * 16, 128:]
        return carry

    lax.fori_loop(0, cells // 16, group, 0, unroll=2)


def regroup(factors, core):
    cells, tiles, ranked = factors.shape
    step = 64
    quads = tiles // 4
    shape = pltpu.HBM((quads, cells, 2 * ranked), BF16)
    block = pl.BlockSpec((quads, step, 2 * ranked), lambda g: (0, g, 0))
    return pl.pallas_call(
        functools.partial(regroup_kernel, tiles),
        grid=(cells // step,),
        in_specs=[SMEM, pl.BlockSpec((step * tiles, ranked), lambda g: (g, 0))],
        out_specs=[block, block],
        out_shape=[shape, shape],
        compiler_params=pltpu.CompilerParams(vmem_limit_bytes=12 << 20),
        cost_estimate=pl.CostEstimate(
            flops=8_000_000_000, bytes_accessed=1 << 24, transcendentals=0
        ),
    )(core, pltpu.with_memory_space_constraint(factors.reshape(cells * tiles, ranked), pltpu.HBM))


def merge_kernel(after_ref, own_ref, other_ref, out_ref, sems):
    copies = [
        pltpu.make_async_copy(ref, out_ref.at[side], sems.at[side])
        for side, ref in enumerate((own_ref, other_ref))
    ]
    for copy in copies:
        copy.start()
    for copy in copies:
        copy.wait()


def merge(after, own, other):
    return pl.pallas_call(
        merge_kernel,
        in_specs=[ANY, ANY, ANY],
        out_specs=VMEM,
        out_shape=jax.ShapeDtypeStruct((2, *own.shape), own.dtype),
        scratch_shapes=[pltpu.SemaphoreType.DMA((2,))],
        compiler_params=pltpu.CompilerParams(vmem_limit_bytes=1 << 20),
        cost_estimate=pl.CostEstimate(
            flops=4_000_000_000, bytes_accessed=1 << 24, transcendentals=0
        ),
    )(after, *[pltpu.with_memory_space_constraint(f, pltpu.HBM) for f in (own, other)])


def expand_kernel(coefficient_ref, f_ref, total_ref, left):
    quads, cells = f_ref.shape[1], f_ref.shape[2]
    half = coefficient_ref.shape[1]

    def arrange(q, carry):
        for pair in range(2):
            one = coefficient_ref[q + 32 * pair]
            two = coefficient_ref[q + 32 * pair + 16]
            low = low_lanes(one)
            lanes = slice(pair * 128, pair * 128 + 128)
            left[q, :half, lanes] = jnp.where(low, one, other_half(two))
            left[q, half:, lanes] = jnp.where(low, other_half(one), two)
        return carry

    lax.fori_loop(0, quads, arrange, 0, unroll=2)
    for side in range(2):
        def block(index, carry):
            at_cell = pl.ds(pl.multiple_of(index * 256, 256), 256)
            total_ref[:, pl.ds(pl.multiple_of(side * cells + index * 256, 256), 256)] = sum(
                lax.dot_general(
                    left[q], f_ref[side, q, at_cell, :], NT, preferred_element_type=F32
                )
                for q in range(quads)
            )
            return carry

        lax.fori_loop(0, cells // 256, block, 0, unroll=2)


def project(values, f_ref, core_ref, ranks_ref, out_ref):
    quads, cells = f_ref.shape[1], f_ref.shape[2]
    half = out_ref.shape[1]
    lane = lax.broadcasted_iota(jnp.int32, (2 * half, 128), 1)
    low = lane < 64
    level = lane % 64 + 64 * core_ref[0]
    low_rows = low[:half]

    def quad(q, carry):
        moved = jnp.dot(
            values[:, :cells], f_ref[0, q], preferred_element_type=F32
        ) + jnp.dot(values[:, cells:], f_ref[1, q], preferred_element_type=F32)
        for pair in range(2):
            one, two = q + 32 * pair, q + 32 * pair + 16
            ranks = jnp.where(low, ranks_ref[one], ranks_ref[two])
            part = moved[:, pair * 128 : pair * 128 + 128]
            part = jnp.where(level < ranks, part, 0.0).astype(BF16)
            turned = other_half(part)
            out_ref[one] = jnp.where(low_rows, part[:half], turned[half:])
            out_ref[two] = jnp.where(low_rows, turned[:half], part[half:])
        return carry

    lax.fori_loop(0, quads, quad, 0, unroll=4)


def complete(total_ref, arrived_ref):
    cells = total_ref.shape[1] // 2
    return [
        total_ref[:, :cells] + arrived_ref[:, cells:],
        total_ref[:, cells:] + arrived_ref[:, :cells],
    ]


def first_kernel(core_ref, ranks_ref, z0_ref, z1_ref, f_ref, out_ref, values):
    cells = z0_ref.shape[1]
    values[:, :cells] = z0_ref[...].astype(BF16)
    values[:, cells:] = z1_ref[...].astype(BF16)
    project(values, f_ref, core_ref, ranks_ref, out_ref)


def row_kernel(
    core_ref, ranks_ref, total_ref, arrived_ref, base_ref, rate_ref, f_ref,
    out_ref, energy_ref, values,
):
    cells = total_ref.shape[1] // 2
    for side, field in enumerate(complete(total_ref, arrived_ref)):
        at = slice(side * cells, (side + 1) * cells)
        rate = rate_ref[:, at]
        exponent = base_ref[:, at] + field
        intensity = jnp.exp(exponent)
        values[:, at] = (rate - intensity).astype(BF16)
        if side == 0:
            energy_ref[...] = jnp.sum(intensity - rate * exponent, axis=1, keepdims=True)
    project(values, f_ref, core_ref, ranks_ref, out_ref)


def col_kernel(
    weight, core_ref, ranks_ref, total_ref, arrived_ref, step_ref, z_ref, m_ref,
    f_ref, out_ref, new_z_ref, new_m_ref, values,
):
    cells = total_ref.shape[1] // 2
    step = step_ref[:, :1]
    for side, pulled in enumerate(complete(total_ref, arrived_ref)):
        at = slice(side * cells, (side + 1) * cells)
        z = z_ref[:, at]
        moment = m_ref[:, at] - weight * step * (z - pulled)
        z = z + step * moment
        new_m_ref[:, at] = moment
        new_z_ref[:, at] = z
        values[:, at] = z.astype(BF16)
    project(values, f_ref, core_ref, ranks_ref, out_ref)


def last_kernel(
    total_ref, arrived_ref, step_ref, z_ref, m_ref, start_z_ref, start_m_ref,
    start_energy_ref, end_energy_ref, new_m_ref, change_ref,
):
    cells = total_ref.shape[1] // 2
    z = z_ref[:, :cells]
    moment = m_ref[:, :cells] - 0.5 * step_ref[:, :1] * (
        z - complete(total_ref, arrived_ref)[0]
    )
    new_m_ref[...] = moment
    start_z = start_z_ref[:, :cells]
    start_m = start_m_ref[:, :cells]
    pieces = 0.5 * (z * z - start_z * start_z + moment * moment - start_m * start_m)
    change_ref[...] = (
        jnp.sum(pieces, axis=1, keepdims=True) + end_energy_ref[...] - start_energy_ref[...]
    )


def call(kernel, specs, outs, scratch, flops, *args):
    return pl.pallas_call(
        kernel,
        in_specs=specs,
        out_specs=[VMEM] * len(outs),
        out_shape=[jax.ShapeDtypeStruct(*o) for o in outs],
        scratch_shapes=scratch,
        compiler_params=pltpu.CompilerParams(vmem_limit_bytes=LIMIT),
        cost_estimate=pl.CostEstimate(
            flops=flops, bytes_accessed=1 << 24, transcendentals=0
        ),
    )(*args)


def on_device(
    position, momentum, row_factors, col_factors, tile_ranks, log_mean, counts, step_size
):
    chains, cells = position.shape
    half = chains // 2
    tiles, ranked = tile_ranks.shape[0], row_factors.shape[2]
    tile = lax.axis_index(CHIPS)
    core = lax.axis_index(CORE).astype(jnp.int32)[None]
    col_ranks = lax.dynamic_slice_in_dim(tile_ranks, tile, 1, 1)[:, 0]
    row_ranks = lax.dynamic_slice_in_dim(tile_ranks, tile, 1, 0)[0]

    coefficients = ((tiles, half, ranked), BF16)
    state = ((chains, 2 * cells), F32)
    own_state = ((chains, cells), F32)
    column = ((chains, 1), F32)
    values = [pltpu.VMEM((chains, 2 * cells), BF16)]
    left = [pltpu.VMEM((tiles // 4, chains, 2 * ranked), BF16)]
    work = 2 * chains * 2 * cells * tiles * ranked // 2

    z_other = swap(position)
    own, send = regroup(col_factors, core)
    send, z_other = lax.optimization_barrier((send, z_other))
    col = merge(z_other, own, swap(send))
    row_own, send = regroup(row_factors, core)
    row_other = swap(send)
    start_z = jnp.concatenate([position, z_other], axis=1)
    start_m = jnp.concatenate([momentum, swap(momentum)], axis=1)
    rate = counts.astype(F32)
    base = jnp.concatenate([log_mean, swap(log_mean)])[None, :]
    rate = jnp.concatenate([rate, swap(rate)])[None, :]
    step = jnp.broadcast_to(step_size[:, None], (chains, ranked))

    def expand(coefficient, factors):
        (total,) = call(
            expand_kernel, [VMEM] * 2, [state], left, 2 * work, coefficient, factors
        )
        return total, swap(total)

    def row_pass(arrived):
        return call(
            row_kernel, [SMEM] * 2 + [VMEM] * 5, [coefficients, column], values, work,
            core, row_ranks, *expand(arrived, row), base, rate, row,
        )

    (out,) = call(
        first_kernel, [SMEM] * 2 + [VMEM] * 3, [coefficients], values, work,
        core, col_ranks, position, z_other, col,
    )
    out, start_z, start_m, base, rate, step, row_ranks = lax.optimization_barrier(
        (out, start_z, start_m, base, rate, step, row_ranks)
    )
    z, m = start_z, start_m
    arrived = spread(out)
    row = merge(arrived, row_own, row_other)
    out, start_energy = row_pass(arrived)
    for weight in (0.5, 1.0):
        out, z, m = call(
            functools.partial(col_kernel, weight),
            [SMEM] * 2 + [VMEM] * 6, [coefficients, state, state], values, work,
            core, col_ranks, *expand(spread(out), col), step, z, m, col,
        )
        out, end_energy = row_pass(spread(out))
    m, change = call(
        last_kernel, [VMEM] * 9, [own_state, column], [], 1 << 24,
        *expand(spread(out), col), step, z, m, start_z, start_m,
        start_energy, end_energy,
    )
    change = change[:, 0]
    change = change + swap(change)
    change = spread(jnp.broadcast_to(change[None], (tiles, chains))).sum(axis=0)
    return z[:, :cells], m, change


def solution(mesh):
    split = Mesh(
        mesh.devices.reshape(4, 4, 4, 2), ("col_0", "col_1", "row_0", "row_1")
    )
    return jax.shard_map(
        on_device,
        mesh=split,
        in_specs=(
            P(None, COL_ROW),
            P(None, COL_ROW),
            P(COL_ROW, None, None),
            P(COL_ROW, None, None),
            P(),
            P(COL_ROW),
            P(COL_ROW),
            P(),
        ),
        out_specs=(P(None, COL_ROW), P(None, COL_ROW), P()),
        check_vma=False,
    )
```

time: 344 us -> 259 us (0.75)
  blocking collectives: 239 us -> 107 us
  Pallas kernels: 0 us -> 72.5 us
  matrix products: 47.6 us -> 0 us
  waiting for transfers between devices: 13.5 us -> 41.3 us
  starting transfers between devices: 8.01 us -> 34.1 us
  local copies, waits for them, and re-layouts: 26 us -> 1.65 us
  other arithmetic: 7.85 us -> 0.73 us
    all_to_all x6 -> x5, blocking collectives: 210 us -> 107 us  [spread(): return lax.all_to_all(value, CHIPS, split_axis=0, concat_axis=0, tiled=True)]
    pallas_call x0 -> x17, Pallas kernels: none -> 72.5 us  [the longest x13 41 us: call(): pl.pallas_call(kernel, in_specs=specs, out_specs=[VMEM] * len(outs), out_...]
    dot_general x9 -> x0, matrix products: 40.5 us -> none  [the longest x3 19.1 us: gradient(): jnp.einsum('yik,ikh->hy', col_factors, returned, preferred_element_type=j...]
    psum x4 -> x0, blocking collectives: 28.8 us -> none  [over_axes(): return functools.reduce(lax.psum, axes, value)]
    unnamed x20, local copies, waits for them, and re-layouts: 25.8 us -> 0.05 us
    all_to_all x0 -> x2, waiting for transfers between devices: none -> 24.7 us  [spread(): return lax.all_to_all(value, CHIPS, split_axis=0, concat_axis=0, tiled=True)]
    all_to_all x0 -> x2, starting transfers between devices: none -> 15.9 us  [spread(): return lax.all_to_all(value, CHIPS, split_axis=0, concat_axis=0, tiled=True)]
    ppermute x6 -> x13, starting transfers between devices: 8.01 us -> 18.2 us  [swap(): return lax.ppermute(value, CORE, [(0, 1), (1, 0)])]
  transfers between devices with their start and end apart: 6 -> 15, of which waited for: 6 -> 11; matrix products, arithmetic and copies ran while one was open for 0% -> 0% of each run, Pallas kernels for 0% -> 12%
where the time goes in v1:
time: 259 us; the launch traced here: 258 us
  blocking collectives  107 us (41%)
  Pallas kernels  72.5 us (28%)
  waiting for transfers between devices  41.3 us (16%)
  starting transfers between devices  34.1 us (13%)
    all_to_all x5, blocking collectives, spread(): return lax.all_to_all(value, CHIPS, split_axis=0, concat_axis=0, tiled=True)  107 us
    pallas_call x13, Pallas kernels, call(): pl.pallas_call(kernel, in_specs=specs, out_specs=[VMEM] * len(outs), out_...  41 us
    all_to_all x2, waiting for transfers between devices, spread(): return lax.all_to_all(value, CHIPS, split_axis=0, concat_axis=0, tiled=True)  24.7 us
    pallas_call x2, Pallas kernels, regroup(): pl.pallas_call(functools.partial(regroup_kernel, tiles), grid=(cells // s...  24.5 us
    ppermute x13, starting transfers between devices, swap(): return lax.ppermute(value, CORE, [(0, 1), (1, 0)])  18.2 us
    ppermute x13, waiting for transfers between devices, swap(): return lax.ppermute(value, CORE, [(0, 1), (1, 0)])  16.5 us
    all_to_all x2, starting transfers between devices, spread(): return lax.all_to_all(value, CHIPS, split_axis=0, concat_axis=0, tiled=True)  15.9 us
    pallas_call x2, Pallas kernels, merge(): pl.pallas_call(merge_kernel, in_specs=[ANY, ANY, ANY], out_specs=VMEM, ou...  6.97 us
  transfers between devices with their start and end apart: 15, of which 11 were waited for; matrix products, arithmetic and copies ran while one was open for 0% of the time, Pallas kernels for 12%

profile of v1, /device:TPU:1, one launch (start us, length us, event | category | flops | bytes accessed | tf_op | source)
XLA Modules:
  0.0 258.1 jit_solution(13779526800746971676)
XLA Ops:
  0.6 1.5 collective-permute-start
  2.1 12.2 %shard_map.103 = (bf16[16,512,256]{2,1,0:T(8,128)(2,1)}, bf16[16,512,256]{2,1,0:T(8,128)(2,1)}) custom-call(s32[1]{0:T(128)} %bitcast.core_ref, bf16[32768,128]{1,0:T(8,128)(2,1)} %bitcast.17), custom_call_target="tpu_custom_call" | custom-call | flops 8000000000 | bytes 16777216 | tf_op jit(solution)/shard_map/pallas_call | solution.py:83
  14.4 12.3 %shard_map.106 = (bf16[16,512,256]{2,1,0:T(8,128)(2,1)}, bf16[16,512,256]{2,1,0:T(8,128)(2,1)}) custom-call(s32[1]{0:T(128)} %bitcast.core_ref, bf16[32768,128]{1,0:T(8,128)(2,1)} %bitcast.18), custom_call_target="tpu_custom_call" | custom-call | flops 8000000000 | bytes 16777216 | tf_op jit(solution)/shard_map/pallas_call | solution.py:83
  26.7 0.5 collective-permute-start.5
  27.2 0.4 collective-permute-start.3
  27.8 0.2 dynamic-slice_reduce_fusion.ranks_ref
  27.9 6.3 %collective-permute-done.4 = f32[512]{0:T(512)S(1)} collective-permute-done((f32[512]{0:T(512)S(1)}, f32[512]{0:T(512)S(1)}, u32[]{:S(2)}, u32[]{:S(2)}) %collective-permute-start.4) | collective-permute-done | bytes 2080 | tf_op jit(solution)/shard_map/ppermute | solution.py:24
  34.6 3.5 %shard_map.104.f_ref = bf16[2,16,512,256]{3,2,1,0:T(8,128)(2,1)S(1)} custom-call(f32[128,512]{1,0:T(8,128)S(1)} %collective-permute-done.after_ref.z1_ref, bf16[16,512,256]{2,1,0:T(8,128)(2,1)} %get-tuple-element.31.own_ref, bf16[16,512,256]{2,1,0:T(8,128)(2,1)} %collective-permute-done.1.other_ref), custom_call_target="tpu_custom_call" | custom-call | flops 4000000000 | bytes 16777216 | tf_op jit(solution)/shard_map/pallas_call | solution.py:108
  38.1 3.7 %shard_map.105 = bf16[64,64,128]{2,1,0:T(8,128)(2,1)} custom-call(s32[1]{0:T(128)} %bitcast.core_ref, s32[64]{0:T(128)S(1)} %dynamic-slice_reduce_fusion.ranks_ref, f32[128,512]{1,0:T(8,128)S(1)} %copy-done.3, f32[128,512]{1,0:T(8,128)S(1)} %collective-permute-done.after_ref.z1_ref, bf16[2,16,512,256]{3,2,1,0:T(8,128)(2,1)S(1)} %shard_map.104.f_ref), custom_call_target="tpu_custom_call" | custom-call | flops 1073741824 | bytes 16777216 | tf_op jit(solution)/shard_map/pallas_call | solution.py:242
  41.9 11.3 %all-to-all-start = ((bf16[64,64,128]{2,1,0:T(8,128)(2,1)}), bf16[64,64,128]{2,1,0:T(8,128)(2,1)S(1)}, u32[]{:S(2)}, u32[]{:S(2)}) async-start(bf16[64,64,128]{2,1,0:T(8,128)(2,1)} %shard_map.105), calls=%async_computation | async-start | bytes 2097152 | tf_op jit(solution)/shard_map/all_to_all | solution.py:28
  53.2 17.0 %all-to-all-done.after_ref.coefficient_ref = bf16[64,64,128]{2,1,0:T(8,128)(2,1)S(1)} async-done(((bf16[64,64,128]{2,1,0:T(8,128)(2,1)}), bf16[64,64,128]{2,1,0:T(8,128)(2,1)S(1)}, u32[]{:S(2)}, u32[]{:S(2)}) %all-to-all-start) | async-done | bytes 1048608 | tf_op jit(solution)/shard_map/all_to_all | solution.py:28
  70.2 3.5 %shard_map.107.f_ref = bf16[2,16,512,256]{3,2,1,0:T(8,128)(2,1)S(1)} custom-call(bf16[64,64,128]{2,1,0:T(8,128)(2,1)S(1)} %all-to-all-done.after_ref.coefficient_ref, bf16[16,512,256]{2,1,0:T(8,128)(2,1)} %get-tuple-element.35.own_ref, bf16[16,512,256]{2,1,0:T(8,128)(2,1)} %collective-permute-done.5.other_ref), custom_call_target="tpu_custom_call" | custom-call | flops 4000000000 | bytes 16777216 | tf_op jit(solution)/shard_map/pallas_call | solution.py:108
  73.7 3.6 %shard_map.108.total_ref = f32[128,1024]{1,0:T(8,128)S(1)} custom-call(bf16[64,64,128]{2,1,0:T(8,128)(2,1)S(1)} %all-to-all-done.after_ref.coefficient_ref, bf16[2,16,512,256]{3,2,1,0:T(8,128)(2,1)S(1)} %shard_map.107.f_ref), custom_call_target="tpu_custom_call" | custom-call | flops 2147483648 | bytes 16777216 | tf_op jit(solution)/shard_map/pallas_call | solution.py:242
  77.3 2.5 collective-permute-start.6
  79.9 1.5 collective-permute-done.6.arrived_ref
  81.4 2.9 %shard_map.109 = (bf16[64,64,128]{2,1,0:T(8,128)(2,1)S(1)}, f32[128,1]{1,0:T(8,128)S(1)}) custom-call(s32[1]{0:T(128)} %bitcast.core_ref, s32[64]{0:T(128)S(1)} %dynamic-slice_bitcast_fusion.ranks_ref, f32[128,1024]{1,0:T(8,128)S(1)} %shard_map.108.total_ref, f32[128,1024]{1,0:T(8,128)S(1)} %collective-permute-done.6.arrived_ref, f32[1,1024]{1,0:T(1,128)S(1)} %bitcast.13, ...), custom_call_target="tpu_custom_call" | custom-call | flops 1073741824 | bytes 16777216 | tf_op jit(solution)/shard_map/pallas_call | solution.py:242
  84.3 21.4 %all_to_all.36.coefficient_ref = bf16[64,64,128]{2,1,0:T(8,128)(2,1)S(1)} all-to-all(bf16[64,64,128]{2,1,0:T(8,128)(2,1)S(1)} %get-tuple-element.39), channel_id=1, replica_groups=mesh['col_0'=4,'col_1'=4,'row_0'=4,'row_1'=2] {'col_0','col_1','row_0'}, dimensions={0} | all-to-all | bytes 2097152 | tf_op jit(solution)/shard_map/all_to_all | solution.py:28
  105.7 3.6 %shard_map.110.total_ref = f32[128,1024]{1,0:T(8,128)S(1)} custom-call(bf16[64,64,128]{2,1,0:T(8,128)(2,1)S(1)} %all_to_all.36.coefficient_ref, bf16[2,16,512,256]{3,2,1,0:T(8,128)(2,1)S(1)} %bitcast.9), custom_call_target="tpu_custom_call" | custom-call | flops 2147483648 | bytes 16777216 | tf_op jit(solution)/shard_map/pallas_call | solution.py:242
  109.3 2.5 collective-permute-start.7
  111.8 1.5 collective-permute-done.7.arrived_ref
  113.3 3.0 %shard_map.111 = (bf16[64,64,128]{2,1,0:T(8,128)(2,1)S(1)}, f32[128,1024]{1,0:T(8,128)S(1)}, f32[128,1024]{1,0:T(8,128)S(1)}) custom-call(s32[1]{0:T(128)} %bitcast.core_ref, s32[64]{0:T(128)S(1)} %dynamic-slice_reduce_fusion.ranks_ref, f32[128,1024]{1,0:T(8,128)S(1)} %shard_map.110.total_ref, f32[128,1024]{1,0:T(8,128)S(1)} %collective-permute-done.7.arrived_ref, ...), custom_call_target="tpu_custom_call" | custom-call | flops 1073741824 | bytes 16777216 | tf_op jit(solution)/shard_map/pallas_call | solution.py:242
  116.3 21.4 %all_to_all.37.coefficient_ref = bf16[64,64,128]{2,1,0:T(8,128)(2,1)S(1)} all-to-all(bf16[64,64,128]{2,1,0:T(8,128)(2,1)S(1)} %get-tuple-element.43), channel_id=1, replica_groups=mesh['col_0'=4,'col_1'=4,'row_0'=4,'row_1'=2] {'col_0','col_1','row_0'}, dimensions={0} | all-to-all | bytes 2097152 | tf_op jit(solution)/shard_map/all_to_all | solution.py:28
  137.7 3.6 %shard_map.112.total_ref = f32[128,1024]{1,0:T(8,128)S(1)} custom-call(bf16[64,64,128]{2,1,0:T(8,128)(2,1)S(1)} %all_to_all.37.coefficient_ref, bf16[2,16,512,256]{3,2,1,0:T(8,128)(2,1)S(1)} %shard_map.107.f_ref), custom_call_target="tpu_custom_call" | custom-call | flops 2147483648 | bytes 16777216 | tf_op jit(solution)/shard_map/pallas_call | solution.py:242
  141.3 2.5 collective-permute-start.8
  143.8 1.5 collective-permute-done.8.arrived_ref
  145.4 3.2 %shard_map.113 = (bf16[64,64,128]{2,1,0:T(8,128)(2,1)S(1)}, f32[128,1]{1,0:T(8,128)}) custom-call(s32[1]{0:T(128)} %bitcast.core_ref, s32[64]{0:T(128)S(1)} %dynamic-slice_bitcast_fusion.ranks_ref, f32[128,1024]{1,0:T(8,128)S(1)} %shard_map.112.total_ref, f32[128,1024]{1,0:T(8,128)S(1)} %collective-permute-done.8.arrived_ref, f32[1,1024]{1,0:T(1,128)S(1)} %bitcast.14, ...), custom_call_target="tpu_custom_call" | custom-call | flops 1073741824 | bytes 16777216 | tf_op jit(solution)/shard_map/pallas_call | solution.py:242
  148.6 21.4 %all_to_all.38.coefficient_ref = bf16[64,64,128]{2,1,0:T(8,128)(2,1)S(1)} all-to-all(bf16[64,64,128]{2,1,0:T(8,128)(2,1)S(1)} %get-tuple-element.44), channel_id=1, replica_groups=mesh['col_0'=4,'col_1'=4,'row_0'=4,'row_1'=2] {'col_0','col_1','row_0'}, dimensions={0} | all-to-all | bytes 2097152 | tf_op jit(solution)/shard_map/all_to_all | solution.py:28
  170.0 3.6 %shard_map.114.total_ref = f32[128,1024]{1,0:T(8,128)S(1)} custom-call(bf16[64,64,128]{2,1,0:T(8,128)(2,1)S(1)} %all_to_all.38.coefficient_ref, bf16[2,16,512,256]{3,2,1,0:T(8,128)(2,1)S(1)} %bitcast.9), custom_call_target="tpu_custom_call" | custom-call | flops 2147483648 | bytes 16777216 | tf_op jit(solution)/shard_map/pallas_call | solution.py:242
  173.6 2.5 collective-permute-start.9
  176.1 1.5 collective-permute-done.9.arrived_ref
  177.7 2.9 %shard_map.115 = (bf16[64,64,128]{2,1,0:T(8,128)(2,1)S(1)}, f32[128,1024]{1,0:T(8,128)S(1)}, f32[128,1024]{1,0:T(8,128)S(1)}) custom-call(s32[1]{0:T(128)} %bitcast.core_ref, s32[64]{0:T(128)S(1)} %dynamic-slice_reduce_fusion.ranks_ref, f32[128,1024]{1,0:T(8,128)S(1)} %shard_map.114.total_ref, f32[128,1024]{1,0:T(8,128)S(1)} %collective-permute-done.9.arrived_ref, ...), custom_call_target="tpu_custom_call" | custom-call | flops 1073741824 | bytes 16777216 | tf_op jit(solution)/shard_map/pallas_call | solution.py:242
  180.6 21.4 %all_to_all.39.coefficient_ref = bf16[64,64,128]{2,1,0:T(8,128)(2,1)S(1)} all-to-all(bf16[64,64,128]{2,1,0:T(8,128)(2,1)S(1)} %get-tuple-element.48), channel_id=1, replica_groups=mesh['col_0'=4,'col_1'=4,'row_0'=4,'row_1'=2] {'col_0','col_1','row_0'}, dimensions={0} | all-to-all | bytes 2097152 | tf_op jit(solution)/shard_map/all_to_all | solution.py:28
  202.0 3.6 %shard_map.116.total_ref = f32[128,1024]{1,0:T(8,128)S(1)} custom-call(bf16[64,64,128]{2,1,0:T(8,128)(2,1)S(1)} %all_to_all.39.coefficient_ref, bf16[2,16,512,256]{3,2,1,0:T(8,128)(2,1)S(1)} %shard_map.107.f_ref), custom_call_target="tpu_custom_call" | custom-call | flops 2147483648 | bytes 16777216 | tf_op jit(solution)/shard_map/pallas_call | solution.py:242
  205.6 2.5 collective-permute-start.10
  208.2 1.5 collective-permute-done.10.arrived_ref
  209.7 2.9 %shard_map.117 = (bf16[64,64,128]{2,1,0:T(8,128)(2,1)S(1)}, f32[128,1]{1,0:T(8,128)S(1)}) custom-call(s32[1]{0:T(128)} %bitcast.core_ref, s32[64]{0:T(128)S(1)} %dynamic-slice_bitcast_fusion.ranks_ref, f32[128,1024]{1,0:T(8,128)S(1)} %shard_map.116.total_ref, f32[128,1024]{1,0:T(8,128)S(1)} %collective-permute-done.10.arrived_ref, f32[1,1024]{1,0:T(1,128)S(1)} %bitcast.15, ...), custom_call_target="tpu_custom_call" | custom-call | flops 1073741824 | bytes 16777216 | tf_op jit(solution)/shard_map/pallas_call | solution.py:242
  212.5 21.4 %all_to_all.40.coefficient_ref = bf16[64,64,128]{2,1,0:T(8,128)(2,1)S(1)} all-to-all(bf16[64,64,128]{2,1,0:T(8,128)(2,1)S(1)} %get-tuple-element.49), channel_id=1, replica_groups=mesh['col_0'=4,'col_1'=4,'row_0'=4,'row_1'=2] {'col_0','col_1','row_0'}, dimensions={0} | all-to-all | bytes 2097152 | tf_op jit(solution)/shard_map/all_to_all | solution.py:28
  233.9 3.6 %shard_map.118.total_ref = f32[128,1024]{1,0:T(8,128)S(1)} custom-call(bf16[64,64,128]{2,1,0:T(8,128)(2,1)S(1)} %all_to_all.40.coefficient_ref, bf16[2,16,512,256]{3,2,1,0:T(8,128)(2,1)S(1)} %bitcast.9), custom_call_target="tpu_custom_call" | custom-call | flops 2147483648 | bytes 16777216 | tf_op jit(solution)/shard_map/pallas_call | solution.py:242
  237.5 2.5 collective-permute-start.11
  240.1 1.5 collective-permute-done.11.arrived_ref
  241.6 0.9 shard_map.119
  242.6 0.5 collective-permute-start.12
  243.0 0.8 collective-permute-done.12
  243.8 0.6 broadcast_in_dim.25
  244.5 4.6 %all-to-all-start.6 = ((f32[64,1,128]{2,1,0:T(1,128)}), f32[64,1,128]{2,1,0:T(1,128)S(1)}, u32[]{:S(2)}, u32[]{:S(2)}) async-start(f32[64,1,128]{2,1,0:T(1,128)} %broadcast_in_dim.25), calls=%async_computation.6 | async-start | bytes 65536 | tf_op jit(solution)/shard_map/all_to_all | solution.py:28
  249.1 0.7 slice.3
  249.8 7.7 %all-to-all-done.6 = f32[64,1,128]{2,1,0:T(1,128)S(1)} async-done(((f32[64,1,128]{2,1,0:T(1,128)}), f32[64,1,128]{2,1,0:T(1,128)S(1)}, u32[]{:S(2)}, u32[]{:S(2)}) %all-to-all-start.6) | async-done | bytes 32800 | tf_op jit(solution)/shard_map/all_to_all | solution.py:28
  257.5 0.5 reduce_sum.9
  (38 shorter events, 0.7 us)
Async XLA Ops:
  0.6 27.1 %copy-start = (s32[64,64]{1,0:T(8,128)S(1)}, s32[64,64]{1,0:T(8,128)}, u32[]{:S(2)}) copy-start(s32[64,64]{1,0:T(8,128)} %param.12) | copy-start | bytes 49156
  0.6 13.7 %collective-permute-start = (f32[128,512]{1,0:T(8,128)}, f32[128,512]{1,0:T(8,128)S(1)}, u32[]{:S(2)}, u32[]{:S(2)}) collective-permute-start(f32[128,512]{1,0:T(8,128)} %z0_ref.1), channel_id=1, source_target_pairs={{0,1},{1,0},{2,3},{3,2},{4,5},{5,4},{6,7},{7,6},{8,9},{9,8},{10,11... | collective-permute-start | bytes 786440 | tf_op jit(solution)/shard_map/ppermute | solution.py:24
  14.3 20.2 %collective-permute-start.1 = (bf16[16,512,256]{2,1,0:T(8,128)(2,1)}, bf16[16,512,256]{2,1,0:T(8,128)(2,1)}, u32[]{:S(2)}, u32[]{:S(2)}) collective-permute-start(bf16[16,512,256]{2,1,0:T(8,128)(2,1)} %get-tuple-element.32), channel_id=1, source_target_pairs={{0,1},{1,0},{2,3},{3,2},{4,5},{5,4},{6,7},{7,6},{8,9},{9,8},{10,11... | collective-permute-start | bytes 12582920 | tf_op jit(solution)/shard_map/ppermute | solution.py:24
  14.3 12.8 %copy-start.5 = (s32[512]{0:T(512)S(1)}, s32[512]{0:T(512)}, u32[]{:S(2)}) copy-start(s32[512]{0:T(512)} %param.14) | copy-start | bytes 6148
  14.3 12.9 %copy-start.6 = (f32[512]{0:T(512)S(1)}, f32[512]{0:T(512)}, u32[]{:S(2)}) copy-start(f32[512]{0:T(512)} %param.13) | copy-start | bytes 6148
  14.3 13.3 %copy-start.4 = (f32[128,512]{1,0:T(8,128)S(1)}, f32[128,512]{1,0:T(8,128)}, u32[]{:S(2)}) copy-start(f32[128,512]{1,0:T(8,128)} %param.9) | copy-start | bytes 786436
  14.4 19.9 %copy-start.3 = (f32[128,512]{1,0:T(8,128)S(1)}, f32[128,512]{1,0:T(8,128)}, u32[]{:S(2)}) copy-start(f32[128,512]{1,0:T(8,128)} %z0_ref.1) | copy-start | bytes 786436
  26.7 26.5 %collective-permute-start.5 = (bf16[16,512,256]{2,1,0:T(8,128)(2,1)}, bf16[16,512,256]{2,1,0:T(8,128)(2,1)}, u32[]{:S(2)}, u32[]{:S(2)}) collective-permute-start(bf16[16,512,256]{2,1,0:T(8,128)(2,1)} %get-tuple-element.36), channel_id=1, source_target_pairs={{0,1},{1,0},{2,3},{3,2},{4,5},{5,4},{6,7},{7,6},{8,9},{9,8},{10,11... | collective-permute-start | bytes 12582920 | tf_op jit(solution)/shard_map/ppermute | solution.py:24
  27.1 7.1 %collective-permute-start.4 = (f32[512]{0:T(512)S(1)}, f32[512]{0:T(512)S(1)}, u32[]{:S(2)}, u32[]{:S(2)}) collective-permute-start(f32[512]{0:T(512)S(1)} %convert_element_type.3), channel_id=1, source_target_pairs={{0,1},{1,0},{2,3},{3,2},{4,5},{5,4},{6,7},{7,6},{8,9},{9,8},{10,11... | collective-permute-start | bytes 6152 | tf_op jit(solution)/shard_map/ppermute | solution.py:24
  27.2 7.0 %collective-permute-start.3 = (f32[512]{0:T(512)S(1)}, f32[512]{0:T(512)S(1)}, u32[]{:S(2)}, u32[]{:S(2)}) collective-permute-start(f32[512]{0:T(512)S(1)} %copy-done.6), channel_id=1, source_target_pairs={{0,1},{1,0},{2,3},{3,2},{4,5},{5,4},{6,7},{7,6},{8,9},{9,8},{10,11... | collective-permute-start | bytes 6152 | tf_op jit(solution)/shard_map/ppermute | solution.py:24
  27.7 6.9 %collective-permute-start.2 = (f32[128,512]{1,0:T(8,128)S(1)}, f32[128,512]{1,0:T(8,128)S(1)}, u32[]{:S(2)}, u32[]{:S(2)}) collective-permute-start(f32[128,512]{1,0:T(8,128)S(1)} %copy-done.4), channel_id=1, source_target_pairs={{0,1},{1,0},{2,3},{3,2},{4,5},{5,4},{6,7},{7,6},{8,9},{9,8},{10,11... | collective-permute-start | bytes 786440 | tf_op jit(solution)/shard_map/ppermute | solution.py:24
  38.1 3.8 %copy-start.2 = (bf16[2,16,512,256]{3,2,1,0:T(8,128)(2,1)}, bf16[2,16,512,256]{3,2,1,0:T(8,128)(2,1)S(1)}, u32[]{:S(2)}) copy-start(bf16[2,16,512,256]{3,2,1,0:T(8,128)(2,1)S(1)} %shard_map.104.f_ref) | copy-start | bytes 25165828
  38.1 3.8 %copy-start.7 = (f32[128]{0:T(128)S(1)}, f32[128]{0:T(128)}, u32[]{:S(2)}) copy-start(f32[128]{0:T(128)} %param.15) | copy-start | bytes 1540
  41.9 28.3 %all-to-all-start = ((bf16[64,64,128]{2,1,0:T(8,128)(2,1)}), bf16[64,64,128]{2,1,0:T(8,128)(2,1)S(1)}, u32[]{:S(2)}, u32[]{:S(2)}) async-start(bf16[64,64,128]{2,1,0:T(8,128)(2,1)} %shard_map.105), calls=%async_computation | async-start | bytes 2097152 | tf_op jit(solution)/shard_map/all_to_all | solution.py:28
  73.7 32.0 %slice-start = ((s8[8388608]{0:T(1024)(128)(4,1)}), s8[4194304]{0:T(1024)(128)(4,1)S(1)}, s32[]{:S(2)}) async-start(s8[8388608]{0:T(1024)(128)(4,1)} %bitcast.8), calls=%async_computation.7 | async-start | bytes 8388608
  77.3 28.3 %slice-start.1 = ((s8[8388608]{0:T(1024)(128)(4,1)}), s8[4194304]{0:T(1024)(128)(4,1)S(1)}, s32[]{:S(2)}) async-start(s8[8388608]{0:T(1024)(128)(4,1)} %bitcast.8), calls=%async_computation.8 | async-start | bytes 8388608
  77.3 4.1 %collective-permute-start.6 = (f32[128,1024]{1,0:T(8,128)S(1)}, f32[128,1024]{1,0:T(8,128)S(1)}, u32[]{:S(2)}, u32[]{:S(2)}) collective-permute-start(f32[128,1024]{1,0:T(8,128)S(1)} %shard_map.108.total_ref), channel_id=1, source_target_pairs={{0,1},{1,0},{2,3},{3,2},{4,5},{5,4},{6,7},{7,6},{8,9},{9,8},{10,11... | collective-permute-start | bytes 1572872 | tf_op jit(solution)/shard_map/ppermute | solution.py:24
  109.3 4.1 %collective-permute-start.7 = (f32[128,1024]{1,0:T(8,128)S(1)}, f32[128,1024]{1,0:T(8,128)S(1)}, u32[]{:S(2)}, u32[]{:S(2)}) collective-permute-start(f32[128,1024]{1,0:T(8,128)S(1)} %shard_map.110.total_ref), channel_id=1, source_target_pairs={{0,1},{1,0},{2,3},{3,2},{4,5},{5,4},{6,7},{7,6},{8,9},{9,8},{10,11... | collective-permute-start | bytes 1572872 | tf_op jit(solution)/shard_map/ppermute | solution.py:24
  141.3 4.1 %collective-permute-start.8 = (f32[128,1024]{1,0:T(8,128)S(1)}, f32[128,1024]{1,0:T(8,128)S(1)}, u32[]{:S(2)}, u32[]{:S(2)}) collective-permute-start(f32[128,1024]{1,0:T(8,128)S(1)} %shard_map.112.total_ref), channel_id=1, source_target_pairs={{0,1},{1,0},{2,3},{3,2},{4,5},{5,4},{6,7},{7,6},{8,9},{9,8},{10,11... | collective-permute-start | bytes 1572872 | tf_op jit(solution)/shard_map/ppermute | solution.py:24
  173.6 4.1 %collective-permute-start.9 = (f32[128,1024]{1,0:T(8,128)S(1)}, f32[128,1024]{1,0:T(8,128)S(1)}, u32[]{:S(2)}, u32[]{:S(2)}) collective-permute-start(f32[128,1024]{1,0:T(8,128)S(1)} %shard_map.114.total_ref), channel_id=1, source_target_pairs={{0,1},{1,0},{2,3},{3,2},{4,5},{5,4},{6,7},{7,6},{8,9},{9,8},{10,11... | collective-permute-start | bytes 1572872 | tf_op jit(solution)/shard_map/ppermute | solution.py:24
  205.6 4.1 %collective-permute-start.10 = (f32[128,1024]{1,0:T(8,128)S(1)}, f32[128,1024]{1,0:T(8,128)S(1)}, u32[]{:S(2)}, u32[]{:S(2)}) collective-permute-start(f32[128,1024]{1,0:T(8,128)S(1)} %shard_map.116.total_ref), channel_id=1, source_target_pairs={{0,1},{1,0},{2,3},{3,2},{4,5},{5,4},{6,7},{7,6},{8,9},{9,8},{10,11... | collective-permute-start | bytes 1572872 | tf_op jit(solution)/shard_map/ppermute | solution.py:24
  233.9 24.1 %copy-start.1 = (s32[64,64]{1,0:T(8,128)S(1)}, s32[64,64]{1,0:T(8,128)}, u32[]{:S(2)}) copy-start(s32[64,64]{1,0:T(8,128)} %param.12) | copy-start | bytes 49156
  237.5 4.1 %collective-permute-start.11 = (f32[128,1024]{1,0:T(8,128)S(1)}, f32[128,1024]{1,0:T(8,128)S(1)}, u32[]{:S(2)}, u32[]{:S(2)}) collective-permute-start(f32[128,1024]{1,0:T(8,128)S(1)} %shard_map.118.total_ref), channel_id=1, source_target_pairs={{0,1},{1,0},{2,3},{3,2},{4,5},{5,4},{6,7},{7,6},{8,9},{9,8},{10,11... | collective-permute-start | bytes 1572872 | tf_op jit(solution)/shard_map/ppermute | solution.py:24
  242.6 1.3 collective-permute-start.12
  244.5 13.1 %all-to-all-start.6 = ((f32[64,1,128]{2,1,0:T(1,128)}), f32[64,1,128]{2,1,0:T(1,128)S(1)}, u32[]{:S(2)}, u32[]{:S(2)}) async-start(f32[64,1,128]{2,1,0:T(1,128)} %broadcast_in_dim.25), calls=%async_computation.6 | async-start | bytes 65536 | tf_op jit(solution)/shard_map/all_to_all | solution.py:28

commit v2 on v1

v2 whole, which is shorter than its diff:
```python
import functools

import jax
import jax.numpy as jnp
from jax import lax
from jax.experimental import pallas as pl
from jax.experimental.pallas import tpu as pltpu
from jax.sharding import Mesh
from jax.sharding import PartitionSpec as P

COL_ROW = ("col_0", "col_1", "row_0", "row_1")
CHIPS = ("col_0", "col_1", "row_0")
CORE = "row_1"
BF16 = jnp.bfloat16
F32 = jnp.float32
LIMIT = 8 << 20
UNROLL = 8
NT = (((1,), (1,)), ((), ()))
VMEM = pl.BlockSpec(memory_space=pltpu.VMEM)
SMEM = pl.BlockSpec(memory_space=pltpu.SMEM)
ANY = pl.BlockSpec(memory_space=pl.ANY)


def swap(value):
    return lax.ppermute(value, CORE, [(0, 1), (1, 0)])


def spread(value):
    return lax.all_to_all(value, CHIPS, split_axis=0, concat_axis=0, tiled=True)


def in_hbm(value):
    return pltpu.with_memory_space_constraint(value, pltpu.HBM)


def other_half(value):
    lanes = value.shape[1] // 2
    return jnp.concatenate([value[:, lanes:], value[:, :lanes]], axis=1)


def low_lanes(value):
    return lax.broadcasted_iota(jnp.int32, value.shape, 1) < value.shape[1] // 2


def regroup_kernel(first, core_ref, raw_ref, *refs):
    if first:
        z_ref, own_live_ref, sent_live_ref, *refs = refs
    own_ref, sent_ref, *refs = refs
    if first:
        keep_ref, send_ref, *refs = refs
    raw, own, sent, in_sems, out_sems, *refs = refs
    quads, cells, _ = own.shape
    tiles = 4 * quads
    step = cells // in_sems.shape[0]

    def arrival(piece):
        rows = pl.ds(pl.multiple_of(piece * step * tiles, 16), step * tiles)
        return pltpu.make_async_copy(raw_ref.at[rows], raw.at[rows], in_sems.at[piece])

    def departures(piece):
        at = pl.ds(pl.multiple_of(piece * step, 16), step)
        return [
            pltpu.make_async_copy(
                held.at[:, at, :], ref.at[:, at, :], out_sems.at[side, piece]
            )
            for side, (held, ref) in enumerate(((own, own_ref), (sent, sent_ref)))
        ]

    def launch(piece, carry):
        arrival(piece).start()
        return carry

    lax.fori_loop(0, in_sems.shape[0], launch, 0)
    to = lax.broadcasted_iota(jnp.int32, (256, 256), 0)
    at = lax.broadcasted_iota(jnp.int32, (256, 256), 1)
    order = (at == (to % 16) * 16 + to // 16).astype(F32).astype(BF16)
    first_core = core_ref[0] == 0

    def turn(piece, carry):
        arrival(piece).wait()
        for group in range(step // 16):
            cell = pl.multiple_of(piece * step + group * 16, 16)
            for block in range(2):
                sides = [
                    jnp.concatenate(
                        [
                            raw[pl.ds(pl.multiple_of((cell + y) * tiles + (2 * block + side) * 16, 16), 16), :]
                            for y in range(16)
                        ],
                        axis=0,
                    )
                    for side in range(2)
                ]
                low = low_lanes(sides[0])
                halves = [
                    jnp.where(low, sides[0], other_half(sides[1])),
                    jnp.where(low, other_half(sides[0]), sides[1]),
                ]
                both = jnp.concatenate(
                    [
                        jnp.where(first_core, halves[0], halves[1]),
                        jnp.where(first_core, halves[1], halves[0]),
                    ],
                    axis=1,
                )
                moved = jnp.dot(order, both, preferred_element_type=F32).astype(BF16)
                lanes = slice(block * 128, block * 128 + 128)
                for q in range(16):
                    own[q, pl.ds(cell, 16), lanes] = moved[q * 16 : (q + 1) * 16, :128]
                    sent[q, pl.ds(cell, 16), lanes] = moved[q * 16 : (q + 1) * 16, 128:]
        for copy in departures(piece):
            copy.start()
        return carry

    lax.fori_loop(0, in_sems.shape[0], turn, 0)
    if first:
        (values,) = refs
        values[...] = z_ref[...].astype(BF16)
        for held, live_ref, out_ref in (
            (sent, sent_live_ref, send_ref),
            (own, own_live_ref, keep_ref),
        ):
            def factor(q):
                return jnp.dot(values[...], held[q], preferred_element_type=F32)

            project(factor, quads, live_ref, out_ref)

    def finish(piece, carry):
        for copy in departures(piece):
            copy.wait()
        return carry

    lax.fori_loop(0, in_sems.shape[0], finish, 0)


def regroup(factors, core, z=None, lives=(), coefficients=None):
    cells, tiles, ranked = factors.shape
    quads = tiles // 4
    first = z is not None
    shape = (quads, cells, 2 * ranked)
    parts = 8
    scratch = [
        pltpu.VMEM((cells * tiles, ranked), BF16),
        pltpu.VMEM(shape, BF16),
        pltpu.VMEM(shape, BF16),
        pltpu.SemaphoreType.DMA((parts,)),
        pltpu.SemaphoreType.DMA((2, parts)),
    ]
    if first:
        scratch.append(pltpu.VMEM(z.shape, BF16))
    return pl.pallas_call(
        functools.partial(regroup_kernel, first),
        in_specs=[SMEM, ANY] + [VMEM] * (3 if first else 0),
        out_specs=[ANY] * 2 + [VMEM] * (2 if first else 0),
        out_shape=[pltpu.HBM(shape, BF16)] * 2
        + ([jax.ShapeDtypeStruct(*coefficients)] * 2 if first else []),
        scratch_shapes=scratch,
        compiler_params=pltpu.CompilerParams(vmem_limit_bytes=24 << 20),
        cost_estimate=pl.CostEstimate(
            flops=8_000_000_000, bytes_accessed=1 << 24, transcendentals=0
        ),
    )(core, in_hbm(factors.reshape(cells * tiles, ranked)), *((z, *lives) if first else ()))


def merge_kernel(after_ref, own_ref, other_ref, out_ref, sems):
    copies = [
        pltpu.make_async_copy(ref, out_ref.at[side], sems.at[side])
        for side, ref in enumerate((own_ref, other_ref))
    ]
    for copy in copies:
        copy.start()
    for copy in copies:
        copy.wait()


def merge(after, own, other):
    return pl.pallas_call(
        merge_kernel,
        in_specs=[ANY, ANY, ANY],
        out_specs=VMEM,
        out_shape=jax.ShapeDtypeStruct((2, *own.shape), own.dtype),
        scratch_shapes=[pltpu.SemaphoreType.DMA((2,))],
        compiler_params=pltpu.CompilerParams(vmem_limit_bytes=1 << 20),
        cost_estimate=pl.CostEstimate(
            flops=4_000_000_000, bytes_accessed=1 << 24, transcendentals=0
        ),
    )(after, in_hbm(own), in_hbm(other))


def expand_kernel(coefficient_ref, f_ref, total_ref, left):
    quads, cells = f_ref.shape[1], f_ref.shape[2]
    half = coefficient_ref.shape[1]

    def arrange(q, carry):
        for pair in range(2):
            one = coefficient_ref[q + 32 * pair]
            two = coefficient_ref[q + 32 * pair + 16]
            low = low_lanes(one)
            lanes = slice(pair * 128, pair * 128 + 128)
            left[q, :half, lanes] = jnp.where(low, one, other_half(two))
            left[q, half:, lanes] = jnp.where(low, other_half(one), two)
        return carry

    lax.fori_loop(0, quads, arrange, 0, unroll=2)
    for side in range(2):
        def block(index, carry):
            at_cell = pl.ds(pl.multiple_of(index * 256, 256), 256)
            total_ref[:, pl.ds(pl.multiple_of(side * cells + index * 256, 256), 256)] = sum(
                lax.dot_general(
                    left[q], f_ref[side, q, at_cell, :], NT, preferred_element_type=F32
                )
                for q in range(quads)
            )
            return carry

        lax.fori_loop(0, cells // 256, block, 0, unroll=2)


def project(factor, quads, live_ref, out_ref):
    half = out_ref.shape[1]
    low = lax.broadcasted_iota(jnp.int32, (half, 128), 1) < 64

    def quad(q, carry):
        moved = factor(q)
        for pair in range(2):
            one, two = q + 32 * pair, q + 32 * pair + 16
            part = moved[:, pair * 128 : pair * 128 + 128] * live_ref[pair * 16 + q, :1]
            part = part.astype(BF16)
            turned = other_half(part)
            out_ref[one] = jnp.where(low, part[:half], turned[half:])
            out_ref[two] = jnp.where(low, turned[:half], part[half:])
        return carry

    lax.fori_loop(0, quads, quad, 0, unroll=UNROLL)


def project_both(values, f_ref, live_ref, out_ref):
    cells = f_ref.shape[2]

    def factor(q):
        return jnp.dot(
            values[:, :cells], f_ref[0, q], preferred_element_type=F32
        ) + jnp.dot(values[:, cells:], f_ref[1, q], preferred_element_type=F32)

    project(factor, f_ref.shape[1], live_ref, out_ref)


def complete(total_ref, arrived_ref):
    cells = total_ref.shape[1] // 2
    return [
        total_ref[:, :cells] + arrived_ref[:, cells:],
        total_ref[:, cells:] + arrived_ref[:, :cells],
    ]


def row_kernel(
    live_ref, total_ref, arrived_ref, base_ref, rate_ref, f_ref,
    out_ref, *refs,
):
    *energy_ref, values = refs
    cells = total_ref.shape[1] // 2
    for side, field in enumerate(complete(total_ref, arrived_ref)):
        at = slice(side * cells, (side + 1) * cells)
        rate = rate_ref[:, at]
        exponent = base_ref[:, at] + field
        intensity = jnp.exp(exponent)
        values[:, at] = (rate - intensity).astype(BF16)
        if side == 0 and energy_ref:
            energy_ref[0][...] = jnp.sum(intensity - rate * exponent, axis=1, keepdims=True)
    project_both(values, f_ref, live_ref, out_ref)


def col_kernel(
    weight, live_ref, total_ref, arrived_ref, step_ref, z_ref, m_ref,
    f_ref, out_ref, new_z_ref, new_m_ref, values,
):
    cells = total_ref.shape[1] // 2
    step = step_ref[:, :1]
    for side, pulled in enumerate(complete(total_ref, arrived_ref)):
        at = slice(side * cells, (side + 1) * cells)
        z = z_ref[:, at]
        moment = m_ref[:, at] - weight * step * (z - pulled)
        z = z + step * moment
        new_m_ref[:, at] = moment
        new_z_ref[:, at] = z
        values[:, at] = z.astype(BF16)
    project_both(values, f_ref, live_ref, out_ref)


def last_kernel(
    total_ref, arrived_ref, step_ref, z_ref, m_ref, start_z_ref, start_m_ref,
    start_energy_ref, end_energy_ref, new_m_ref, change_ref,
):
    cells = total_ref.shape[1] // 2
    z = z_ref[:, :cells]
    moment = m_ref[:, :cells] - 0.5 * step_ref[:, :1] * (
        z - complete(total_ref, arrived_ref)[0]
    )
    new_m_ref[...] = moment
    start_z = start_z_ref[:, :cells]
    start_m = start_m_ref[:, :cells]
    pieces = 0.5 * (z * z - start_z * start_z + moment * moment - start_m * start_m)
    change_ref[...] = (
        jnp.sum(pieces, axis=1, keepdims=True) + end_energy_ref[...] - start_energy_ref[...]
    )


def call(kernel, specs, outs, scratch, flops, *args):
    return pl.pallas_call(
        kernel,
        in_specs=specs,
        out_specs=[VMEM] * len(outs),
        out_shape=[jax.ShapeDtypeStruct(*o) for o in outs],
        scratch_shapes=scratch,
        compiler_params=pltpu.CompilerParams(vmem_limit_bytes=LIMIT),
        cost_estimate=pl.CostEstimate(
            flops=flops, bytes_accessed=1 << 24, transcendentals=0
        ),
    )(*args)


def on_device(
    position, momentum, row_factors, col_factors, tile_ranks, log_mean, counts, step_size
):
    chains, cells = position.shape
    half = chains // 2
    tiles, ranked = tile_ranks.shape[0], row_factors.shape[2]
    tile = lax.axis_index(CHIPS)
    core = lax.axis_index(CORE).astype(jnp.int32)[None]
    lane = jnp.arange(ranked, dtype=jnp.int32)

    def live(ranks, which):
        tops = ranks.reshape(2, 2, tiles // 4)
        top = jnp.where(lane < ranked // 2, tops[:, 0, :, None], tops[:, 1, :, None])
        level = lane % (ranked // 2) + ranked // 2 * which
        alive = (level < top).astype(F32).reshape(tiles // 2, 1, ranked)
        return jnp.broadcast_to(alive, (tiles // 2, 8, ranked))

    col_ranks = lax.dynamic_slice_in_dim(tile_ranks, tile, 1, 1)[:, 0]
    row_ranks = lax.dynamic_slice_in_dim(tile_ranks, tile, 1, 0)[0]
    col_live, sent_live = live(col_ranks, core[0]), live(col_ranks, 1 - core[0])
    row_live = live(row_ranks, core[0])

    coefficients = ((tiles, half, ranked), BF16)
    state = ((chains, 2 * cells), F32)
    own_state = ((chains, cells), F32)
    column = ((chains, 1), F32)
    values = [pltpu.VMEM((chains, 2 * cells), BF16)]
    left = [pltpu.VMEM((tiles // 4, chains, 2 * ranked), BF16)]
    work = 2 * chains * 2 * cells * tiles * ranked // 2

    z_other = swap(position)
    col_own, col_sent, keep, send = regroup(
        col_factors, core, position, (col_live, sent_live), coefficients
    )
    arrived = swap(send)
    out = (keep.astype(F32) + arrived.astype(F32)).astype(BF16)
    start_z = jnp.concatenate([position, z_other], axis=1)
    start_m = jnp.concatenate([momentum, swap(momentum)], axis=1)
    rate = counts.astype(F32)
    base = jnp.concatenate([log_mean, swap(log_mean)])[None, :]
    rate = jnp.concatenate([rate, swap(rate)])[None, :]
    step = jnp.broadcast_to(step_size[:, None], (chains, ranked))

    def expand(coefficient, factors):
        (total,) = call(
            expand_kernel, [VMEM] * 2, [state], left, 2 * work, coefficient, factors
        )
        return total, swap(total)

    def row_pass(arrived, energy=True):
        return call(
            row_kernel, [VMEM] * 6, [coefficients] + [column] * energy, values, work,
            row_live, *expand(arrived, row), base, rate, row,
        )

    col_sent, out, start_z, start_m, base, rate, step, row_live, row_raw = (
        lax.optimization_barrier(
            (col_sent, out, start_z, start_m, base, rate, step, row_live, row_factors)
        )
    )
    row_own, row_sent = regroup(row_raw, core)
    row_other = swap(row_sent)
    col_other = swap(col_sent)
    z, m = start_z, start_m
    arrived = spread(out)
    row = merge(arrived, row_own, row_other)
    out, start_energy = row_pass(arrived)
    out, col_other = lax.optimization_barrier((out, col_other))
    arrived = spread(out)
    col = merge(arrived, col_own, col_other)
    for weight in (0.5, 1.0):
        out, z, m = call(
            functools.partial(col_kernel, weight),
            [VMEM] * 7, [coefficients, state, state], values, work,
            col_live, *expand(arrived, col), step, z, m, col,
        )
        last = weight == 1.0
        out, *energy = row_pass(spread(out), last)
        arrived = spread(out)
    (end_energy,) = energy
    m, change = call(
        last_kernel, [VMEM] * 9, [own_state, column], [], 1 << 24,
        *expand(arrived, col), step, z, m, start_z, start_m,
        start_energy, end_energy,
    )
    change = change[:, 0]
    change = change + swap(change)
    change = spread(jnp.broadcast_to(change[None], (tiles, chains))).sum(axis=0)
    return z[:, :cells], m, change


def solution(mesh):
    split = Mesh(
        mesh.devices.reshape(4, 4, 4, 2), ("col_0", "col_1", "row_0", "row_1")
    )
    return jax.shard_map(
        on_device,
        mesh=split,
        in_specs=(
            P(None, COL_ROW),
            P(None, COL_ROW),
            P(COL_ROW, None, None),
            P(COL_ROW, None, None),
            P(),
            P(COL_ROW),
            P(COL_ROW),
            P(),
        ),
        out_specs=(P(None, COL_ROW), P(None, COL_ROW), P()),
        check_vma=False,
    )
```

time: 259 us -> 243 us (0.938)
  blocking collectives: 107 us -> 135 us
  waiting for transfers between devices: 41.3 us -> 19.7 us
  Pallas kernels: 72.5 us -> 55.9 us
  starting transfers between devices: 34.1 us -> 23.4 us
  local copies, waits for them, and re-layouts: 1.65 us -> 5.86 us
    all_to_all x5 -> x6, blocking collectives: 107 us -> 135 us  [spread(): return lax.all_to_all(value, CHIPS, split_axis=0, concat_axis=0, tiled=True)]
    all_to_all x2 -> x1, waiting for transfers between devices: 24.7 us -> 7.66 us  [spread(): return lax.all_to_all(value, CHIPS, split_axis=0, concat_axis=0, tiled=True)]
    all_to_all x2 -> x1, starting transfers between devices: 15.9 us -> 4.55 us  [spread(): return lax.all_to_all(value, CHIPS, split_axis=0, concat_axis=0, tiled=True)]
    pallas_call x13 -> x12, Pallas kernels: 41 us -> 31.3 us  [call(): pl.pallas_call(kernel, in_specs=specs, out_specs=[VMEM] * len(outs), out_...]
    pallas_call x2, Pallas kernels: 24.5 us -> 17.6 us  [regroup(): pl.pallas_call(functools.partial(regroup_kernel, first), in_specs=[SMEM,...]
    ppermute x13 -> x14, waiting for transfers between devices: 16.5 us -> 12.1 us  [swap(): return lax.ppermute(value, CORE, [(0, 1), (1, 0)])]
    unnamed x20, local copies, waits for them, and re-layouts: 0.05 us -> 3.68 us
    ppermute x13 -> x14, starting transfers between devices: 18.2 us -> 18.9 us  [swap(): return lax.ppermute(value, CORE, [(0, 1), (1, 0)])]
  transfers between devices with their start and end apart: 15 -> 15, of which waited for: 11 -> 10; matrix products, arithmetic and copies ran while one was open for 0% -> 0% of each run, Pallas kernels for 12% -> 4%
where the time goes in v2:
time: 243 us; the launch traced here: 242 us
  blocking collectives  135 us (56%)
  Pallas kernels  55.9 us (23%)
  starting transfers between devices  23.4 us (10%)
  waiting for transfers between devices  19.7 us (8%)
  local copies, waits for them, and re-layouts  5.86 us (2%)
    all_to_all x6, blocking collectives, spread(): return lax.all_to_all(value, CHIPS, split_axis=0, concat_axis=0, tiled=True)  135 us
    pallas_call x12, Pallas kernels, call(): pl.pallas_call(kernel, in_specs=specs, out_specs=[VMEM] * len(outs), out_...  31.3 us
    ppermute x14, starting transfers between devices, swap(): return lax.ppermute(value, CORE, [(0, 1), (1, 0)])  18.9 us
    pallas_call x2, Pallas kernels, regroup(): pl.pallas_call(functools.partial(regroup_kernel, first), in_specs=[SMEM,...  17.6 us
    ppermute x14, waiting for transfers between devices, swap(): return lax.ppermute(value, CORE, [(0, 1), (1, 0)])  12.1 us
    all_to_all x1, waiting for transfers between devices, spread(): return lax.all_to_all(value, CHIPS, split_axis=0, concat_axis=0, tiled=True)  7.66 us
    pallas_call x2, Pallas kernels, merge(): pl.pallas_call(merge_kernel, in_specs=[ANY, ANY, ANY], out_specs=VMEM, ou...  6.97 us
  transfers between devices with their start and end apart: 15, of which 10 were waited for; matrix products, arithmetic and copies ran while one was open for 0% of the time, Pallas kernels for 4%

profile of v2, /device:TPU:1, one launch (start us, length us, event | category | flops | bytes accessed | tf_op | source)
XLA Modules:
  0.0 242.1 jit_solution(1246007448779371642)
XLA Ops:
  0.7 0.7 copy-done
  2.3 0.9 copy-done.2
  3.2 9.3 %shard_map.103 = (bf16[16,512,256]{2,1,0:T(8,128)(2,1)}, bf16[16,512,256]{2,1,0:T(8,128)(2,1)}, bf16[64,64,128]{2,1,0:T(8,128)(2,1)S(1)}, bf16[64,64,128]{2,1,0:T(8,128)(2,1)S(1)}) custom-call(s32[1]{0:T(128)} %bitcast.core_ref, bf16[32768,128]{1,0:T(8,128)(2,1)} %bitcast.13, f32[128,512]{1,0:T(8,128)S(1)} %copy-done.2, ...), custom_call_target="tpu_custom_call" | custom-call | flops 8000000000 | bytes 16777216 | tf_op jit(solution)/shard_map/pallas_call | solution.py:151
  12.5 1.5 collective-permute-start
  14.1 0.4 collective-permute-start.4
  15.0 1.6 collective-permute-done.4
  17.7 8.3 %shard_map.104 = (bf16[16,512,256]{2,1,0:T(8,128)(2,1)}, bf16[16,512,256]{2,1,0:T(8,128)(2,1)}) custom-call(s32[1]{0:T(128)} %bitcast.core_ref, bf16[32768,128]{1,0:T(8,128)(2,1)} %bitcast.14), custom_call_target="tpu_custom_call" | custom-call | flops 8000000000 | bytes 16777216 | tf_op jit(solution)/shard_map/pallas_call | solution.py:151
  26.0 0.5 collective-permute-start.5
  26.6 28.1 %all_to_all.36.after_ref.coefficient_ref = bf16[64,64,128]{2,1,0:T(8,128)(2,1)S(1)} all-to-all(bf16[64,64,128]{2,1,0:T(8,128)(2,1)S(1)} %add_convert_fusion), channel_id=1, replica_groups=mesh['col_0'=4,'col_1'=4,'row_0'=4,'row_1'=2] {'col_0','col_1','row_0'}, dimensions={0} | all-to-all | bytes 2097152 | tf_op jit(solution)/shard_map/all_to_all | solution.py:29
  54.7 2.0 copy-done.4
  56.6 3.5 %shard_map.105.f_ref = bf16[2,16,512,256]{3,2,1,0:T(8,128)(2,1)S(1)} custom-call(bf16[64,64,128]{2,1,0:T(8,128)(2,1)S(1)} %all_to_all.36.after_ref.coefficient_ref, bf16[16,512,256]{2,1,0:T(8,128)(2,1)} %get-tuple-element.38.own_ref, bf16[16,512,256]{2,1,0:T(8,128)(2,1)} %copy-done.4), custom_call_target="tpu_custom_call" | custom-call | flops 4000000000 | bytes 16777216 | tf_op jit(solution)/shard_map/pallas_call | solution.py:177
  60.1 3.6 %shard_map.106.total_ref = f32[128,1024]{1,0:T(8,128)S(1)} custom-call(bf16[64,64,128]{2,1,0:T(8,128)(2,1)S(1)} %all_to_all.36.after_ref.coefficient_ref, bf16[2,16,512,256]{3,2,1,0:T(8,128)(2,1)S(1)} %shard_map.105.f_ref), custom_call_target="tpu_custom_call" | custom-call | flops 2147483648 | bytes 16777216 | tf_op jit(solution)/shard_map/pallas_call | solution.py:309
  63.7 2.5 %collective-permute-start.6 = (f32[128,1024]{1,0:T(8,128)S(1)}, f32[128,1024]{1,0:T(8,128)S(1)}, u32[]{:S(2)}, u32[]{:S(2)}) collective-permute-start(f32[128,1024]{1,0:T(8,128)S(1)} %shard_map.106.total_ref), channel_id=1, source_target_pairs={{0,1},{1,0},{2,3},{3,2},{4,5},{5,4},{6,7},{7,6},{8,9},{9,8},{10,11... | collective-permute-start | bytes 1572872 | tf_op jit(solution)/shard_map/ppermute | solution.py:25
  66.2 1.5 collective-permute-done.6.arrived_ref
  67.8 1.8 shard_map.107
  69.6 21.4 %all_to_all.37.after_ref.coefficient_ref = bf16[64,64,128]{2,1,0:T(8,128)(2,1)S(1)} all-to-all(bf16[64,64,128]{2,1,0:T(8,128)(2,1)S(1)} %get-tuple-element.44), channel_id=1, replica_groups=mesh['col_0'=4,'col_1'=4,'row_0'=4,'row_1'=2] {'col_0','col_1','row_0'}, dimensions={0} | all-to-all | bytes 2097152 | tf_op jit(solution)/shard_map/all_to_all | solution.py:29
  91.0 3.5 %shard_map.108.f_ref = bf16[2,16,512,256]{3,2,1,0:T(8,128)(2,1)S(1)} custom-call(bf16[64,64,128]{2,1,0:T(8,128)(2,1)S(1)} %all_to_all.37.after_ref.coefficient_ref, bf16[16,512,256]{2,1,0:T(8,128)(2,1)} %get-tuple-element.45.own_ref, bf16[16,512,256]{2,1,0:T(8,128)(2,1)} %copy-done.3), custom_call_target="tpu_custom_call" | custom-call | flops 4000000000 | bytes 16777216 | tf_op jit(solution)/shard_map/pallas_call | solution.py:177
  94.5 3.6 %shard_map.109.total_ref = f32[128,1024]{1,0:T(8,128)S(1)} custom-call(bf16[64,64,128]{2,1,0:T(8,128)(2,1)S(1)} %all_to_all.37.after_ref.coefficient_ref, bf16[2,16,512,256]{3,2,1,0:T(8,128)(2,1)S(1)} %shard_map.108.f_ref), custom_call_target="tpu_custom_call" | custom-call | flops 2147483648 | bytes 16777216 | tf_op jit(solution)/shard_map/pallas_call | solution.py:309
  98.1 2.7 %collective-permute-start.8 = (f32[128,1024]{1,0:T(8,128)S(1)}, f32[128,1024]{1,0:T(8,128)S(1)}, u32[]{:S(2)}, u32[]{:S(2)}) collective-permute-start(f32[128,1024]{1,0:T(8,128)S(1)} %shard_map.109.total_ref), channel_id=1, source_target_pairs={{0,1},{1,0},{2,3},{3,2},{4,5},{5,4},{6,7},{7,6},{8,9},{9,8},{10,11... | collective-permute-start | bytes 1572872 | tf_op jit(solution)/shard_map/ppermute | solution.py:25
  100.8 1.5 collective-permute-done.8.arrived_ref
  102.4 1.8 shard_map.110
  104.2 21.4 %all_to_all.38.coefficient_ref = bf16[64,64,128]{2,1,0:T(8,128)(2,1)S(1)} all-to-all(bf16[64,64,128]{2,1,0:T(8,128)(2,1)S(1)} %get-tuple-element.50), channel_id=1, replica_groups=mesh['col_0'=4,'col_1'=4,'row_0'=4,'row_1'=2] {'col_0','col_1','row_0'}, dimensions={0} | all-to-all | bytes 2097152 | tf_op jit(solution)/shard_map/all_to_all | solution.py:29
  125.6 3.6 %shard_map.111.total_ref = f32[128,1024]{1,0:T(8,128)S(1)} custom-call(bf16[64,64,128]{2,1,0:T(8,128)(2,1)S(1)} %all_to_all.38.coefficient_ref, bf16[2,16,512,256]{3,2,1,0:T(8,128)(2,1)S(1)} %shard_map.105.f_ref), custom_call_target="tpu_custom_call" | custom-call | flops 2147483648 | bytes 16777216 | tf_op jit(solution)/shard_map/pallas_call | solution.py:309
  129.2 2.5 %collective-permute-start.9 = (f32[128,1024]{1,0:T(8,128)S(1)}, f32[128,1024]{1,0:T(8,128)S(1)}, u32[]{:S(2)}, u32[]{:S(2)}) collective-permute-start(f32[128,1024]{1,0:T(8,128)S(1)} %shard_map.111.total_ref), channel_id=1, source_target_pairs={{0,1},{1,0},{2,3},{3,2},{4,5},{5,4},{6,7},{7,6},{8,9},{9,8},{10,11... | collective-permute-start | bytes 1572872 | tf_op jit(solution)/shard_map/ppermute | solution.py:25
  131.7 1.5 collective-permute-done.9.arrived_ref
  133.2 1.7 shard_map.112
  134.9 21.4 %all_to_all.39.coefficient_ref = bf16[64,64,128]{2,1,0:T(8,128)(2,1)S(1)} all-to-all(bf16[64,64,128]{2,1,0:T(8,128)(2,1)S(1)} %shard_map.112), channel_id=1, replica_groups=mesh['col_0'=4,'col_1'=4,'row_0'=4,'row_1'=2] {'col_0','col_1','row_0'}, dimensions={0} | all-to-all | bytes 2097152 | tf_op jit(solution)/shard_map/all_to_all | solution.py:29
  156.3 3.6 %shard_map.113.total_ref = f32[128,1024]{1,0:T(8,128)S(1)} custom-call(bf16[64,64,128]{2,1,0:T(8,128)(2,1)S(1)} %all_to_all.39.coefficient_ref, bf16[2,16,512,256]{3,2,1,0:T(8,128)(2,1)S(1)} %shard_map.108.f_ref), custom_call_target="tpu_custom_call" | custom-call | flops 2147483648 | bytes 16777216 | tf_op jit(solution)/shard_map/pallas_call | solution.py:309
  159.9 2.5 %collective-permute-start.10 = (f32[128,1024]{1,0:T(8,128)S(1)}, f32[128,1024]{1,0:T(8,128)S(1)}, u32[]{:S(2)}, u32[]{:S(2)}) collective-permute-start(f32[128,1024]{1,0:T(8,128)S(1)} %shard_map.113.total_ref), channel_id=1, source_target_pairs={{0,1},{1,0},{2,3},{3,2},{4,5},{5,4},{6,7},{7,6},{8,9},{9,8},{10,11... | collective-permute-start | bytes 1572872 | tf_op jit(solution)/shard_map/ppermute | solution.py:25
  162.5 1.5 collective-permute-done.10.arrived_ref
  164.0 1.8 shard_map.114
  165.8 21.4 %all_to_all.40.coefficient_ref = bf16[64,64,128]{2,1,0:T(8,128)(2,1)S(1)} all-to-all(bf16[64,64,128]{2,1,0:T(8,128)(2,1)S(1)} %get-tuple-element.54), channel_id=1, replica_groups=mesh['col_0'=4,'col_1'=4,'row_0'=4,'row_1'=2] {'col_0','col_1','row_0'}, dimensions={0} | all-to-all | bytes 2097152 | tf_op jit(solution)/shard_map/all_to_all | solution.py:29
  187.2 3.6 %shard_map.115.total_ref = f32[128,1024]{1,0:T(8,128)S(1)} custom-call(bf16[64,64,128]{2,1,0:T(8,128)(2,1)S(1)} %all_to_all.40.coefficient_ref, bf16[2,16,512,256]{3,2,1,0:T(8,128)(2,1)S(1)} %shard_map.105.f_ref), custom_call_target="tpu_custom_call" | custom-call | flops 2147483648 | bytes 16777216 | tf_op jit(solution)/shard_map/pallas_call | solution.py:309
  190.8 2.5 %collective-permute-start.11 = (f32[128,1024]{1,0:T(8,128)S(1)}, f32[128,1024]{1,0:T(8,128)S(1)}, u32[]{:S(2)}, u32[]{:S(2)}) collective-permute-start(f32[128,1024]{1,0:T(8,128)S(1)} %shard_map.115.total_ref), channel_id=1, source_target_pairs={{0,1},{1,0},{2,3},{3,2},{4,5},{5,4},{6,7},{7,6},{8,9},{9,8},{10,11... | collective-permute-start | bytes 1572872 | tf_op jit(solution)/shard_map/ppermute | solution.py:25
  193.3 1.5 collective-permute-done.11.arrived_ref
  194.9 1.8 shard_map.116
  196.7 21.4 %all_to_all.41.coefficient_ref = bf16[64,64,128]{2,1,0:T(8,128)(2,1)S(1)} all-to-all(bf16[64,64,128]{2,1,0:T(8,128)(2,1)S(1)} %get-tuple-element.55), channel_id=1, replica_groups=mesh['col_0'=4,'col_1'=4,'row_0'=4,'row_1'=2] {'col_0','col_1','row_0'}, dimensions={0} | all-to-all | bytes 2097152 | tf_op jit(solution)/shard_map/all_to_all | solution.py:29
  218.1 3.6 %shard_map.117.total_ref = f32[128,1024]{1,0:T(8,128)S(1)} custom-call(bf16[64,64,128]{2,1,0:T(8,128)(2,1)S(1)} %all_to_all.41.coefficient_ref, bf16[2,16,512,256]{3,2,1,0:T(8,128)(2,1)S(1)} %shard_map.108.f_ref), custom_call_target="tpu_custom_call" | custom-call | flops 2147483648 | bytes 16777216 | tf_op jit(solution)/shard_map/pallas_call | solution.py:309
  221.7 2.5 %collective-permute-start.12 = (f32[128,1024]{1,0:T(8,128)S(1)}, f32[128,1024]{1,0:T(8,128)S(1)}, u32[]{:S(2)}, u32[]{:S(2)}) collective-permute-start(f32[128,1024]{1,0:T(8,128)S(1)} %shard_map.117.total_ref), channel_id=1, source_target_pairs={{0,1},{1,0},{2,3},{3,2},{4,5},{5,4},{6,7},{7,6},{8,9},{9,8},{10,11... | collective-permute-start | bytes 1572872 | tf_op jit(solution)/shard_map/ppermute | solution.py:25
  224.2 1.5 collective-permute-done.12.arrived_ref
  225.8 0.9 shard_map.118
  226.7 0.5 collective-permute-start.13
  227.2 0.8 collective-permute-done.13
  228.0 0.6 broadcast_in_dim.103
  228.6 4.6 %all-to-all-start.6 = ((f32[64,1,128]{2,1,0:T(1,128)}), f32[64,1,128]{2,1,0:T(1,128)S(1)}, u32[]{:S(2)}, u32[]{:S(2)}) async-start(f32[64,1,128]{2,1,0:T(1,128)} %broadcast_in_dim.103), calls=%async_computation.6 | async-start | bytes 65536 | tf_op jit(solution)/shard_map/all_to_all | solution.py:29
  233.2 0.7 slice.21
  233.9 7.7 %all-to-all-done.6 = f32[64,1,128]{2,1,0:T(1,128)S(1)} async-done(((f32[64,1,128]{2,1,0:T(1,128)}), f32[64,1,128]{2,1,0:T(1,128)S(1)}, u32[]{:S(2)}, u32[]{:S(2)}) %all-to-all-start.6) | async-done | bytes 32800 | tf_op jit(solution)/shard_map/all_to_all | solution.py:29
  241.6 0.5 reduce_sum.9
  (51 shorter events, 2.7 us)
Async XLA Ops:
  0.6 0.8 copy-start
  2.3 1.0 copy-start.2
  3.2 10.8 %copy-start.5 = (f32[128,512]{1,0:T(8,128)S(1)}, f32[128,512]{1,0:T(8,128)}, u32[]{:S(2)}) copy-start(f32[128,512]{1,0:T(8,128)} %param.9) | copy-start | bytes 786436
  3.2 10.9 %copy-start.6 = (s32[512]{0:T(512)S(1)}, s32[512]{0:T(512)}, u32[]{:S(2)}) copy-start(s32[512]{0:T(512)} %param.14) | copy-start | bytes 6148
  3.2 11.4 %copy-start.7 = (f32[512]{0:T(512)S(1)}, f32[512]{0:T(512)}, u32[]{:S(2)}) copy-start(f32[512]{0:T(512)} %param.13) | copy-start | bytes 6148
  12.5 5.0 %copy-start.8 = (f32[128]{0:T(128)S(1)}, f32[128]{0:T(128)}, u32[]{:S(2)}) copy-start(f32[128]{0:T(128)} %param.15) | copy-start | bytes 1540
  12.5 4.6 %collective-permute-start = (bf16[64,64,128]{2,1,0:T(8,128)(2,1)S(1)}, bf16[64,64,128]{2,1,0:T(8,128)(2,1)S(1)}, u32[]{:S(2)}, u32[]{:S(2)}) collective-permute-start(bf16[64,64,128]{2,1,0:T(8,128)(2,1)S(1)} %get-tuple-element.34), channel_id=1, source_target_pairs={{0,1},{1,0},{2,3},{3,2},{4,5},{5,4},{6,7},{7,6},{8,9},{9,8},{10,11... | collective-permute-start | bytes 3145736 | tf_op jit(solution)/shard_map/ppermute | solution.py:25
  14.0 3.1 %collective-permute-start.2 = (f32[128,512]{1,0:T(8,128)S(1)}, f32[128,512]{1,0:T(8,128)S(1)}, u32[]{:S(2)}, u32[]{:S(2)}) collective-permute-start(f32[128,512]{1,0:T(8,128)S(1)} %copy-done.5), channel_id=1, source_target_pairs={{0,1},{1,0},{2,3},{3,2},{4,5},{5,4},{6,7},{7,6},{8,9},{9,8},{10,11... | collective-permute-start | bytes 786440 | tf_op jit(solution)/shard_map/ppermute | solution.py:25
  14.1 2.6 %collective-permute-start.4 = (f32[512]{0:T(512)S(1)}, f32[512]{0:T(512)S(1)}, u32[]{:S(2)}, u32[]{:S(2)}) collective-permute-start(f32[512]{0:T(512)S(1)} %convert_element_type.38), channel_id=1, source_target_pairs={{0,1},{1,0},{2,3},{3,2},{4,5},{5,4},{6,7},{7,6},{8,9},{9,8},{10,11... | collective-permute-start | bytes 6152 | tf_op jit(solution)/shard_map/ppermute | solution.py:25
  14.5 2.6 %collective-permute-start.1 = (f32[128,512]{1,0:T(8,128)S(1)}, f32[128,512]{1,0:T(8,128)S(1)}, u32[]{:S(2)}, u32[]{:S(2)}) collective-permute-start(f32[128,512]{1,0:T(8,128)S(1)} %copy-done.2), channel_id=1, source_target_pairs={{0,1},{1,0},{2,3},{3,2},{4,5},{5,4},{6,7},{7,6},{8,9},{9,8},{10,11... | collective-permute-start | bytes 786440 | tf_op jit(solution)/shard_map/ppermute | solution.py:25
  14.6 2.4 collective-permute-start.3
  17.7 8.7 %copy-start.9 = (bf16[16,512,256]{2,1,0:T(8,128)(2,1)S(1)}, bf16[16,512,256]{2,1,0:T(8,128)(2,1)}, u32[]{:S(2)}) copy-start(bf16[16,512,256]{2,1,0:T(8,128)(2,1)} %get-tuple-element.43) | copy-start | bytes 12582916
  26.0 28.7 %collective-permute-start.5 = (bf16[16,512,256]{2,1,0:T(8,128)(2,1)}, bf16[16,512,256]{2,1,0:T(8,128)(2,1)S(1)}, u32[]{:S(2)}, u32[]{:S(2)}) collective-permute-start(bf16[16,512,256]{2,1,0:T(8,128)(2,1)} %get-tuple-element.39), channel_id=1, source_target_pairs={{0,1},{1,0},{2,3},{3,2},{4,5},{5,4},{6,7},{7,6},{8,9},{9,8},{10,11... | collective-permute-start | bytes 12582920 | tf_op jit(solution)/shard_map/ppermute | solution.py:25
  26.4 43.2 %collective-permute-start.7 = (bf16[16,512,256]{2,1,0:T(8,128)(2,1)S(1)}, bf16[16,512,256]{2,1,0:T(8,128)(2,1)S(1)}, u32[]{:S(2)}, u32[]{:S(2)}) collective-permute-start(bf16[16,512,256]{2,1,0:T(8,128)(2,1)S(1)} %copy-done.9), channel_id=1, source_target_pairs={{0,1},{1,0},{2,3},{3,2},{4,5},{5,4},{6,7},{7,6},{8,9},{9,8},{10,11... | collective-permute-start | bytes 12582920 | tf_op jit(solution)/shard_map/ppermute | solution.py:25
  54.6 2.0 copy-start.4
  63.7 4.1 %collective-permute-start.6 = (f32[128,1024]{1,0:T(8,128)S(1)}, f32[128,1024]{1,0:T(8,128)S(1)}, u32[]{:S(2)}, u32[]{:S(2)}) collective-permute-start(f32[128,1024]{1,0:T(8,128)S(1)} %shard_map.106.total_ref), channel_id=1, source_target_pairs={{0,1},{1,0},{2,3},{3,2},{4,5},{5,4},{6,7},{7,6},{8,9},{9,8},{10,11... | collective-permute-start | bytes 1572872 | tf_op jit(solution)/shard_map/ppermute | solution.py:25
  69.6 21.4 %copy-start.3 = (bf16[16,512,256]{2,1,0:T(8,128)(2,1)}, bf16[16,512,256]{2,1,0:T(8,128)(2,1)S(1)}, u32[]{:S(2)}) copy-start(bf16[16,512,256]{2,1,0:T(8,128)(2,1)S(1)} %collective-permute-done.7.other_ref) | copy-start | bytes 12582916
  98.1 4.3 %collective-permute-start.8 = (f32[128,1024]{1,0:T(8,128)S(1)}, f32[128,1024]{1,0:T(8,128)S(1)}, u32[]{:S(2)}, u32[]{:S(2)}) collective-permute-start(f32[128,1024]{1,0:T(8,128)S(1)} %shard_map.109.total_ref), channel_id=1, source_target_pairs={{0,1},{1,0},{2,3},{3,2},{4,5},{5,4},{6,7},{7,6},{8,9},{9,8},{10,11... | collective-permute-start | bytes 1572872 | tf_op jit(solution)/shard_map/ppermute | solution.py:25
  129.2 4.0 %collective-permute-start.9 = (f32[128,1024]{1,0:T(8,128)S(1)}, f32[128,1024]{1,0:T(8,128)S(1)}, u32[]{:S(2)}, u32[]{:S(2)}) collective-permute-start(f32[128,1024]{1,0:T(8,128)S(1)} %shard_map.111.total_ref), channel_id=1, source_target_pairs={{0,1},{1,0},{2,3},{3,2},{4,5},{5,4},{6,7},{7,6},{8,9},{9,8},{10,11... | collective-permute-start | bytes 1572872 | tf_op jit(solution)/shard_map/ppermute | solution.py:25
  159.9 4.1 %collective-permute-start.10 = (f32[128,1024]{1,0:T(8,128)S(1)}, f32[128,1024]{1,0:T(8,128)S(1)}, u32[]{:S(2)}, u32[]{:S(2)}) collective-permute-start(f32[128,1024]{1,0:T(8,128)S(1)} %shard_map.113.total_ref), channel_id=1, source_target_pairs={{0,1},{1,0},{2,3},{3,2},{4,5},{5,4},{6,7},{7,6},{8,9},{9,8},{10,11... | collective-permute-start | bytes 1572872 | tf_op jit(solution)/shard_map/ppermute | solution.py:25
  190.8 4.1 %collective-permute-start.11 = (f32[128,1024]{1,0:T(8,128)S(1)}, f32[128,1024]{1,0:T(8,128)S(1)}, u32[]{:S(2)}, u32[]{:S(2)}) collective-permute-start(f32[128,1024]{1,0:T(8,128)S(1)} %shard_map.115.total_ref), channel_id=1, source_target_pairs={{0,1},{1,0},{2,3},{3,2},{4,5},{5,4},{6,7},{7,6},{8,9},{9,8},{10,11... | collective-permute-start | bytes 1572872 | tf_op jit(solution)/shard_map/ppermute | solution.py:25
  218.1 24.0 %copy-start.1 = (s32[64,64]{1,0:T(8,128)S(1)}, s32[64,64]{1,0:T(8,128)}, u32[]{:S(2)}) copy-start(s32[64,64]{1,0:T(8,128)} %param.12) | copy-start | bytes 49156
  221.7 4.1 %collective-permute-start.12 = (f32[128,1024]{1,0:T(8,128)S(1)}, f32[128,1024]{1,0:T(8,128)S(1)}, u32[]{:S(2)}, u32[]{:S(2)}) collective-permute-start(f32[128,1024]{1,0:T(8,128)S(1)} %shard_map.117.total_ref), channel_id=1, source_target_pairs={{0,1},{1,0},{2,3},{3,2},{4,5},{5,4},{6,7},{7,6},{8,9},{9,8},{10,11... | collective-permute-start | bytes 1572872 | tf_op jit(solution)/shard_map/ppermute | solution.py:25
  226.7 1.3 collective-permute-start.13
  228.6 12.9 %all-to-all-start.6 = ((f32[64,1,128]{2,1,0:T(1,128)}), f32[64,1,128]{2,1,0:T(1,128)S(1)}, u32[]{:S(2)}, u32[]{:S(2)}) async-start(f32[64,1,128]{2,1,0:T(1,128)} %broadcast_in_dim.103), calls=%async_computation.6 | async-start | bytes 65536 | tf_op jit(solution)/shard_map/all_to_all | solution.py:29

commit v3 on v2

v3 whole, which is shorter than its diff:
```python
import functools

import jax
import jax.numpy as jnp
from jax import lax
from jax.experimental import pallas as pl
from jax.experimental.pallas import tpu as pltpu
from jax.sharding import Mesh
from jax.sharding import PartitionSpec as P

COL_ROW = ("col_0", "col_1", "row_0", "row_1")
CHIPS = ("col_0", "col_1", "row_0")
CORE = "row_1"
BF16 = jnp.bfloat16
F32 = jnp.float32
LIMIT = 8 << 20
UNROLL = 8
NT = (((1,), (1,)), ((), ()))
VMEM = pl.BlockSpec(memory_space=pltpu.VMEM)
SMEM = pl.BlockSpec(memory_space=pltpu.SMEM)
ANY = pl.BlockSpec(memory_space=pl.ANY)


def swap(value):
    return lax.ppermute(value, CORE, [(0, 1), (1, 0)])


def spread(value):
    return lax.all_to_all(value, CHIPS, split_axis=0, concat_axis=0, tiled=True)


def in_hbm(value):
    return pltpu.with_memory_space_constraint(value, pltpu.HBM)


def other_half(value):
    lanes = value.shape[1] // 2
    return jnp.concatenate([value[:, lanes:], value[:, :lanes]], axis=1)


def low_lanes(value):
    return lax.broadcasted_iota(jnp.int32, value.shape, 1) < value.shape[1] // 2


def one_hot(index):
    to = lax.broadcasted_iota(jnp.int32, (256, 256), 0)
    at = lax.broadcasted_iota(jnp.int32, (256, 256), 1)
    return (at == index(to)).astype(F32).astype(BF16)


def tile_major(to):
    return (to % 16) * 16 + to // 16


def read_blocks(raw, cell, tiles):
    return [
        jnp.concatenate(
            [
                raw[pl.ds(pl.multiple_of((cell + y) * tiles + block * 16, 16), 16), :]
                for y in range(16)
            ],
            axis=0,
        )
        for block in range(tiles // 16)
    ]


def half_lanes(one, two, which):
    low = low_lanes(one)
    if which == 0:
        return jnp.where(low, one, other_half(two))
    return jnp.where(low, other_half(one), two)


def col_setup_kernel(
    place_ref, raw_ref, ranks_ref, z_ref, own_ref, sent_ref, keep_ref, send_ref,
    raw, moved, ranks, z, values, in_sems, out_sems, small_sems,
):
    _, quads, cells, _ = moved.shape
    tiles = 4 * quads
    parts = in_sems.shape[0]
    step = cells // parts
    core, tile = place_ref[0], place_ref[1]

    def arrival(piece):
        rows = pl.ds(pl.multiple_of(piece * step * tiles, 16), step * tiles)
        return pltpu.make_async_copy(raw_ref.at[rows], raw.at[rows], in_sems.at[piece])

    def departures(piece):
        at = pl.ds(pl.multiple_of(piece * step, 16), step)
        return [
            pltpu.make_async_copy(
                moved.at[which, :, at, :], ref.at[:, at, :], out_sems.at[side, piece]
            )
            for side, (which, ref) in enumerate(((core, own_ref), (1 - core, sent_ref)))
        ]

    def launch(piece, carry):
        arrival(piece).start()
        return carry

    lax.fori_loop(0, parts, launch, 0)
    small = [
        pltpu.make_async_copy(z_ref, z, small_sems.at[0]),
        pltpu.make_async_copy(ranks_ref, ranks, small_sems.at[1]),
    ]
    for copy in small:
        copy.start()
    order = one_hot(tile_major)

    def turn(piece, carry):
        arrival(piece).wait()
        for group in range(step // 16):
            cell = pl.multiple_of(piece * step + group * 16, 16)
            blocks = read_blocks(raw, cell, tiles)
            for pair in range(2):
                one, two = blocks[2 * pair : 2 * pair + 2]
                both = jnp.concatenate(
                    [half_lanes(one, two, 0), half_lanes(one, two, 1)], axis=1
                )
                turned = jnp.dot(order, both, preferred_element_type=F32).astype(BF16)
                lanes = slice(pair * 128, pair * 128 + 128)
                for q in range(16):
                    for which in range(2):
                        moved[which, q, pl.ds(cell, 16), lanes] = turned[
                            q * 16 : (q + 1) * 16, which * 128 : which * 128 + 128
                        ]
        for copy in departures(piece):
            copy.start()
        return carry

    lax.fori_loop(0, parts, turn, 0)
    for copy in small:
        copy.wait()
    values[...] = z[...].astype(BF16)
    lane = lax.broadcasted_iota(jnp.int32, (8, 128), 1)
    low_lane = lane < 64
    for which, out_ref in ((1 - core, send_ref), (core, keep_ref)):
        level = lane % 64 + 64 * which

        def factor(q):
            return jnp.dot(values[...], moved[which, q], preferred_element_type=F32)

        def live(pair, q):
            one = q + 32 * pair
            top = jnp.where(low_lane, ranks[one, tile], ranks[one + 16, tile])
            return (level < top).astype(F32)[:1]

        project(factor, quads, live, out_ref)

    def finish(piece, carry):
        for copy in departures(piece):
            copy.wait()
        return carry

    lax.fori_loop(0, parts, finish, 0)


def col_setup(factors, place, tile_ranks, z, coefficients):
    cells, tiles, ranked = factors.shape
    shape = (tiles // 4, cells, 2 * ranked)
    parts = 8
    return pl.pallas_call(
        col_setup_kernel,
        in_specs=[SMEM, ANY, ANY, ANY],
        out_specs=[ANY] * 2 + [VMEM] * 2,
        out_shape=[pltpu.HBM(shape, BF16)] * 2 + [jax.ShapeDtypeStruct(*coefficients)] * 2,
        scratch_shapes=[
            pltpu.VMEM((cells * tiles, ranked), BF16),
            pltpu.VMEM((2, *shape), BF16),
            pltpu.SMEM(tile_ranks.shape, jnp.int32),
            pltpu.VMEM(z.shape, F32),
            pltpu.VMEM(z.shape, BF16),
            pltpu.SemaphoreType.DMA((parts,)),
            pltpu.SemaphoreType.DMA((2, parts)),
            pltpu.SemaphoreType.DMA((2,)),
        ],
        compiler_params=pltpu.CompilerParams(vmem_limit_bytes=24 << 20),
        cost_estimate=pl.CostEstimate(
            flops=8_000_000_000, bytes_accessed=1 << 24, transcendentals=0
        ),
    )(place, in_hbm(factors.reshape(cells * tiles, ranked)), in_hbm(tile_ranks), in_hbm(z))


def row_setup_kernel(place_ref, own_raw_ref, other_raw_ref, out_ref, raw, moved, in_sems, out_sems):
    _, quads, cells, _ = moved.shape
    tiles = 4 * quads
    parts = in_sems.shape[1]
    step = cells // parts
    order = one_hot(tile_major)

    def arrival(side, piece):
        rows = pl.ds(pl.multiple_of(piece * step * tiles, 16), step * tiles)
        source = (own_raw_ref, other_raw_ref)[side]
        return pltpu.make_async_copy(
            source.at[rows], raw.at[side, rows], in_sems.at[side, piece]
        )

    def departure(side, piece):
        at = pl.ds(pl.multiple_of(piece * step, 16), step)
        return pltpu.make_async_copy(
            moved.at[side, :, at, :], out_ref.at[side, :, at, :], out_sems.at[side, piece]
        )

    for side in range(2):
        def launch(piece, carry):
            arrival(side, piece).start()
            return carry

        lax.fori_loop(0, parts, launch, 0)
    for which in range(2):
        @pl.when(place_ref[0] == which)
        def _():
            for side in range(2):
                def turn(piece, carry):
                    arrival(side, piece).wait()
                    for group in range(step // 16):
                        cell = pl.multiple_of(piece * step + group * 16, 16)
                        blocks = read_blocks(raw.at[side], cell, tiles)
                        both = jnp.concatenate(
                            [
                                half_lanes(*blocks[2 * pair : 2 * pair + 2], which)
                                for pair in range(2)
                            ],
                            axis=1,
                        )
                        turned = jnp.dot(
                            order, both, preferred_element_type=F32
                        ).astype(BF16)
                        for q in range(16):
                            moved[side, q, pl.ds(cell, 16), :] = turned[
                                q * 16 : (q + 1) * 16
                            ]
                    departure(side, piece).start()
                    return carry

                lax.fori_loop(0, parts, turn, 0)

    for side in range(2):
        def finish(piece, carry):
            departure(side, piece).wait()
            return carry

        lax.fori_loop(0, parts, finish, 0)


def row_setup(own, other, place):
    cells, tiles, ranked = own.shape
    shape = (2, tiles // 4, cells, 2 * ranked)
    parts = 8
    rows = (cells * tiles, ranked)
    return pl.pallas_call(
        row_setup_kernel,
        in_specs=[SMEM, ANY, ANY],
        out_specs=ANY,
        out_shape=pltpu.HBM(shape, BF16),
        scratch_shapes=[
            pltpu.VMEM((2, *rows), BF16),
            pltpu.VMEM(shape, BF16),
            pltpu.SemaphoreType.DMA((2, parts)),
            pltpu.SemaphoreType.DMA((2, parts)),
        ],
        compiler_params=pltpu.CompilerParams(vmem_limit_bytes=32 << 20),
        cost_estimate=pl.CostEstimate(
            flops=8_000_000_000, bytes_accessed=1 << 24, transcendentals=0
        ),
    )(place, in_hbm(own.reshape(rows)), in_hbm(other.reshape(rows)))


def merge_kernel(after_ref, *refs):
    sources, (out_ref, turned_ref, sems) = refs[:-3], refs[-3:]
    if len(sources) == 1:
        sources = sources[0].at[0], sources[0].at[1]
    quads, cells = out_ref.shape[1], out_ref.shape[2]
    size = quads // sems.shape[1]
    same = one_hot(lambda to: to)

    def copies(group):
        quad = pl.ds(group * size, size)
        return [
            pltpu.make_async_copy(
                source.at[quad], out_ref.at[side, quad], sems.at[side, group]
            )
            for side, source in enumerate(sources)
        ]

    def launch(group, carry):
        for copy in copies(group):
            copy.start()
        return carry

    lax.fori_loop(0, sems.shape[1], launch, 0)

    def turn(group, carry):
        for copy in copies(group):
            copy.wait()
        for q in range(size):
            quad = group * size + q
            for side in range(2):
                for block in range(cells // 256):
                    at_cell = slice(256 * block, 256 * block + 256)
                    turned_ref[side, quad, :, at_cell] = lax.dot_general(
                        same, out_ref[side, quad, at_cell, :], NT,
                        preferred_element_type=F32,
                    ).astype(BF16)
        return carry

    lax.fori_loop(0, sems.shape[1], turn, 0)


def merge(after, *parts):
    quads, cells, lanes = parts[0].shape[-3:]
    return pl.pallas_call(
        merge_kernel,
        in_specs=[ANY] * (1 + len(parts)),
        out_specs=[VMEM] * 2,
        out_shape=[
            jax.ShapeDtypeStruct((2, quads, cells, lanes), BF16),
            jax.ShapeDtypeStruct((2, quads, lanes, cells), BF16),
        ],
        scratch_shapes=[pltpu.SemaphoreType.DMA((2, 8))],
        compiler_params=pltpu.CompilerParams(vmem_limit_bytes=4 << 20),
        cost_estimate=pl.CostEstimate(
            flops=4_000_000_000, bytes_accessed=1 << 24, transcendentals=0
        ),
    )(after, *[in_hbm(part) for part in parts])


def add_kernel(keep_ref, arrived_ref, out_ref):
    out_ref[...] = (keep_ref[...].astype(F32) + arrived_ref[...].astype(F32)).astype(BF16)


def expand_kernel(coefficient_ref, turned_ref, total_ref, left):
    quads, cells = turned_ref.shape[1], turned_ref.shape[3]
    half = coefficient_ref.shape[1]

    def arrange(q, carry):
        for pair in range(2):
            one = coefficient_ref[q + 32 * pair]
            two = coefficient_ref[q + 32 * pair + 16]
            low = low_lanes(one)
            lanes = slice(pair * 128, pair * 128 + 128)
            left[q, :half, lanes] = jnp.where(low, one, other_half(two))
            left[q, half:, lanes] = jnp.where(low, other_half(one), two)
        return carry

    lax.fori_loop(0, quads, arrange, 0, unroll=4)

    def side_of(side, carry):
        for block in range(cells // 256):
            at_cell = slice(256 * block, 256 * block + 256)
            at = pl.ds(pl.multiple_of(side * cells + 256 * block, 256), 256)
            total_ref[:, at] = sum(
                jnp.dot(
                    left[q], turned_ref[side, q, :, at_cell], preferred_element_type=F32
                )
                for q in range(quads)
            )
        return carry

    lax.fori_loop(0, 2, side_of, 0)


def project(factor, quads, live, out_ref):
    half = out_ref.shape[1]
    low = lax.broadcasted_iota(jnp.int32, (half, 128), 1) < 64

    def quad(q, carry):
        moved = factor(q)
        for pair in range(2):
            one, two = q + 32 * pair, q + 32 * pair + 16
            part = moved[:, pair * 128 : pair * 128 + 128] * live(pair, q)
            part = part.astype(BF16)
            turned = other_half(part)
            out_ref[one] = jnp.where(low, part[:half], turned[half:])
            out_ref[two] = jnp.where(low, turned[:half], part[half:])
        return carry

    lax.fori_loop(0, quads, quad, 0, unroll=UNROLL)


def project_both(values, f_ref, live_ref, out_ref):
    cells = f_ref.shape[2]

    def factor(q):
        return jnp.dot(
            values[:, :cells], f_ref[0, q], preferred_element_type=F32
        ) + jnp.dot(values[:, cells:], f_ref[1, q], preferred_element_type=F32)

    def live(pair, q):
        return live_ref[pair * 16 + q, :1]

    project(factor, f_ref.shape[1], live, out_ref)


def complete(total_ref, arrived_ref):
    cells = total_ref.shape[1] // 2
    return [
        total_ref[:, :cells] + arrived_ref[:, cells:],
        total_ref[:, cells:] + arrived_ref[:, :cells],
    ]


def row_kernel(
    live_ref, total_ref, arrived_ref, base_ref, rate_ref, f_ref,
    out_ref, *refs,
):
    *energy_ref, values = refs
    cells = total_ref.shape[1] // 2
    for side, field in enumerate(complete(total_ref, arrived_ref)):
        at = slice(side * cells, (side + 1) * cells)
        rate = rate_ref[:, at]
        exponent = base_ref[:, at] + field
        intensity = jnp.exp(exponent)
        values[:, at] = (rate - intensity).astype(BF16)
        if side == 0 and energy_ref:
            energy_ref[0][...] = jnp.sum(intensity - rate * exponent, axis=1, keepdims=True)
    project_both(values, f_ref, live_ref, out_ref)


def col_kernel(
    weight, live_ref, total_ref, arrived_ref, step_ref, z_ref, m_ref,
    f_ref, out_ref, new_z_ref, new_m_ref, values,
):
    cells = total_ref.shape[1] // 2
    step = step_ref[:, :1]
    for side, pulled in enumerate(complete(total_ref, arrived_ref)):
        at = slice(side * cells, (side + 1) * cells)
        z = z_ref[:, at]
        moment = m_ref[:, at] - weight * step * (z - pulled)
        z = z + step * moment
        new_m_ref[:, at] = moment
        new_z_ref[:, at] = z
        values[:, at] = z.astype(BF16)
    project_both(values, f_ref, live_ref, out_ref)


def last_kernel(
    total_ref, arrived_ref, step_ref, z_ref, m_ref, start_z_ref, start_m_ref,
    start_energy_ref, end_energy_ref, new_m_ref, change_ref,
):
    cells = total_ref.shape[1] // 2
    z = z_ref[:, :cells]
    moment = m_ref[:, :cells] - 0.5 * step_ref[:, :1] * (
        z - complete(total_ref, arrived_ref)[0]
    )
    new_m_ref[...] = moment
    start_z = start_z_ref[:, :cells]
    start_m = start_m_ref[:, :cells]
    pieces = 0.5 * (z * z - start_z * start_z + moment * moment - start_m * start_m)
    change = (
        jnp.sum(pieces, axis=1, keepdims=True) + end_energy_ref[...] - start_energy_ref[...]
    )
    row = jnp.transpose(jnp.broadcast_to(change, (change.shape[0], change.shape[0])))[:1]
    change_ref[...] = jnp.broadcast_to(row[None], change_ref.shape)


def call(kernel, specs, outs, scratch, flops, *args):
    return pl.pallas_call(
        kernel,
        in_specs=specs,
        out_specs=[VMEM] * len(outs),
        out_shape=[jax.ShapeDtypeStruct(*o) for o in outs],
        scratch_shapes=scratch,
        compiler_params=pltpu.CompilerParams(vmem_limit_bytes=LIMIT),
        cost_estimate=pl.CostEstimate(
            flops=flops, bytes_accessed=1 << 24, transcendentals=0
        ),
    )(*args)


def on_device(
    position, momentum, row_factors, col_factors, tile_ranks, log_mean, counts, step_size
):
    chains, cells = position.shape
    half = chains // 2
    tiles, ranked = tile_ranks.shape[0], row_factors.shape[2]
    tile = lax.axis_index(CHIPS)
    core = lax.axis_index(CORE).astype(jnp.int32)
    place = jnp.stack([core, tile.astype(jnp.int32)])
    lane = jnp.arange(ranked, dtype=jnp.int32)

    def live(ranks):
        tops = ranks.reshape(2, 2, tiles // 4)
        top = jnp.where(lane < ranked // 2, tops[:, 0, :, None], tops[:, 1, :, None])
        level = lane % (ranked // 2) + ranked // 2 * core
        alive = (level < top).astype(F32).reshape(tiles // 2, 1, ranked)
        return jnp.broadcast_to(alive, (tiles // 2, 8, ranked))

    coefficients = ((tiles, half, ranked), BF16)
    state = ((chains, 2 * cells), F32)
    own_state = ((chains, cells), F32)
    column = ((chains, 1), F32)
    values = [pltpu.VMEM((chains, 2 * cells), BF16)]
    left = [pltpu.VMEM((tiles // 4, chains, 2 * ranked), BF16)]
    work = 2 * chains * 2 * cells * tiles * ranked // 2

    row_arrived = swap(row_factors)
    col_own, col_sent, keep, send = col_setup(
        col_factors, place, tile_ranks, position, coefficients
    )
    (out,) = call(add_kernel, [VMEM] * 2, [coefficients], [], 1 << 24, keep, swap(send))
    out, col_sent, row_factors, row_arrived, late = lax.optimization_barrier(
        (
            out, col_sent, row_factors, row_arrived,
            (position, momentum, tile_ranks, log_mean, counts, step_size),
        )
    )
    arrived = spread(out)
    position, momentum, tile_ranks, log_mean, counts, step_size = late
    row_whole = row_setup(row_factors, row_arrived, place)
    rate = counts.astype(F32)
    z_other, m_other = swap(position), swap(momentum)
    base_other, rate_other = swap(log_mean), swap(rate)
    col_other = swap(col_sent)
    col_live = live(lax.dynamic_slice_in_dim(tile_ranks, tile, 1, 1)[:, 0])
    row_live = live(lax.dynamic_slice_in_dim(tile_ranks, tile, 1, 0)[0])
    start_z = jnp.concatenate([position, z_other], axis=1)
    start_m = jnp.concatenate([momentum, m_other], axis=1)
    base = jnp.concatenate([log_mean, base_other])[None, :]
    rate = jnp.concatenate([rate, rate_other])[None, :]
    step = jnp.broadcast_to(step_size[:, None], (chains, ranked))

    def expand(coefficient, factors):
        (total,) = call(
            expand_kernel, [VMEM] * 2, [state], left, 2 * work, coefficient, factors[1]
        )
        return total, swap(total)

    def row_pass(arrived, energy=True):
        return call(
            row_kernel, [VMEM] * 6, [coefficients] + [column] * energy, values, work,
            row_live, *expand(arrived, row), base, rate, row[0],
        )

    arrived, start_z, start_m, base, rate, step, row_live, col_live = (
        lax.optimization_barrier(
            (arrived, start_z, start_m, base, rate, step, row_live, col_live)
        )
    )
    z, m = start_z, start_m
    row = merge(arrived, row_whole)
    out, start_energy = row_pass(arrived)
    out, col_other = lax.optimization_barrier((out, col_other))
    arrived = spread(out)
    col = merge(arrived, col_own, col_other)
    for weight in (0.5, 1.0):
        out, z, m = call(
            functools.partial(col_kernel, weight),
            [VMEM] * 7, [coefficients, state, state], values, work,
            col_live, *expand(arrived, col), step, z, m, col[0],
        )
        last = weight == 1.0
        out, *energy = row_pass(spread(out), last)
        arrived = spread(out)
    (end_energy,) = energy
    m, change = call(
        last_kernel, [VMEM] * 9, [own_state, ((tiles, 1, chains), F32)], [], 1 << 24,
        *expand(arrived, col), step, z, m, start_z, start_m,
        start_energy, end_energy,
    )
    change = spread(change)
    z = z[:, :cells]
    change = change.sum(axis=(0, 1))
    change = change + swap(change)
    return z, m, change


def solution(mesh):
    split = Mesh(
        mesh.devices.reshape(4, 4, 4, 2), ("col_0", "col_1", "row_0", "row_1")
    )
    return jax.shard_map(
        on_device,
        mesh=split,
        in_specs=(
            P(None, COL_ROW),
            P(None, COL_ROW),
            P(COL_ROW, None, None),
            P(COL_ROW, None, None),
            P(),
            P(COL_ROW),
            P(COL_ROW),
            P(),
        ),
        out_specs=(P(None, COL_ROW), P(None, COL_ROW), P()),
        check_vma=False,
    )
```

time: 243 us -> 227 us (0.934)
  blocking collectives: 135 us -> 120 us
  starting transfers between devices: 23.4 us -> 31.3 us
  local copies, waits for them, and re-layouts: 5.86 us -> 1.57 us
    all_to_all x6, blocking collectives: 135 us -> 120 us  [spread(): return lax.all_to_all(value, CHIPS, split_axis=0, concat_axis=0, tiled=True)]
    pallas_call x12 -> x13, Pallas kernels: 31.3 us -> 23 us  [call(): pl.pallas_call(kernel, in_specs=specs, out_specs=[VMEM] * len(outs), out_...]
    all_to_all x1, starting transfers between devices: 4.55 us -> 11.3 us  [spread(): return lax.all_to_all(value, CHIPS, split_axis=0, concat_axis=0, tiled=True)]
    pallas_call x4, Pallas kernels: 24.5 us -> 31.2 us  [the longest x1 10.9 us: row_setup(): pl.pallas_call(row_setup_kernel, in_specs=[SMEM, ANY, ANY], out_specs=ANY...]
    unnamed x20 -> x12, local copies, waits for them, and re-layouts: 3.68 us -> 0.02 us
    all_to_all x1, waiting for transfers between devices: 7.66 us -> 4.2 us  [spread(): return lax.all_to_all(value, CHIPS, split_axis=0, concat_axis=0, tiled=True)]
  transfers between devices with their start and end apart: 15 -> 15, of which waited for: 10 -> 9; matrix products, arithmetic and copies ran while one was open for 0% -> 1% of each run, Pallas kernels for 4% -> 14%
where the time goes in v3:
time: 227 us; the launch traced here: 226 us
  blocking collectives  120 us (53%)
  Pallas kernels  54.2 us (24%)
  starting transfers between devices  31.3 us (14%)
  waiting for transfers between devices  17.9 us (8%)
    all_to_all x6, blocking collectives, spread(): return lax.all_to_all(value, CHIPS, split_axis=0, concat_axis=0, tiled=True)  120 us
    pallas_call x13, Pallas kernels, call(): pl.pallas_call(kernel, in_specs=specs, out_specs=[VMEM] * len(outs), out_...  23 us
    ppermute x14, starting transfers between devices, swap(): return lax.ppermute(value, CORE, [(0, 1), (1, 0)])  20 us
    ppermute x14, waiting for transfers between devices, swap(): return lax.ppermute(value, CORE, [(0, 1), (1, 0)])  13.7 us
    all_to_all x1, starting transfers between devices, spread(): return lax.all_to_all(value, CHIPS, split_axis=0, concat_axis=0, tiled=True)  11.3 us
    pallas_call x1, Pallas kernels, row_setup(): pl.pallas_call(row_setup_kernel, in_specs=[SMEM, ANY, ANY], out_specs=ANY...  10.9 us
    pallas_call x2, Pallas kernels, merge(): pl.pallas_call(merge_kernel, in_specs=[ANY] * (1 + len(parts)), out_specs...  10.3 us
    pallas_call x1, Pallas kernels, col_setup(): pl.pallas_call(col_setup_kernel, in_specs=[SMEM, ANY, ANY, ANY], out_spec...  9.95 us
  transfers between devices with their start and end apart: 15, of which 9 were waited for; matrix products, arithmetic and copies ran while one was open for 1% of the time, Pallas kernels for 14%

profile of v3, /device:TPU:1, one launch (start us, length us, event | category | flops | bytes accessed | tf_op | source)
XLA Modules:
  0.0 226.4 jit_solution(10790711345950283386)
XLA Ops:
  0.6 1.5 collective-permute-start.1
  2.2 10.0 %shard_map.103 = (bf16[16,512,256]{2,1,0:T(8,128)(2,1)}, bf16[16,512,256]{2,1,0:T(8,128)(2,1)}, bf16[64,64,128]{2,1,0:T(8,128)(2,1)S(1)}, bf16[64,64,128]{2,1,0:T(8,128)(2,1)S(1)}) custom-call(s32[2]{0:T(128)S(1)} %pad_add_fusion.place_ref, bf16[32768,128]{1,0:T(8,128)(2,1)} %bitcast.13, s32[64,64]{1,0:T(8,128)} %ranks_ref.1, f32[128,512]{1,0:T(8,128)} %z_ref.1), custom_call_target="tpu_custom_call" | custom-call | flops 8000000000 | bytes 16777216 | tf_op jit(solution)/shard_map/pallas_call | solution.py:163
  12.1 0.1 collective-permute-start
  12.3 4.3 %collective-permute-done.arrived_ref = bf16[64,64,128]{2,1,0:T(8,128)(2,1)S(1)} collective-permute-done((bf16[64,64,128]{2,1,0:T(8,128)(2,1)S(1)}, bf16[64,64,128]{2,1,0:T(8,128)(2,1)S(1)}, u32[]{:S(2)}, u32[]{:S(2)}) %collective-permute-start) | collective-permute-done | bytes 1048608 | tf_op jit(solution)/shard_map/ppermute | solution.py:25
  16.6 1.3 shard_map.104
  17.9 0.4 collective-permute-start.7
  18.3 11.3 %all-to-all-start = ((bf16[64,64,128]{2,1,0:T(8,128)(2,1)}), bf16[64,64,128]{2,1,0:T(8,128)(2,1)S(1)}, u32[]{:S(2)}, u32[]{:S(2)}) async-start(bf16[64,64,128]{2,1,0:T(8,128)(2,1)} %shard_map.104), calls=%async_computation | async-start | bytes 2097152 | tf_op jit(solution)/shard_map/all_to_all | solution.py:29
  29.5 0.5 collective-permute-start.5
  30.0 0.1 collective-permute-start.4
  30.1 0.4 collective-permute-start.2
  30.7 10.9 %shard_map.105.refs_0_ = bf16[2,16,512,256]{3,2,1,0:T(8,128)(2,1)} custom-call(s32[2]{0:T(128)S(1)} %pad_add_fusion.place_ref, bf16[32768,128]{1,0:T(8,128)(2,1)} %bitcast.14, bf16[32768,128]{1,0:T(8,128)(2,1)} %bitcast.6.other_raw_ref), custom_call_target="tpu_custom_call" | custom-call | flops 8000000000 | bytes 16777216 | tf_op jit(solution)/shard_map/pallas_call | solution.py:252
  41.7 0.2 dynamic-slice_reduce_fusion
  42.6 4.2 %all-to-all-done.after_ref.coefficient_ref = bf16[64,64,128]{2,1,0:T(8,128)(2,1)S(1)} async-done(((bf16[64,64,128]{2,1,0:T(8,128)(2,1)}), bf16[64,64,128]{2,1,0:T(8,128)(2,1)S(1)}, u32[]{:S(2)}, u32[]{:S(2)}) %all-to-all-start) | async-done | bytes 1048608 | tf_op jit(solution)/shard_map/all_to_all | solution.py:29
  46.9 5.2 %shard_map.106 = (bf16[2,16,512,256]{3,2,1,0:T(8,128)(2,1)S(1)}, bf16[2,16,256,512]{3,2,1,0:T(8,128)(2,1)S(1)}) custom-call(bf16[64,64,128]{2,1,0:T(8,128)(2,1)S(1)} %all-to-all-done.after_ref.coefficient_ref, bf16[2,16,512,256]{3,2,1,0:T(8,128)(2,1)} %shard_map.105.refs_0_), custom_call_target="tpu_custom_call" | custom-call | flops 4000000000 | bytes 16777216 | tf_op jit(solution)/shard_map/pallas_call | solution.py:313
  52.1 2.0 shard_map.107.total_ref
  54.1 2.3 %collective-permute-start.6 = (f32[128,1024]{1,0:T(8,128)S(1)}, f32[128,1024]{1,0:T(8,128)S(1)}, u32[]{:S(2)}, u32[]{:S(2)}) collective-permute-start(f32[128,1024]{1,0:T(8,128)S(1)} %shard_map.107.total_ref), channel_id=1, source_target_pairs={{0,1},{1,0},{2,3},{3,2},{4,5},{5,4},{6,7},{7,6},{8,9},{9,8},{10,11... | collective-permute-start | bytes 1572872 | tf_op jit(solution)/shard_map/ppermute | solution.py:25
  56.4 1.5 collective-permute-done.6.arrived_ref
  57.9 1.8 shard_map.108
  59.8 21.3 %all_to_all.35.after_ref.coefficient_ref = bf16[64,64,128]{2,1,0:T(8,128)(2,1)S(1)} all-to-all(bf16[64,64,128]{2,1,0:T(8,128)(2,1)S(1)} %get-tuple-element.64), channel_id=1, replica_groups=mesh['col_0'=4,'col_1'=4,'row_0'=4,'row_1'=2] {'col_0','col_1','row_0'}, dimensions={0} | all-to-all | bytes 2097152 | tf_op jit(solution)/shard_map/all_to_all | solution.py:29
  81.1 5.2 %shard_map.109 = (bf16[2,16,512,256]{3,2,1,0:T(8,128)(2,1)S(1)}, bf16[2,16,256,512]{3,2,1,0:T(8,128)(2,1)S(1)}) custom-call(bf16[64,64,128]{2,1,0:T(8,128)(2,1)S(1)} %all_to_all.35.after_ref.coefficient_ref, bf16[16,512,256]{2,1,0:T(8,128)(2,1)} %get-tuple-element.65.refs_0_, bf16[16,512,256]{2,1,0:T(8,128)(2,1)} %collective-permute-done.7.refs_1_), custom_call_target="tpu_custom_call" | custom-call | flops 4000000000 | bytes 16777216 | tf_op jit(solution)/shard_map/pallas_call | solution.py:313
  86.3 2.0 shard_map.110.total_ref
  88.3 2.7 %collective-permute-start.8 = (f32[128,1024]{1,0:T(8,128)S(1)}, f32[128,1024]{1,0:T(8,128)S(1)}, u32[]{:S(2)}, u32[]{:S(2)}) collective-permute-start(f32[128,1024]{1,0:T(8,128)S(1)} %shard_map.110.total_ref), channel_id=1, source_target_pairs={{0,1},{1,0},{2,3},{3,2},{4,5},{5,4},{6,7},{7,6},{8,9},{9,8},{10,11... | collective-permute-start | bytes 1572872 | tf_op jit(solution)/shard_map/ppermute | solution.py:25
  91.0 1.5 collective-permute-done.8.arrived_ref
  92.5 1.8 shard_map.111
  94.3 21.4 %all_to_all.36.coefficient_ref = bf16[64,64,128]{2,1,0:T(8,128)(2,1)S(1)} all-to-all(bf16[64,64,128]{2,1,0:T(8,128)(2,1)S(1)} %get-tuple-element.72), channel_id=1, replica_groups=mesh['col_0'=4,'col_1'=4,'row_0'=4,'row_1'=2] {'col_0','col_1','row_0'}, dimensions={0} | all-to-all | bytes 2097152 | tf_op jit(solution)/shard_map/all_to_all | solution.py:29
  115.7 2.0 shard_map.112.total_ref
  117.7 2.5 %collective-permute-start.9 = (f32[128,1024]{1,0:T(8,128)S(1)}, f32[128,1024]{1,0:T(8,128)S(1)}, u32[]{:S(2)}, u32[]{:S(2)}) collective-permute-start(f32[128,1024]{1,0:T(8,128)S(1)} %shard_map.112.total_ref), channel_id=1, source_target_pairs={{0,1},{1,0},{2,3},{3,2},{4,5},{5,4},{6,7},{7,6},{8,9},{9,8},{10,11... | collective-permute-start | bytes 1572872 | tf_op jit(solution)/shard_map/ppermute | solution.py:25
  120.2 1.5 collective-permute-done.9.arrived_ref
  121.8 1.7 shard_map.113
  123.5 21.4 %all_to_all.37.coefficient_ref = bf16[64,64,128]{2,1,0:T(8,128)(2,1)S(1)} all-to-all(bf16[64,64,128]{2,1,0:T(8,128)(2,1)S(1)} %shard_map.113), channel_id=1, replica_groups=mesh['col_0'=4,'col_1'=4,'row_0'=4,'row_1'=2] {'col_0','col_1','row_0'}, dimensions={0} | all-to-all | bytes 2097152 | tf_op jit(solution)/shard_map/all_to_all | solution.py:29
  144.9 2.0 shard_map.114.total_ref
  146.9 2.5 %collective-permute-start.10 = (f32[128,1024]{1,0:T(8,128)S(1)}, f32[128,1024]{1,0:T(8,128)S(1)}, u32[]{:S(2)}, u32[]{:S(2)}) collective-permute-start(f32[128,1024]{1,0:T(8,128)S(1)} %shard_map.114.total_ref), channel_id=1, source_target_pairs={{0,1},{1,0},{2,3},{3,2},{4,5},{5,4},{6,7},{7,6},{8,9},{9,8},{10,11... | collective-permute-start | bytes 1572872 | tf_op jit(solution)/shard_map/ppermute | solution.py:25
  149.4 1.5 collective-permute-done.10.arrived_ref
  150.9 1.8 shard_map.115
  152.7 21.4 %all_to_all.38.coefficient_ref = bf16[64,64,128]{2,1,0:T(8,128)(2,1)S(1)} all-to-all(bf16[64,64,128]{2,1,0:T(8,128)(2,1)S(1)} %get-tuple-element.76), channel_id=1, replica_groups=mesh['col_0'=4,'col_1'=4,'row_0'=4,'row_1'=2] {'col_0','col_1','row_0'}, dimensions={0} | all-to-all | bytes 2097152 | tf_op jit(solution)/shard_map/all_to_all | solution.py:29
  174.1 2.0 shard_map.116.total_ref
  176.1 2.5 %collective-permute-start.11 = (f32[128,1024]{1,0:T(8,128)S(1)}, f32[128,1024]{1,0:T(8,128)S(1)}, u32[]{:S(2)}, u32[]{:S(2)}) collective-permute-start(f32[128,1024]{1,0:T(8,128)S(1)} %shard_map.116.total_ref), channel_id=1, source_target_pairs={{0,1},{1,0},{2,3},{3,2},{4,5},{5,4},{6,7},{7,6},{8,9},{9,8},{10,11... | collective-permute-start | bytes 1572872 | tf_op jit(solution)/shard_map/ppermute | solution.py:25
  178.6 1.5 collective-permute-done.11.arrived_ref
  180.2 1.8 shard_map.117
  182.0 21.4 %all_to_all.39.coefficient_ref = bf16[64,64,128]{2,1,0:T(8,128)(2,1)S(1)} all-to-all(bf16[64,64,128]{2,1,0:T(8,128)(2,1)S(1)} %get-tuple-element.77), channel_id=1, replica_groups=mesh['col_0'=4,'col_1'=4,'row_0'=4,'row_1'=2] {'col_0','col_1','row_0'}, dimensions={0} | all-to-all | bytes 2097152 | tf_op jit(solution)/shard_map/all_to_all | solution.py:29
  203.4 2.0 shard_map.118.total_ref
  205.4 2.5 %collective-permute-start.12 = (f32[128,1024]{1,0:T(8,128)S(1)}, f32[128,1024]{1,0:T(8,128)S(1)}, u32[]{:S(2)}, u32[]{:S(2)}) collective-permute-start(f32[128,1024]{1,0:T(8,128)S(1)} %shard_map.118.total_ref), channel_id=1, source_target_pairs={{0,1},{1,0},{2,3},{3,2},{4,5},{5,4},{6,7},{7,6},{8,9},{9,8},{10,11... | collective-permute-start | bytes 1572872 | tf_op jit(solution)/shard_map/ppermute | solution.py:25
  207.9 1.5 collective-permute-done.12.arrived_ref
  209.5 0.9 shard_map.119
  210.4 12.8 %all_to_all.40 = f32[64,1,128]{2,1,0:T(1,128)S(1)} all-to-all(f32[64,1,128]{2,1,0:T(1,128)S(1)} %get-tuple-element.82), channel_id=1, replica_groups=mesh['col_0'=4,'col_1'=4,'row_0'=4,'row_1'=2] {'col_0','col_1','row_0'}, dimensions={0} | all-to-all | bytes 65536 | tf_op jit(solution)/shard_map/all_to_all | solution.py:29
  223.2 1.9 collective-permute-start.13
  225.1 0.7 slice.19
  225.9 0.5 add.43
  (41 shorter events, 1.2 us)
Async XLA Ops:
  0.6 17.2 %collective-permute-start.1 = (bf16[512,64,128]{2,1,0:T(8,128)(2,1)}, bf16[512,64,128]{2,1,0:T(8,128)(2,1)}, u32[]{:S(2)}, u32[]{:S(2)}) collective-permute-start(bf16[512,64,128]{2,1,0:T(8,128)(2,1)} %param.10), channel_id=1, source_target_pairs={{0,1},{1,0},{2,3},{3,2},{4,5},{5,4},{6,7},{7,6},{8,9},{9,8},{10,11... | collective-permute-start | bytes 25165832 | tf_op jit(solution)/shard_map/ppermute | solution.py:25
  2.2 16.1 %copy-start.3 = (s32[512]{0:T(512)S(1)}, s32[512]{0:T(512)}, u32[]{:S(2)}) copy-start(s32[512]{0:T(512)} %param.14) | copy-start | bytes 6148
  2.2 27.9 %copy-start.4 = (f32[512]{0:T(512)S(1)}, f32[512]{0:T(512)}, u32[]{:S(2)}) copy-start(f32[512]{0:T(512)} %param.13) | copy-start | bytes 6148
  2.2 28.0 %copy-start = (f32[128,512]{1,0:T(8,128)S(1)}, f32[128,512]{1,0:T(8,128)}, u32[]{:S(2)}) copy-start(f32[128,512]{1,0:T(8,128)} %z_ref.1) | copy-start | bytes 786436
  2.2 28.4 %copy-start.1 = (f32[128,512]{1,0:T(8,128)S(1)}, f32[128,512]{1,0:T(8,128)}, u32[]{:S(2)}) copy-start(f32[128,512]{1,0:T(8,128)} %param.9) | copy-start | bytes 786436
  12.1 4.4 %collective-permute-start = (bf16[64,64,128]{2,1,0:T(8,128)(2,1)S(1)}, bf16[64,64,128]{2,1,0:T(8,128)(2,1)S(1)}, u32[]{:S(2)}, u32[]{:S(2)}) collective-permute-start(bf16[64,64,128]{2,1,0:T(8,128)(2,1)S(1)} %get-tuple-element.44), channel_id=1, source_target_pairs={{0,1},{1,0},{2,3},{3,2},{4,5},{5,4},{6,7},{7,6},{8,9},{9,8},{10,11... | collective-permute-start | bytes 3145736 | tf_op jit(solution)/shard_map/ppermute | solution.py:25
  17.9 41.9 %collective-permute-start.7 = (bf16[16,512,256]{2,1,0:T(8,128)(2,1)}, bf16[16,512,256]{2,1,0:T(8,128)(2,1)}, u32[]{:S(2)}, u32[]{:S(2)}) collective-permute-start(bf16[16,512,256]{2,1,0:T(8,128)(2,1)} %get-tuple-element.63), channel_id=1, source_target_pairs={{0,1},{1,0},{2,3},{3,2},{4,5},{5,4},{6,7},{7,6},{8,9},{9,8},{10,11... | collective-permute-start | bytes 12582920 | tf_op jit(solution)/shard_map/ppermute | solution.py:25
  18.3 28.5 %all-to-all-start = ((bf16[64,64,128]{2,1,0:T(8,128)(2,1)}), bf16[64,64,128]{2,1,0:T(8,128)(2,1)S(1)}, u32[]{:S(2)}, u32[]{:S(2)}) async-start(bf16[64,64,128]{2,1,0:T(8,128)(2,1)} %shard_map.104), calls=%async_computation | async-start | bytes 2097152 | tf_op jit(solution)/shard_map/all_to_all | solution.py:29
  29.5 12.9 %collective-permute-start.5 = (f32[512]{0:T(512)S(1)}, f32[512]{0:T(512)S(1)}, u32[]{:S(2)}, u32[]{:S(2)}) collective-permute-start(f32[512]{0:T(512)S(1)} %convert_element_type.17), channel_id=1, source_target_pairs={{0,1},{1,0},{2,3},{3,2},{4,5},{5,4},{6,7},{7,6},{8,9},{9,8},{10,11... | collective-permute-start | bytes 6152 | tf_op jit(solution)/shard_map/ppermute | solution.py:25
  30.0 12.4 %collective-permute-start.4 = (f32[512]{0:T(512)S(1)}, f32[512]{0:T(512)S(1)}, u32[]{:S(2)}, u32[]{:S(2)}) collective-permute-start(f32[512]{0:T(512)S(1)} %copy-done.4), channel_id=1, source_target_pairs={{0,1},{1,0},{2,3},{3,2},{4,5},{5,4},{6,7},{7,6},{8,9},{9,8},{10,11... | collective-permute-start | bytes 6152 | tf_op jit(solution)/shard_map/ppermute | solution.py:25
  30.1 12.4 %collective-permute-start.2 = (f32[128,512]{1,0:T(8,128)S(1)}, f32[128,512]{1,0:T(8,128)S(1)}, u32[]{:S(2)}, u32[]{:S(2)}) collective-permute-start(f32[128,512]{1,0:T(8,128)S(1)} %copy-done), channel_id=1, source_target_pairs={{0,1},{1,0},{2,3},{3,2},{4,5},{5,4},{6,7},{7,6},{8,9},{9,8},{10,11... | collective-permute-start | bytes 786440 | tf_op jit(solution)/shard_map/ppermute | solution.py:25
  30.6 12.0 %collective-permute-start.3 = (f32[128,512]{1,0:T(8,128)S(1)}, f32[128,512]{1,0:T(8,128)S(1)}, u32[]{:S(2)}, u32[]{:S(2)}) collective-permute-start(f32[128,512]{1,0:T(8,128)S(1)} %copy-done.1), channel_id=1, source_target_pairs={{0,1},{1,0},{2,3},{3,2},{4,5},{5,4},{6,7},{7,6},{8,9},{9,8},{10,11... | collective-permute-start | bytes 786440 | tf_op jit(solution)/shard_map/ppermute | solution.py:25
  30.7 11.0 %copy-start.2 = (s32[64,64]{1,0:T(8,128)S(1)}, s32[64,64]{1,0:T(8,128)}, u32[]{:S(2)}) copy-start(s32[64,64]{1,0:T(8,128)} %ranks_ref.1) | copy-start | bytes 49156
  30.7 16.2 %copy-start.5 = (f32[128]{0:T(128)S(1)}, f32[128]{0:T(128)}, u32[]{:S(2)}) copy-start(f32[128]{0:T(128)} %param.15) | copy-start | bytes 1540
  54.1 3.8 %collective-permute-start.6 = (f32[128,1024]{1,0:T(8,128)S(1)}, f32[128,1024]{1,0:T(8,128)S(1)}, u32[]{:S(2)}, u32[]{:S(2)}) collective-permute-start(f32[128,1024]{1,0:T(8,128)S(1)} %shard_map.107.total_ref), channel_id=1, source_target_pairs={{0,1},{1,0},{2,3},{3,2},{4,5},{5,4},{6,7},{7,6},{8,9},{9,8},{10,11... | collective-permute-start | bytes 1572872 | tf_op jit(solution)/shard_map/ppermute | solution.py:25
  88.3 4.2 %collective-permute-start.8 = (f32[128,1024]{1,0:T(8,128)S(1)}, f32[128,1024]{1,0:T(8,128)S(1)}, u32[]{:S(2)}, u32[]{:S(2)}) collective-permute-start(f32[128,1024]{1,0:T(8,128)S(1)} %shard_map.110.total_ref), channel_id=1, source_target_pairs={{0,1},{1,0},{2,3},{3,2},{4,5},{5,4},{6,7},{7,6},{8,9},{9,8},{10,11... | collective-permute-start | bytes 1572872 | tf_op jit(solution)/shard_map/ppermute | solution.py:25
  117.7 4.1 %collective-permute-start.9 = (f32[128,1024]{1,0:T(8,128)S(1)}, f32[128,1024]{1,0:T(8,128)S(1)}, u32[]{:S(2)}, u32[]{:S(2)}) collective-permute-start(f32[128,1024]{1,0:T(8,128)S(1)} %shard_map.112.total_ref), channel_id=1, source_target_pairs={{0,1},{1,0},{2,3},{3,2},{4,5},{5,4},{6,7},{7,6},{8,9},{9,8},{10,11... | collective-permute-start | bytes 1572872 | tf_op jit(solution)/shard_map/ppermute | solution.py:25
  146.9 4.1 %collective-permute-start.10 = (f32[128,1024]{1,0:T(8,128)S(1)}, f32[128,1024]{1,0:T(8,128)S(1)}, u32[]{:S(2)}, u32[]{:S(2)}) collective-permute-start(f32[128,1024]{1,0:T(8,128)S(1)} %shard_map.114.total_ref), channel_id=1, source_target_pairs={{0,1},{1,0},{2,3},{3,2},{4,5},{5,4},{6,7},{7,6},{8,9},{9,8},{10,11... | collective-permute-start | bytes 1572872 | tf_op jit(solution)/shard_map/ppermute | solution.py:25
  176.1 4.1 %collective-permute-start.11 = (f32[128,1024]{1,0:T(8,128)S(1)}, f32[128,1024]{1,0:T(8,128)S(1)}, u32[]{:S(2)}, u32[]{:S(2)}) collective-permute-start(f32[128,1024]{1,0:T(8,128)S(1)} %shard_map.116.total_ref), channel_id=1, source_target_pairs={{0,1},{1,0},{2,3},{3,2},{4,5},{5,4},{6,7},{7,6},{8,9},{9,8},{10,11... | collective-permute-start | bytes 1572872 | tf_op jit(solution)/shard_map/ppermute | solution.py:25
  205.4 4.1 %collective-permute-start.12 = (f32[128,1024]{1,0:T(8,128)S(1)}, f32[128,1024]{1,0:T(8,128)S(1)}, u32[]{:S(2)}, u32[]{:S(2)}) collective-permute-start(f32[128,1024]{1,0:T(8,128)S(1)} %shard_map.118.total_ref), channel_id=1, source_target_pairs={{0,1},{1,0},{2,3},{3,2},{4,5},{5,4},{6,7},{7,6},{8,9},{9,8},{10,11... | collective-permute-start | bytes 1572872 | tf_op jit(solution)/shard_map/ppermute | solution.py:25
  223.2 2.7 %collective-permute-start.13 = (f32[128]{0:T(128)S(1)}, f32[128]{0:T(128)S(1)}, u32[]{:S(2)}, u32[]{:S(2)}) collective-permute-start(f32[128]{0:T(128)S(1)} %reduce_sum.9), channel_id=1, source_target_pairs={{0,1},{1,0},{2,3},{3,2},{4,5},{5,4},{6,7},{7,6},{8,9},{9,8},{10,11... | collective-permute-start | bytes 1544 | tf_op jit(solution)/shard_map/ppermute | solution.py:25

commit v4 on v3

--- a/solution.py
+++ b/solution.py
@@ -15,7 +15,6 @@
 F32 = jnp.float32
 LIMIT = 8 << 20
 UNROLL = 8
-NT = (((1,), (1,)), ((), ()))
 VMEM = pl.BlockSpec(memory_space=pltpu.VMEM)
 SMEM = pl.BlockSpec(memory_space=pltpu.SMEM)
 ANY = pl.BlockSpec(memory_space=pl.ANY)
@@ -273,7 +272,6 @@
         sources = sources[0].at[0], sources[0].at[1]
     quads, cells = out_ref.shape[1], out_ref.shape[2]
     size = quads // sems.shape[1]
-    same = one_hot(lambda to: to)
 
     def copies(group):
         quad = pl.ds(group * size, size)
@@ -299,10 +297,9 @@
             for side in range(2):
                 for block in range(cells // 256):
                     at_cell = slice(256 * block, 256 * block + 256)
-                    turned_ref[side, quad, :, at_cell] = lax.dot_general(
-                        same, out_ref[side, quad, at_cell, :], NT,
-                        preferred_element_type=F32,
-                    ).astype(BF16)
+                    turned_ref[side, quad, :, at_cell] = jnp.transpose(
+                        out_ref[side, quad, at_cell, :]
+                    )
         return carry
 
     lax.fori_loop(0, sems.shape[1], turn, 0)
@@ -330,8 +327,19 @@
     out_ref[...] = (keep_ref[...].astype(F32) + arrived_ref[...].astype(F32)).astype(BF16)
 
 
-def expand_kernel(coefficient_ref, turned_ref, total_ref, left):
+def expand_side(side, left_ref, turned_ref, total_ref):
     quads, cells = turned_ref.shape[1], turned_ref.shape[3]
+    for block in range(cells // 256):
+        at_cell = slice(256 * block, 256 * block + 256)
+        total_ref[:, at_cell] = sum(
+            jnp.dot(
+                left_ref[q], turned_ref[side, q, :, at_cell], preferred_element_type=F32
+            )
+            for q in range(quads)
+        )
+
+
+def expand_first_kernel(side, coefficient_ref, turned_ref, total_ref, left_ref):
     half = coefficient_ref.shape[1]
 
     def arrange(q, carry):
@@ -340,25 +348,12 @@
             two = coefficient_ref[q + 32 * pair + 16]
             low = low_lanes(one)
             lanes = slice(pair * 128, pair * 128 + 128)
-            left[q, :half, lanes] = jnp.where(low, one, other_half(two))
-            left[q, half:, lanes] = jnp.where(low, other_half(one), two)
-        return carry
-
-    lax.fori_loop(0, quads, arrange, 0, unroll=4)
-
-    def side_of(side, carry):
-        for block in range(cells // 256):
-            at_cell = slice(256 * block, 256 * block + 256)
-            at = pl.ds(pl.multiple_of(side * cells + 256 * block, 256), 256)
-            total_ref[:, at] = sum(
-                jnp.dot(
-                    left[q], turned_ref[side, q, :, at_cell], preferred_element_type=F32
-                )
-                for q in range(quads)
-            )
-        return carry
-
-    lax.fori_loop(0, 2, side_of, 0)
+            left_ref[q, :half, lanes] = jnp.where(low, one, other_half(two))
+            left_ref[q, half:, lanes] = jnp.where(low, other_half(one), two)
+        return carry
+
+    lax.fori_loop(0, left_ref.shape[0], arrange, 0, unroll=4)
+    expand_side(side, left_ref, turned_ref, total_ref)
 
 
 def project(factor, quads, live, out_ref):
@@ -379,74 +374,92 @@
     lax.fori_loop(0, quads, quad, 0, unroll=UNROLL)
 
 
-def project_both(values, f_ref, live_ref, out_ref):
-    cells = f_ref.shape[2]
-
+def row_values(total_ref, arrived_ref, base_ref, rate_ref, values):
+    rate = rate_ref[...]
+    exponent = base_ref[...] + (total_ref[...] + arrived_ref[...])
+    intensity = jnp.exp(exponent)
+    values[...] = (rate - intensity).astype(BF16)
+    return intensity - rate * exponent
+
+
+def col_values(
+    weight, total_ref, arrived_ref, step_ref, z_ref, m_ref, new_z_ref, new_m_ref, values
+):
+    step = step_ref[:, :1]
+    z = z_ref[...]
+    moment = m_ref[...] - weight * step * (z - (total_ref[...] + arrived_ref[...]))
+    z = z + step * moment
+    new_m_ref[...] = moment
+    new_z_ref[...] = z
+    values[...] = z.astype(BF16)
+
+
+def project_first(values, f_ref, part_ref):
+    def quad(q, carry):
+        part_ref[q] = jnp.dot(values[...], f_ref[1, q], preferred_element_type=F32)
+        return carry
+
+    lax.fori_loop(0, part_ref.shape[0], quad, 0, unroll=UNROLL)
+
+
+def project_second(values, f_ref, part_ref, live_ref, out_ref):
     def factor(q):
-        return jnp.dot(
-            values[:, :cells], f_ref[0, q], preferred_element_type=F32
-        ) + jnp.dot(values[:, cells:], f_ref[1, q], preferred_element_type=F32)
+        return part_ref[q] + jnp.dot(
+            values[...], f_ref[0, q], preferred_element_type=F32
+        )
 
     def live(pair, q):
         return live_ref[pair * 16 + q, :1]
 
-    project(factor, f_ref.shape[1], live, out_ref)
-
-
-def complete(total_ref, arrived_ref):
-    cells = total_ref.shape[1] // 2
-    return [
-        total_ref[:, :cells] + arrived_ref[:, cells:],
-        total_ref[:, cells:] + arrived_ref[:, :cells],
-    ]
-
-
-def row_kernel(
-    live_ref, total_ref, arrived_ref, base_ref, rate_ref, f_ref,
-    out_ref, *refs,
+    project(factor, part_ref.shape[0], live, out_ref)
+
+
+def row_first_kernel(total_ref, arrived_ref, base_ref, rate_ref, f_ref, part_ref, values):
+    row_values(total_ref, arrived_ref, base_ref, rate_ref, values)
+    project_first(values, f_ref, part_ref)
+
+
+def row_second_kernel(
+    live_ref, total_ref, arrived_ref, base_ref, rate_ref, f_ref, part_ref, out_ref, *refs
 ):
     *energy_ref, values = refs
-    cells = total_ref.shape[1] // 2
-    for side, field in enumerate(complete(total_ref, arrived_ref)):
-        at = slice(side * cells, (side + 1) * cells)
-        rate = rate_ref[:, at]
-        exponent = base_ref[:, at] + field
-        intensity = jnp.exp(exponent)
-        values[:, at] = (rate - intensity).astype(BF16)
-        if side == 0 and energy_ref:
-            energy_ref[0][...] = jnp.sum(intensity - rate * exponent, axis=1, keepdims=True)
-    project_both(values, f_ref, live_ref, out_ref)
-
-
-def col_kernel(
-    weight, live_ref, total_ref, arrived_ref, step_ref, z_ref, m_ref,
-    f_ref, out_ref, new_z_ref, new_m_ref, values,
+    energy = row_values(total_ref, arrived_ref, base_ref, rate_ref, values)
+    if energy_ref:
+        energy_ref[0][...] = jnp.sum(energy, axis=1, keepdims=True)
+    project_second(values, f_ref, part_ref, live_ref, out_ref)
+
+
+def col_first_kernel(
+    weight, total_ref, arrived_ref, step_ref, z_ref, m_ref, f_ref,
+    part_ref, new_z_ref, new_m_ref, values,
 ):
-    cells = total_ref.shape[1] // 2
-    step = step_ref[:, :1]
-    for side, pulled in enumerate(complete(total_ref, arrived_ref)):
-        at = slice(side * cells, (side + 1) * cells)
-        z = z_ref[:, at]
-        moment = m_ref[:, at] - weight * step * (z - pulled)
-        z = z + step * moment
-        new_m_ref[:, at] = moment
-        new_z_ref[:, at] = z
-        values[:, at] = z.astype(BF16)
-    project_both(values, f_ref, live_ref, out_ref)
+    col_values(
+        weight, total_ref, arrived_ref, step_ref, z_ref, m_ref, new_z_ref, new_m_ref, values
+    )
+    project_first(values, f_ref, part_ref)
+
+
+def col_second_kernel(
+    weight, live_ref, total_ref, arrived_ref, step_ref, z_ref, m_ref, f_ref, part_ref,
+    out_ref, new_z_ref, new_m_ref, values,
+):
+    col_values(
+        weight, total_ref, arrived_ref, step_ref, z_ref, m_ref, new_z_ref, new_m_ref, values
+    )
+    project_second(values, f_ref, part_ref, live_ref, out_ref)
 
 
 def last_kernel(
     total_ref, arrived_ref, step_ref, z_ref, m_ref, start_z_ref, start_m_ref,
     start_energy_ref, end_energy_ref, new_m_ref, change_ref,
 ):
-    cells = total_ref.shape[1] // 2
-    z = z_ref[:, :cells]
-    moment = m_ref[:, :cells] - 0.5 * step_ref[:, :1] * (
-        z - complete(total_ref, arrived_ref)[0]
+    z = z_ref[...]
+    moment = m_ref[...] - 0.5 * step_ref[:, :1] * (
+        z - (total_ref[...] + arrived_ref[...])
     )
     new_m_ref[...] = moment
-    start_z = start_z_ref[:, :cells]
-    start_m = start_m_ref[:, :cells]
+    start_z = start_z_ref[...]
+    start_m = start_m_ref[...]
     pieces = 0.5 * (z * z - start_z * start_z + moment * moment - start_m * start_m)
     change = (
         jnp.sum(pieces, axis=1, keepdims=True) + end_energy_ref[...] - start_energy_ref[...]
@@ -488,21 +501,22 @@
         return jnp.broadcast_to(alive, (tiles // 2, 8, ranked))
 
     coefficients = ((tiles, half, ranked), BF16)
-    state = ((chains, 2 * cells), F32)
-    own_state = ((chains, cells), F32)
+    state = ((chains, cells), F32)
+    part = ((tiles // 4, chains, 2 * ranked), F32)
+    left = ((tiles // 4, chains, 2 * ranked), BF16)
     column = ((chains, 1), F32)
-    values = [pltpu.VMEM((chains, 2 * cells), BF16)]
-    left = [pltpu.VMEM((tiles // 4, chains, 2 * ranked), BF16)]
-    work = 2 * chains * 2 * cells * tiles * ranked // 2
+    values = [pltpu.VMEM((chains, cells), BF16)]
+    work = 2 * chains * cells * tiles * ranked // 2
 
     row_arrived = swap(row_factors)
     col_own, col_sent, keep, send = col_setup(
         col_factors, place, tile_ranks, position, coefficients
     )
-    (out,) = call(add_kernel, [VMEM] * 2, [coefficients], [], 1 << 24, keep, swap(send))
-    out, col_sent, row_factors, row_arrived, late = lax.optimization_barrier(
+    sent = swap(send)
+    (out,) = call(add_kernel, [VMEM] * 2, [coefficients], [], 1 << 24, keep, sent)
+    out, col_sent, row_factors, late = lax.optimization_barrier(
         (
-            out, col_sent, row_factors, row_arrived,
+            out, col_sent, row_factors,
             (position, momentum, tile_ranks, log_mean, counts, step_size),
         )
     )
@@ -515,55 +529,75 @@
     col_other = swap(col_sent)
     col_live = live(lax.dynamic_slice_in_dim(tile_ranks, tile, 1, 1)[:, 0])
     row_live = live(lax.dynamic_slice_in_dim(tile_ranks, tile, 1, 0)[0])
-    start_z = jnp.concatenate([position, z_other], axis=1)
-    start_m = jnp.concatenate([momentum, m_other], axis=1)
-    base = jnp.concatenate([log_mean, base_other])[None, :]
-    rate = jnp.concatenate([rate, rate_other])[None, :]
+    base = log_mean[None, :], base_other[None, :]
+    rate = rate[None, :], rate_other[None, :]
     step = jnp.broadcast_to(step_size[:, None], (chains, ranked))
 
-    def expand(coefficient, factors):
-        (total,) = call(
-            expand_kernel, [VMEM] * 2, [state], left, 2 * work, coefficient, factors[1]
-        )
-        return total, swap(total)
+    def expand(coefficient, factors, first):
+        one, rows = call(
+            functools.partial(expand_first_kernel, first), [VMEM] * 2, [state, left], [],
+            2 * work, coefficient, factors[1],
+        )
+        one_arrived = swap(one)
+        (two,) = call(
+            functools.partial(expand_side, 1 - first), [VMEM] * 2, [state], [],
+            2 * work, rows, factors[1],
+        )
+        return one, two, one_arrived
 
     def row_pass(arrived, energy=True):
+        own, other, for_other = expand(arrived, row, 0)
+        for_own = swap(other)
+        (share,) = call(
+            row_first_kernel, [VMEM] * 5, [part], values, work,
+            other, for_other, base[1], rate[1], row[0],
+        )
         return call(
-            row_kernel, [VMEM] * 6, [coefficients] + [column] * energy, values, work,
-            row_live, *expand(arrived, row), base, rate, row[0],
-        )
-
-    arrived, start_z, start_m, base, rate, step, row_live, col_live = (
+            row_second_kernel, [VMEM] * 7, [coefficients] + [column] * energy, values, work,
+            row_live, own, for_own, base[0], rate[0], row[0], share,
+        )
+
+    def col_pass(weight, arrived, z, m):
+        own, other, for_other = expand(arrived, col, 0)
+        for_own = swap(other)
+        share, z_partner, m_partner = call(
+            functools.partial(col_first_kernel, weight), [VMEM] * 6, [part, state, state],
+            values, work, other, for_other, step, z[1], m[1], col[0],
+        )
+        out, z_here, m_here = call(
+            functools.partial(col_second_kernel, weight), [VMEM] * 8,
+            [coefficients, state, state], values, work,
+            col_live, own, for_own, step, z[0], m[0], col[0], share,
+        )
+        return out, (z_here, z_partner), (m_here, m_partner)
+
+    arrived, position, momentum, z_other, m_other, base, rate, step, row_live, col_live = (
         lax.optimization_barrier(
-            (arrived, start_z, start_m, base, rate, step, row_live, col_live)
-        )
-    )
-    z, m = start_z, start_m
+            (
+                arrived, position, momentum, z_other, m_other,
+                base, rate, step, row_live, col_live,
+            )
+        )
+    )
+    z, m = (position, z_other), (momentum, m_other)
     row = merge(arrived, row_whole)
     out, start_energy = row_pass(arrived)
     out, col_other = lax.optimization_barrier((out, col_other))
     arrived = spread(out)
     col = merge(arrived, col_own, col_other)
-    for weight in (0.5, 1.0):
-        out, z, m = call(
-            functools.partial(col_kernel, weight),
-            [VMEM] * 7, [coefficients, state, state], values, work,
-            col_live, *expand(arrived, col), step, z, m, col[0],
-        )
-        last = weight == 1.0
-        out, *energy = row_pass(spread(out), last)
-        arrived = spread(out)
-    (end_energy,) = energy
+    out, z, m = col_pass(0.5, arrived, z, m)
+    (out,) = row_pass(spread(out), False)
+    out, z, m = col_pass(1.0, spread(out), z, m)
+    out, end_energy = row_pass(spread(out))
+    _, own, for_own = expand(spread(out), col, 1)
     m, change = call(
-        last_kernel, [VMEM] * 9, [own_state, ((tiles, 1, chains), F32)], [], 1 << 24,
-        *expand(arrived, col), step, z, m, start_z, start_m,
-        start_energy, end_energy,
+        last_kernel, [VMEM] * 9, [state, ((tiles, 1, chains), F32)], [], 1 << 24,
+        own, for_own, step, z[0], m[0], position, momentum, start_energy, end_energy,
     )
     change = spread(change)
-    z = z[:, :cells]
     change = change.sum(axis=(0, 1))
     change = change + swap(change)
-    return z, m, change
+    return z[0], m, change
 
 
 def solution(mesh):

time: 227 us -> 232 us (1.022)
  waiting for transfers between devices: 17.9 us -> 23.2 us
    all_to_all x1, waiting for transfers between devices: 4.2 us -> 14.3 us  [spread(): return lax.all_to_all(value, CHIPS, split_axis=0, concat_axis=0, tiled=True)]
    ppermute x14 -> x19, waiting for transfers between devices: 13.7 us -> 8.96 us  [swap(): return lax.ppermute(value, CORE, [(0, 1), (1, 0)])]
    pallas_call x2, Pallas kernels: 10.3 us -> 7.92 us  [merge(): pl.pallas_call(merge_kernel, in_specs=[ANY] * (1 + len(parts)), out_specs...]
    pallas_call x13 -> x24, Pallas kernels: 23 us -> 25.2 us  [call(): pl.pallas_call(kernel, in_specs=specs, out_specs=[VMEM] * len(outs), out_...]
    ppermute x14 -> x19, starting transfers between devices: 20 us -> 19.9 us  [swap(): return lax.ppermute(value, CORE, [(0, 1), (1, 0)])]
  transfers between devices with their start and end apart: 15 -> 20, of which waited for: 9 -> 14; matrix products, arithmetic and copies ran while one was open for 1% -> 0% of each run, Pallas kernels for 14% -> 16%
where the time goes in v4:
time: 232 us; the launch traced here: 231 us
  blocking collectives  120 us (52%)
  Pallas kernels  54.1 us (23%)
  starting transfers between devices  31.2 us (13%)
  waiting for transfers between devices  23.2 us (10%)
    all_to_all x6, blocking collectives, spread(): return lax.all_to_all(value, CHIPS, split_axis=0, concat_axis=0, tiled=True)  120 us
    pallas_call x24, Pallas kernels, call(): pl.pallas_call(kernel, in_specs=specs, out_specs=[VMEM] * len(outs), out_...  25.2 us
    ppermute x19, starting transfers between devices, swap(): return lax.ppermute(value, CORE, [(0, 1), (1, 0)])  19.9 us
    all_to_all x1, waiting for transfers between devices, spread(): return lax.all_to_all(value, CHIPS, split_axis=0, concat_axis=0, tiled=True)  14.3 us
    all_to_all x1, starting transfers between devices, spread(): return lax.all_to_all(value, CHIPS, split_axis=0, concat_axis=0, tiled=True)  11.2 us
    pallas_call x1, Pallas kernels, row_setup(): pl.pallas_call(row_setup_kernel, in_specs=[SMEM, ANY, ANY], out_specs=ANY...  11 us
    pallas_call x1, Pallas kernels, col_setup(): pl.pallas_call(col_setup_kernel, in_specs=[SMEM, ANY, ANY, ANY], out_spec...  9.95 us
    ppermute x19, waiting for transfers between devices, swap(): return lax.ppermute(value, CORE, [(0, 1), (1, 0)])  8.96 us
  transfers between devices with their start and end apart: 20, of which 14 were waited for; matrix products, arithmetic and copies ran while one was open for 0% of the time, Pallas kernels for 16%

profile of v4, /device:TPU:1, one launch (start us, length us, event | category | flops | bytes accessed | tf_op | source)
XLA Modules:
  0.0 231.2 jit_solution(4346338083304711350)
XLA Ops:
  0.6 1.5 collective-permute-start.5
  2.2 10.0 %shard_map.103 = (bf16[16,512,256]{2,1,0:T(8,128)(2,1)}, bf16[16,512,256]{2,1,0:T(8,128)(2,1)}, bf16[64,64,128]{2,1,0:T(8,128)(2,1)S(1)}, bf16[64,64,128]{2,1,0:T(8,128)(2,1)S(1)}) custom-call(s32[2]{0:T(128)S(1)} %pad_add_fusion.place_ref, bf16[32768,128]{1,0:T(8,128)(2,1)} %bitcast.21, s32[64,64]{1,0:T(8,128)} %ranks_ref.1, f32[128,512]{1,0:T(8,128)} %start_z_ref), custom_call_target="tpu_custom_call" | custom-call | flops 8000000000 | bytes 16777216 | tf_op jit(solution)/shard_map/pallas_call | solution.py:162
  12.3 4.3 %collective-permute-done.arrived_ref = bf16[64,64,128]{2,1,0:T(8,128)(2,1)S(1)} collective-permute-done((bf16[64,64,128]{2,1,0:T(8,128)(2,1)S(1)}, bf16[64,64,128]{2,1,0:T(8,128)(2,1)S(1)}, u32[]{:S(2)}, u32[]{:S(2)}) %collective-permute-start) | collective-permute-done | bytes 1048608 | tf_op jit(solution)/shard_map/ppermute | solution.py:24
  16.6 1.3 shard_map.104
  18.3 11.2 %all-to-all-start = ((bf16[64,64,128]{2,1,0:T(8,128)(2,1)}), bf16[64,64,128]{2,1,0:T(8,128)(2,1)S(1)}, u32[]{:S(2)}, u32[]{:S(2)}) async-start(bf16[64,64,128]{2,1,0:T(8,128)(2,1)} %shard_map.104), calls=%async_computation | async-start | bytes 2097152 | tf_op jit(solution)/shard_map/all_to_all | solution.py:28
  31.7 0.8 collective-permute-done.3
  32.5 14.3 %all-to-all-done.after_ref.coefficient_ref = bf16[64,64,128]{2,1,0:T(8,128)(2,1)S(1)} async-done(((bf16[64,64,128]{2,1,0:T(8,128)(2,1)}), bf16[64,64,128]{2,1,0:T(8,128)(2,1)S(1)}, u32[]{:S(2)}, u32[]{:S(2)}) %all-to-all-start) | async-done | bytes 1048608 | tf_op jit(solution)/shard_map/all_to_all | solution.py:28
  46.9 11.0 %shard_map.105.refs_0_ = bf16[2,16,512,256]{3,2,1,0:T(8,128)(2,1)} custom-call(s32[2]{0:T(128)S(1)} %pad_add_fusion.place_ref, bf16[32768,128]{1,0:T(8,128)(2,1)} %bitcast.22, bf16[32768,128]{1,0:T(8,128)(2,1)} %bitcast.8.other_raw_ref), custom_call_target="tpu_custom_call" | custom-call | flops 8000000000 | bytes 16777216 | tf_op jit(solution)/shard_map/pallas_call | solution.py:251
  57.9 4.0 %shard_map.106 = (bf16[2,16,512,256]{3,2,1,0:T(8,128)(2,1)S(1)}, bf16[2,16,256,512]{3,2,1,0:T(8,128)(2,1)S(1)}) custom-call(bf16[64,64,128]{2,1,0:T(8,128)(2,1)S(1)} %all-to-all-done.after_ref.coefficient_ref, bf16[2,16,512,256]{3,2,1,0:T(8,128)(2,1)} %shard_map.105.refs_0_), custom_call_target="tpu_custom_call" | custom-call | flops 4000000000 | bytes 16777216 | tf_op jit(solution)/shard_map/pallas_call | solution.py:310
  61.9 1.2 shard_map.107
  63.1 2.3 %collective-permute-start.7 = (f32[128,512]{1,0:T(8,128)S(1)}, f32[128,512]{1,0:T(8,128)S(1)}, u32[]{:S(2)}, u32[]{:S(2)}) collective-permute-start(f32[128,512]{1,0:T(8,128)S(1)} %get-tuple-element.77.total_ref), channel_id=1, source_target_pairs={{0,1},{1,0},{2,3},{3,2},{4,5},{5,4},{6,7},{7,6},{8,9},{9,8},{10,11... | collective-permute-start | bytes 786440 | tf_op jit(solution)/shard_map/ppermute | solution.py:24
  65.5 0.7 shard_map.108.total_ref
  66.6 1.0 shard_map.109.part_ref
  67.8 1.2 shard_map.110
  69.0 21.5 %all_to_all.35.after_ref.coefficient_ref = bf16[64,64,128]{2,1,0:T(8,128)(2,1)S(1)} all-to-all(bf16[64,64,128]{2,1,0:T(8,128)(2,1)S(1)} %get-tuple-element.86), channel_id=1, replica_groups=mesh['col_0'=4,'col_1'=4,'row_0'=4,'row_1'=2] {'col_0','col_1','row_0'}, dimensions={0} | all-to-all | bytes 2097152 | tf_op jit(solution)/shard_map/all_to_all | solution.py:28
  90.5 4.0 %shard_map.111 = (bf16[2,16,512,256]{3,2,1,0:T(8,128)(2,1)S(1)}, bf16[2,16,256,512]{3,2,1,0:T(8,128)(2,1)S(1)}) custom-call(bf16[64,64,128]{2,1,0:T(8,128)(2,1)S(1)} %all_to_all.35.after_ref.coefficient_ref, bf16[16,512,256]{2,1,0:T(8,128)(2,1)} %get-tuple-element.87.refs_0_, bf16[16,512,256]{2,1,0:T(8,128)(2,1)} %collective-permute-done.8.refs_1_), custom_call_target="tpu_custom_call" | custom-call | flops 4000000000 | bytes 16777216 | tf_op jit(solution)/shard_map/pallas_call | solution.py:310
  94.5 1.2 shard_map.112
  95.7 2.3 %collective-permute-start.10 = (f32[128,512]{1,0:T(8,128)S(1)}, f32[128,512]{1,0:T(8,128)S(1)}, u32[]{:S(2)}, u32[]{:S(2)}) collective-permute-start(f32[128,512]{1,0:T(8,128)S(1)} %get-tuple-element.90.total_ref), channel_id=1, source_target_pairs={{0,1},{1,0},{2,3},{3,2},{4,5},{5,4},{6,7},{7,6},{8,9},{9,8},{10,11... | collective-permute-start | bytes 786440 | tf_op jit(solution)/shard_map/ppermute | solution.py:24
  98.1 0.7 shard_map.113.total_ref
  99.2 1.0 shard_map.114
  100.4 1.2 shard_map.115
  101.6 21.4 %all_to_all.36.coefficient_ref = bf16[64,64,128]{2,1,0:T(8,128)(2,1)S(1)} all-to-all(bf16[64,64,128]{2,1,0:T(8,128)(2,1)S(1)} %get-tuple-element.99), channel_id=1, replica_groups=mesh['col_0'=4,'col_1'=4,'row_0'=4,'row_1'=2] {'col_0','col_1','row_0'}, dimensions={0} | all-to-all | bytes 2097152 | tf_op jit(solution)/shard_map/all_to_all | solution.py:28
  123.0 1.2 shard_map.116
  124.3 2.4 %collective-permute-start.12 = (f32[128,512]{1,0:T(8,128)S(1)}, f32[128,512]{1,0:T(8,128)S(1)}, u32[]{:S(2)}, u32[]{:S(2)}) collective-permute-start(f32[128,512]{1,0:T(8,128)S(1)} %get-tuple-element.100.total_ref), channel_id=1, source_target_pairs={{0,1},{1,0},{2,3},{3,2},{4,5},{5,4},{6,7},{7,6},{8,9},{9,8},{10,11... | collective-permute-start | bytes 786440 | tf_op jit(solution)/shard_map/ppermute | solution.py:24
  126.7 0.7 shard_map.117.total_ref
  127.9 0.9 shard_map.118.part_ref
  129.1 1.1 shard_map.119
  130.2 21.6 %all_to_all.37.coefficient_ref = bf16[64,64,128]{2,1,0:T(8,128)(2,1)S(1)} all-to-all(bf16[64,64,128]{2,1,0:T(8,128)(2,1)S(1)} %shard_map.119), channel_id=1, replica_groups=mesh['col_0'=4,'col_1'=4,'row_0'=4,'row_1'=2] {'col_0','col_1','row_0'}, dimensions={0} | all-to-all | bytes 2097152 | tf_op jit(solution)/shard_map/all_to_all | solution.py:28
  151.7 1.2 shard_map.120
  153.0 2.3 %collective-permute-start.14 = (f32[128,512]{1,0:T(8,128)S(1)}, f32[128,512]{1,0:T(8,128)S(1)}, u32[]{:S(2)}, u32[]{:S(2)}) collective-permute-start(f32[128,512]{1,0:T(8,128)S(1)} %get-tuple-element.102.total_ref), channel_id=1, source_target_pairs={{0,1},{1,0},{2,3},{3,2},{4,5},{5,4},{6,7},{7,6},{8,9},{9,8},{10,11... | collective-permute-start | bytes 786440 | tf_op jit(solution)/shard_map/ppermute | solution.py:24
  155.3 0.7 shard_map.121.total_ref
  156.5 1.4 shard_map.122
  157.9 1.4 shard_map.123
  159.3 21.3 %all_to_all.38.coefficient_ref = bf16[64,64,128]{2,1,0:T(8,128)(2,1)S(1)} all-to-all(bf16[64,64,128]{2,1,0:T(8,128)(2,1)S(1)} %get-tuple-element.110), channel_id=1, replica_groups=mesh['col_0'=4,'col_1'=4,'row_0'=4,'row_1'=2] {'col_0','col_1','row_0'}, dimensions={0} | all-to-all | bytes 2097152 | tf_op jit(solution)/shard_map/all_to_all | solution.py:28
  180.6 1.2 shard_map.124
  181.8 2.5 %collective-permute-start.16 = (f32[128,512]{1,0:T(8,128)S(1)}, f32[128,512]{1,0:T(8,128)S(1)}, u32[]{:S(2)}, u32[]{:S(2)}) collective-permute-start(f32[128,512]{1,0:T(8,128)S(1)} %get-tuple-element.111.total_ref), channel_id=1, source_target_pairs={{0,1},{1,0},{2,3},{3,2},{4,5},{5,4},{6,7},{7,6},{8,9},{9,8},{10,11... | collective-permute-start | bytes 786440 | tf_op jit(solution)/shard_map/ppermute | solution.py:24
  184.4 0.7 shard_map.125.total_ref
  185.5 0.9 shard_map.126.part_ref
  186.7 1.2 shard_map.127
  187.9 21.6 %all_to_all.39.coefficient_ref = bf16[64,64,128]{2,1,0:T(8,128)(2,1)S(1)} all-to-all(bf16[64,64,128]{2,1,0:T(8,128)(2,1)S(1)} %get-tuple-element.113), channel_id=1, replica_groups=mesh['col_0'=4,'col_1'=4,'row_0'=4,'row_1'=2] {'col_0','col_1','row_0'}, dimensions={0} | all-to-all | bytes 2097152 | tf_op jit(solution)/shard_map/all_to_all | solution.py:28
  209.5 1.2 shard_map.128
  210.7 2.3 %collective-permute-start.17 = (f32[128,512]{1,0:T(8,128)S(1)}, f32[128,512]{1,0:T(8,128)S(1)}, u32[]{:S(2)}, u32[]{:S(2)}) collective-permute-start(f32[128,512]{1,0:T(8,128)S(1)} %get-tuple-element.115), channel_id=1, source_target_pairs={{0,1},{1,0},{2,3},{3,2},{4,5},{5,4},{6,7},{7,6},{8,9},{9,8},{10,11... | collective-permute-start | bytes 786440 | tf_op jit(solution)/shard_map/ppermute | solution.py:24
  213.1 0.7 shard_map.129.total_ref
  214.3 0.9 shard_map.130
  215.2 12.7 %all_to_all.40 = f32[64,1,128]{2,1,0:T(1,128)S(1)} all-to-all(f32[64,1,128]{2,1,0:T(1,128)S(1)} %get-tuple-element.120), channel_id=1, replica_groups=mesh['col_0'=4,'col_1'=4,'row_0'=4,'row_1'=2] {'col_0','col_1','row_0'}, dimensions={0} | all-to-all | bytes 65536 | tf_op jit(solution)/shard_map/all_to_all | solution.py:28
  228.0 1.9 collective-permute-start.18
  229.8 0.8 collective-permute-done.18
  230.7 0.5 add.43
  (59 shorter events, 6.4 us)
Async XLA Ops:
  0.6 46.3 %collective-permute-start.5 = (bf16[512,64,128]{2,1,0:T(8,128)(2,1)}, bf16[512,64,128]{2,1,0:T(8,128)(2,1)}, u32[]{:S(2)}, u32[]{:S(2)}) collective-permute-start(bf16[512,64,128]{2,1,0:T(8,128)(2,1)} %param.10), channel_id=1, source_target_pairs={{0,1},{1,0},{2,3},{3,2},{4,5},{5,4},{6,7},{7,6},{8,9},{9,8},{10,11... | collective-permute-start | bytes 25165832 | tf_op jit(solution)/shard_map/ppermute | solution.py:24
  2.2 27.4 %copy-start.4 = (s32[64,64]{1,0:T(8,128)S(1)}, s32[64,64]{1,0:T(8,128)}, u32[]{:S(2)}) copy-start(s32[64,64]{1,0:T(8,128)} %ranks_ref.1) | copy-start | bytes 49156
  2.2 27.8 %copy-start.5 = (s32[512]{0:T(512)S(1)}, s32[512]{0:T(512)}, u32[]{:S(2)}) copy-start(s32[512]{0:T(512)} %param.14) | copy-start | bytes 6148
  2.2 28.3 %copy-start = (f32[128,512]{1,0:T(8,128)S(1)}, f32[128,512]{1,0:T(8,128)}, u32[]{:S(2)}) copy-start(f32[128,512]{1,0:T(8,128)} %start_z_ref) | copy-start | bytes 786436
  2.2 28.4 %copy-start.1 = (f32[128,512]{1,0:T(8,128)S(1)}, f32[128,512]{1,0:T(8,128)}, u32[]{:S(2)}) copy-start(f32[128,512]{1,0:T(8,128)} %start_m_ref) | copy-start | bytes 786436
  2.2 29.1 %copy-start.3 = (f32[512]{0:T(512)S(1)}, f32[512]{0:T(512)}, u32[]{:S(2)}) copy-start(f32[512]{0:T(512)} %param.13) | copy-start | bytes 6148
  2.2 44.6 %copy-start.6 = (f32[128]{0:T(128)S(1)}, f32[128]{0:T(128)}, u32[]{:S(2)}) copy-start(f32[128]{0:T(128)} %param.15) | copy-start | bytes 1540
  12.2 4.4 %collective-permute-start = (bf16[64,64,128]{2,1,0:T(8,128)(2,1)S(1)}, bf16[64,64,128]{2,1,0:T(8,128)(2,1)S(1)}, u32[]{:S(2)}, u32[]{:S(2)}) collective-permute-start(bf16[64,64,128]{2,1,0:T(8,128)(2,1)S(1)} %get-tuple-element.63), channel_id=1, source_target_pairs={{0,1},{1,0},{2,3},{3,2},{4,5},{5,4},{6,7},{7,6},{8,9},{9,8},{10,11... | collective-permute-start | bytes 3145736 | tf_op jit(solution)/shard_map/ppermute | solution.py:24
  17.9 51.1 %collective-permute-start.8 = (bf16[16,512,256]{2,1,0:T(8,128)(2,1)}, bf16[16,512,256]{2,1,0:T(8,128)(2,1)}, u32[]{:S(2)}, u32[]{:S(2)}) collective-permute-start(bf16[16,512,256]{2,1,0:T(8,128)(2,1)} %get-tuple-element.85), channel_id=1, source_target_pairs={{0,1},{1,0},{2,3},{3,2},{4,5},{5,4},{6,7},{7,6},{8,9},{9,8},{10,11... | collective-permute-start | bytes 12582920 | tf_op jit(solution)/shard_map/ppermute | solution.py:24
  18.3 28.5 %all-to-all-start = ((bf16[64,64,128]{2,1,0:T(8,128)(2,1)}), bf16[64,64,128]{2,1,0:T(8,128)(2,1)S(1)}, u32[]{:S(2)}, u32[]{:S(2)}) async-start(bf16[64,64,128]{2,1,0:T(8,128)(2,1)} %shard_map.104), calls=%async_computation | async-start | bytes 2097152 | tf_op jit(solution)/shard_map/all_to_all | solution.py:28
  30.0 1.4 collective-permute-start.4
  30.4 2.1 collective-permute-start.1
  30.6 2.0 collective-permute-start.2
  31.3 1.2 collective-permute-start.3
  63.1 3.5 %collective-permute-start.7 = (f32[128,512]{1,0:T(8,128)S(1)}, f32[128,512]{1,0:T(8,128)S(1)}, u32[]{:S(2)}, u32[]{:S(2)}) collective-permute-start(f32[128,512]{1,0:T(8,128)S(1)} %get-tuple-element.77.total_ref), channel_id=1, source_target_pairs={{0,1},{1,0},{2,3},{3,2},{4,5},{5,4},{6,7},{7,6},{8,9},{9,8},{10,11... | collective-permute-start | bytes 786440 | tf_op jit(solution)/shard_map/ppermute | solution.py:24
  66.2 1.6 collective-permute-start.6
  95.7 3.5 %collective-permute-start.10 = (f32[128,512]{1,0:T(8,128)S(1)}, f32[128,512]{1,0:T(8,128)S(1)}, u32[]{:S(2)}, u32[]{:S(2)}) collective-permute-start(f32[128,512]{1,0:T(8,128)S(1)} %get-tuple-element.90.total_ref), channel_id=1, source_target_pairs={{0,1},{1,0},{2,3},{3,2},{4,5},{5,4},{6,7},{7,6},{8,9},{9,8},{10,11... | collective-permute-start | bytes 786440 | tf_op jit(solution)/shard_map/ppermute | solution.py:24
  98.8 1.6 collective-permute-start.9
  124.3 3.6 %collective-permute-start.12 = (f32[128,512]{1,0:T(8,128)S(1)}, f32[128,512]{1,0:T(8,128)S(1)}, u32[]{:S(2)}, u32[]{:S(2)}) collective-permute-start(f32[128,512]{1,0:T(8,128)S(1)} %get-tuple-element.100.total_ref), channel_id=1, source_target_pairs={{0,1},{1,0},{2,3},{3,2},{4,5},{5,4},{6,7},{7,6},{8,9},{9,8},{10,11... | collective-permute-start | bytes 786440 | tf_op jit(solution)/shard_map/ppermute | solution.py:24
  127.4 1.6 collective-permute-start.11
  153.0 3.5 %collective-permute-start.14 = (f32[128,512]{1,0:T(8,128)S(1)}, f32[128,512]{1,0:T(8,128)S(1)}, u32[]{:S(2)}, u32[]{:S(2)}) collective-permute-start(f32[128,512]{1,0:T(8,128)S(1)} %get-tuple-element.102.total_ref), channel_id=1, source_target_pairs={{0,1},{1,0},{2,3},{3,2},{4,5},{5,4},{6,7},{7,6},{8,9},{9,8},{10,11... | collective-permute-start | bytes 786440 | tf_op jit(solution)/shard_map/ppermute | solution.py:24
  156.0 1.8 collective-permute-start.13
  181.8 3.7 %collective-permute-start.16 = (f32[128,512]{1,0:T(8,128)S(1)}, f32[128,512]{1,0:T(8,128)S(1)}, u32[]{:S(2)}, u32[]{:S(2)}) collective-permute-start(f32[128,512]{1,0:T(8,128)S(1)} %get-tuple-element.111.total_ref), channel_id=1, source_target_pairs={{0,1},{1,0},{2,3},{3,2},{4,5},{5,4},{6,7},{7,6},{8,9},{9,8},{10,11... | collective-permute-start | bytes 786440 | tf_op jit(solution)/shard_map/ppermute | solution.py:24
  185.1 1.6 collective-permute-start.15
  209.5 4.8 %copy-start.2 = (f32[128,512]{1,0:T(8,128)S(1)}, f32[128,512]{1,0:T(8,128)}, u32[]{:S(2)}) copy-start(f32[128,512]{1,0:T(8,128)} %get-tuple-element.59.z_ref) | copy-start | bytes 786436
  210.7 3.5 %collective-permute-start.17 = (f32[128,512]{1,0:T(8,128)S(1)}, f32[128,512]{1,0:T(8,128)S(1)}, u32[]{:S(2)}, u32[]{:S(2)}) collective-permute-start(f32[128,512]{1,0:T(8,128)S(1)} %get-tuple-element.115), channel_id=1, source_target_pairs={{0,1},{1,0},{2,3},{3,2},{4,5},{5,4},{6,7},{7,6},{8,9},{9,8},{10,11... | collective-permute-start | bytes 786440 | tf_op jit(solution)/shard_map/ppermute | solution.py:24
  228.0 2.7 %collective-permute-start.18 = (f32[128]{0:T(128)S(1)}, f32[128]{0:T(128)S(1)}, u32[]{:S(2)}, u32[]{:S(2)}) collective-permute-start(f32[128]{0:T(128)S(1)} %reduce_sum.9), channel_id=1, source_target_pairs={{0,1},{1,0},{2,3},{3,2},{4,5},{5,4},{6,7},{7,6},{8,9},{9,8},{10,11... | collective-permute-start | bytes 1544 | tf_op jit(solution)/shard_map/ppermute | solution.py:24

commit v5 on v4

--- a/solution.py
+++ b/solution.py
@@ -340,20 +340,32 @@
 
 
 def expand_first_kernel(side, coefficient_ref, turned_ref, total_ref, left_ref):
-    half = coefficient_ref.shape[1]
-
-    def arrange(q, carry):
+    quads, cells = turned_ref.shape[1], turned_ref.shape[3]
+    blocks = [slice(256 * b, 256 * b + 256) for b in range(cells // 256)]
+    totals = [0.0] * len(blocks)
+    for q in range(quads):
+        pairs = []
         for pair in range(2):
             one = coefficient_ref[q + 32 * pair]
             two = coefficient_ref[q + 32 * pair + 16]
             low = low_lanes(one)
-            lanes = slice(pair * 128, pair * 128 + 128)
-            left_ref[q, :half, lanes] = jnp.where(low, one, other_half(two))
-            left_ref[q, half:, lanes] = jnp.where(low, other_half(one), two)
-        return carry
-
-    lax.fori_loop(0, left_ref.shape[0], arrange, 0, unroll=4)
-    expand_side(side, left_ref, turned_ref, total_ref)
+            pairs.append(
+                jnp.concatenate(
+                    [
+                        jnp.where(low, one, other_half(two)),
+                        jnp.where(low, other_half(one), two),
+                    ],
+                    axis=0,
+                )
+            )
+        left = jnp.concatenate(pairs, axis=1)
+        left_ref[q] = left
+        for b, at_cell in enumerate(blocks):
+            totals[b] += jnp.dot(
+                left, turned_ref[side, q, :, at_cell], preferred_element_type=F32
+            )
+    for b, at_cell in enumerate(blocks):
+        total_ref[:, at_cell] = totals[b]
 
 
 def project(factor, quads, live, out_ref):
@@ -383,14 +395,14 @@
 
 
 def col_values(
-    weight, total_ref, arrived_ref, step_ref, z_ref, m_ref, new_z_ref, new_m_ref, values
+    weight, total_ref, arrived_ref, step_ref, z_ref, m_ref, state_refs, values
 ):
     step = step_ref[:, :1]
     z = z_ref[...]
     moment = m_ref[...] - weight * step * (z - (total_ref[...] + arrived_ref[...]))
     z = z + step * moment
-    new_m_ref[...] = moment
-    new_z_ref[...] = z
+    for ref, new in zip(state_refs, (z, moment)):
+        ref[...] = new
     values[...] = z.astype(BF16)
 
 
@@ -430,11 +442,11 @@
 
 
 def col_first_kernel(
-    weight, total_ref, arrived_ref, step_ref, z_ref, m_ref, f_ref,
-    part_ref, new_z_ref, new_m_ref, values,
+    weight, total_ref, arrived_ref, step_ref, z_ref, m_ref, f_ref, part_ref, *refs
 ):
+    *state_refs, values = refs
     col_values(
-        weight, total_ref, arrived_ref, step_ref, z_ref, m_ref, new_z_ref, new_m_ref, values
+        weight, total_ref, arrived_ref, step_ref, z_ref, m_ref, state_refs, values
     )
     project_first(values, f_ref, part_ref)
 
@@ -444,7 +456,8 @@
     out_ref, new_z_ref, new_m_ref, values,
 ):
     col_values(
-        weight, total_ref, arrived_ref, step_ref, z_ref, m_ref, new_z_ref, new_m_ref, values
+        weight, total_ref, arrived_ref, step_ref, z_ref, m_ref,
+        (new_z_ref, new_m_ref), values,
     )
     project_second(values, f_ref, part_ref, live_ref, out_ref)
 
@@ -514,14 +527,10 @@
     )
     sent = swap(send)
     (out,) = call(add_kernel, [VMEM] * 2, [coefficients], [], 1 << 24, keep, sent)
-    out, col_sent, row_factors, late = lax.optimization_barrier(
-        (
-            out, col_sent, row_factors,
-            (position, momentum, tile_ranks, log_mean, counts, step_size),
-        )
+    out, col_sent, row_factors, tile_ranks, step_size = lax.optimization_barrier(
+        (out, col_sent, row_factors, tile_ranks, step_size)
     )
     arrived = spread(out)
-    position, momentum, tile_ranks, log_mean, counts, step_size = late
     row_whole = row_setup(row_factors, row_arrived, place)
     rate = counts.astype(F32)
     z_other, m_other = swap(position), swap(momentum)
@@ -557,19 +566,19 @@
             row_live, own, for_own, base[0], rate[0], row[0], share,
         )
 
-    def col_pass(weight, arrived, z, m):
+    def col_pass(weight, arrived, z, m, final=False):
         own, other, for_other = expand(arrived, col, 0)
         for_own = swap(other)
-        share, z_partner, m_partner = call(
-            functools.partial(col_first_kernel, weight), [VMEM] * 6, [part, state, state],
-            values, work, other, for_other, step, z[1], m[1], col[0],
+        share, *partner = call(
+            functools.partial(col_first_kernel, weight), [VMEM] * 6,
+            [part] + [state] * (0 if final else 2), values, work, other, for_other, step, z[1], m[1], col[0],
         )
         out, z_here, m_here = call(
             functools.partial(col_second_kernel, weight), [VMEM] * 8,
             [coefficients, state, state], values, work,
             col_live, own, for_own, step, z[0], m[0], col[0], share,
         )
-        return out, (z_here, z_partner), (m_here, m_partner)
+        return out, (z_here, *partner[:1]), (m_here, *partner[1:])
 
     arrived, position, momentum, z_other, m_other, base, rate, step, row_live, col_live = (
         lax.optimization_barrier(
@@ -587,7 +596,7 @@
     col = merge(arrived, col_own, col_other)
     out, z, m = col_pass(0.5, arrived, z, m)
     (out,) = row_pass(spread(out), False)
-    out, z, m = col_pass(1.0, spread(out), z, m)
+    out, z, m = col_pass(1.0, spread(out), z, m, final=True)
     out, end_energy = row_pass(spread(out))
     _, own, for_own = expand(spread(out), col, 1)
     m, change = call(

time: 232 us -> 229 us (0.987)
  Pallas kernels: 54.1 us -> 50.8 us
    pallas_call x24, Pallas kernels: 25.2 us -> 21.9 us  [call(): pl.pallas_call(kernel, in_specs=specs, out_specs=[VMEM] * len(outs), out_...]
  transfers between devices with their start and end apart: 20 -> 20, of which waited for: 14 -> 15; matrix products, arithmetic and copies ran while one was open for 0% -> 0% of each run, Pallas kernels for 16% -> 16%
where the time goes in v5:
time: 229 us; the launch traced here: 228 us
  blocking collectives  120 us (52%)
  Pallas kernels  50.8 us (22%)
  starting transfers between devices  31.3 us (14%)
  waiting for transfers between devices  23.4 us (10%)
    all_to_all x6, blocking collectives, spread(): return lax.all_to_all(value, CHIPS, split_axis=0, concat_axis=0, tiled=True)  120 us
    pallas_call x24, Pallas kernels, call(): pl.pallas_call(kernel, in_specs=specs, out_specs=[VMEM] * len(outs), out_...  21.9 us
    ppermute x19, starting transfers between devices, swap(): return lax.ppermute(value, CORE, [(0, 1), (1, 0)])  20.1 us
    all_to_all x1, waiting for transfers between devices, spread(): return lax.all_to_all(value, CHIPS, split_axis=0, concat_axis=0, tiled=True)  14.3 us
    all_to_all x1, starting transfers between devices, spread(): return lax.all_to_all(value, CHIPS, split_axis=0, concat_axis=0, tiled=True)  11.2 us
    pallas_call x1, Pallas kernels, row_setup(): pl.pallas_call(row_setup_kernel, in_specs=[SMEM, ANY, ANY], out_specs=ANY...  11 us
    pallas_call x1, Pallas kernels, col_setup(): pl.pallas_call(col_setup_kernel, in_specs=[SMEM, ANY, ANY, ANY], out_spec...  9.95 us
    ppermute x19, waiting for transfers between devices, swap(): return lax.ppermute(value, CORE, [(0, 1), (1, 0)])  9.12 us
  transfers between devices with their start and end apart: 20, of which 15 were waited for; matrix products, arithmetic and copies ran while one was open for 0% of the time, Pallas kernels for 16%

profile of v5, /device:TPU:1, one launch (start us, length us, event | category | flops | bytes accessed | tf_op | source)
XLA Modules:
  0.0 228.2 jit_solution(14263576620944791035)
XLA Ops:
  0.6 1.5 collective-permute-start.5
  2.2 10.0 %shard_map.103 = (bf16[16,512,256]{2,1,0:T(8,128)(2,1)}, bf16[16,512,256]{2,1,0:T(8,128)(2,1)}, bf16[64,64,128]{2,1,0:T(8,128)(2,1)S(1)}, bf16[64,64,128]{2,1,0:T(8,128)(2,1)S(1)}) custom-call(s32[2]{0:T(128)S(1)} %pad_add_fusion.place_ref, bf16[32768,128]{1,0:T(8,128)(2,1)} %bitcast.21, s32[64,64]{1,0:T(8,128)} %ranks_ref.1, f32[128,512]{1,0:T(8,128)} %start_z_ref), custom_call_target="tpu_custom_call" | custom-call | flops 8000000000 | bytes 16777216 | tf_op jit(solution)/shard_map/pallas_call | solution.py:162
  12.3 4.3 %collective-permute-done.arrived_ref = bf16[64,64,128]{2,1,0:T(8,128)(2,1)S(1)} collective-permute-done((bf16[64,64,128]{2,1,0:T(8,128)(2,1)S(1)}, bf16[64,64,128]{2,1,0:T(8,128)(2,1)S(1)}, u32[]{:S(2)}, u32[]{:S(2)}) %collective-permute-start) | collective-permute-done | bytes 1048608 | tf_op jit(solution)/shard_map/ppermute | solution.py:24
  16.6 1.3 shard_map.104
  18.2 11.2 %all-to-all-start = ((bf16[64,64,128]{2,1,0:T(8,128)(2,1)}), bf16[64,64,128]{2,1,0:T(8,128)(2,1)S(1)}, u32[]{:S(2)}, u32[]{:S(2)}) async-start(bf16[64,64,128]{2,1,0:T(8,128)(2,1)} %shard_map.104), calls=%async_computation | async-start | bytes 2097152 | tf_op jit(solution)/shard_map/all_to_all | solution.py:28
  31.6 0.8 collective-permute-done.3
  32.5 14.3 %all-to-all-done.after_ref.coefficient_ref = bf16[64,64,128]{2,1,0:T(8,128)(2,1)S(1)} async-done(((bf16[64,64,128]{2,1,0:T(8,128)(2,1)}), bf16[64,64,128]{2,1,0:T(8,128)(2,1)S(1)}, u32[]{:S(2)}, u32[]{:S(2)}) %all-to-all-start) | async-done | bytes 1048608 | tf_op jit(solution)/shard_map/all_to_all | solution.py:28
  46.9 11.0 %shard_map.105.refs_0_ = bf16[2,16,512,256]{3,2,1,0:T(8,128)(2,1)} custom-call(s32[2]{0:T(128)S(1)} %pad_add_fusion.place_ref, bf16[32768,128]{1,0:T(8,128)(2,1)} %bitcast.22, bf16[32768,128]{1,0:T(8,128)(2,1)} %bitcast.8.other_raw_ref), custom_call_target="tpu_custom_call" | custom-call | flops 8000000000 | bytes 16777216 | tf_op jit(solution)/shard_map/pallas_call | solution.py:251
  57.9 4.0 %shard_map.106 = (bf16[2,16,512,256]{3,2,1,0:T(8,128)(2,1)S(1)}, bf16[2,16,256,512]{3,2,1,0:T(8,128)(2,1)S(1)}) custom-call(bf16[64,64,128]{2,1,0:T(8,128)(2,1)S(1)} %all-to-all-done.after_ref.coefficient_ref, bf16[2,16,512,256]{3,2,1,0:T(8,128)(2,1)} %shard_map.105.refs_0_), custom_call_target="tpu_custom_call" | custom-call | flops 4000000000 | bytes 16777216 | tf_op jit(solution)/shard_map/pallas_call | solution.py:310
  61.9 0.7 shard_map.107
  62.6 2.3 %collective-permute-start.7 = (f32[128,512]{1,0:T(8,128)S(1)}, f32[128,512]{1,0:T(8,128)S(1)}, u32[]{:S(2)}, u32[]{:S(2)}) collective-permute-start(f32[128,512]{1,0:T(8,128)S(1)} %get-tuple-element.68.total_ref), channel_id=1, source_target_pairs={{0,1},{1,0},{2,3},{3,2},{4,5},{5,4},{6,7},{7,6},{8,9},{9,8},{10,11... | collective-permute-start | bytes 786440 | tf_op jit(solution)/shard_map/ppermute | solution.py:24
  65.0 0.7 shard_map.108.total_ref
  66.1 1.0 shard_map.109.part_ref
  67.3 1.2 shard_map.110
  68.5 21.5 %all_to_all.35.after_ref.coefficient_ref = bf16[64,64,128]{2,1,0:T(8,128)(2,1)S(1)} all-to-all(bf16[64,64,128]{2,1,0:T(8,128)(2,1)S(1)} %get-tuple-element.77), channel_id=1, replica_groups=mesh['col_0'=4,'col_1'=4,'row_0'=4,'row_1'=2] {'col_0','col_1','row_0'}, dimensions={0} | all-to-all | bytes 2097152 | tf_op jit(solution)/shard_map/all_to_all | solution.py:28
  90.0 4.0 %shard_map.111 = (bf16[2,16,512,256]{3,2,1,0:T(8,128)(2,1)S(1)}, bf16[2,16,256,512]{3,2,1,0:T(8,128)(2,1)S(1)}) custom-call(bf16[64,64,128]{2,1,0:T(8,128)(2,1)S(1)} %all_to_all.35.after_ref.coefficient_ref, bf16[16,512,256]{2,1,0:T(8,128)(2,1)} %get-tuple-element.78.refs_0_, bf16[16,512,256]{2,1,0:T(8,128)(2,1)} %collective-permute-done.8.refs_1_), custom_call_target="tpu_custom_call" | custom-call | flops 4000000000 | bytes 16777216 | tf_op jit(solution)/shard_map/pallas_call | solution.py:310
  94.0 0.8 shard_map.112
  94.8 2.3 %collective-permute-start.10 = (f32[128,512]{1,0:T(8,128)S(1)}, f32[128,512]{1,0:T(8,128)S(1)}, u32[]{:S(2)}, u32[]{:S(2)}) collective-permute-start(f32[128,512]{1,0:T(8,128)S(1)} %get-tuple-element.81.total_ref), channel_id=1, source_target_pairs={{0,1},{1,0},{2,3},{3,2},{4,5},{5,4},{6,7},{7,6},{8,9},{9,8},{10,11... | collective-permute-start | bytes 786440 | tf_op jit(solution)/shard_map/ppermute | solution.py:24
  97.1 0.7 shard_map.113.total_ref
  98.3 1.0 shard_map.114
  99.4 1.2 shard_map.115
  100.6 21.4 %all_to_all.36.coefficient_ref = bf16[64,64,128]{2,1,0:T(8,128)(2,1)S(1)} all-to-all(bf16[64,64,128]{2,1,0:T(8,128)(2,1)S(1)} %get-tuple-element.90), channel_id=1, replica_groups=mesh['col_0'=4,'col_1'=4,'row_0'=4,'row_1'=2] {'col_0','col_1','row_0'}, dimensions={0} | all-to-all | bytes 2097152 | tf_op jit(solution)/shard_map/all_to_all | solution.py:28
  122.1 0.8 shard_map.116
  122.8 2.4 %collective-permute-start.12 = (f32[128,512]{1,0:T(8,128)S(1)}, f32[128,512]{1,0:T(8,128)S(1)}, u32[]{:S(2)}, u32[]{:S(2)}) collective-permute-start(f32[128,512]{1,0:T(8,128)S(1)} %get-tuple-element.91.total_ref), channel_id=1, source_target_pairs={{0,1},{1,0},{2,3},{3,2},{4,5},{5,4},{6,7},{7,6},{8,9},{9,8},{10,11... | collective-permute-start | bytes 786440 | tf_op jit(solution)/shard_map/ppermute | solution.py:24
  125.3 0.7 shard_map.117.total_ref
  126.4 0.9 shard_map.118.part_ref
  127.6 1.1 shard_map.119
  128.7 21.6 %all_to_all.37.coefficient_ref = bf16[64,64,128]{2,1,0:T(8,128)(2,1)S(1)} all-to-all(bf16[64,64,128]{2,1,0:T(8,128)(2,1)S(1)} %shard_map.119), channel_id=1, replica_groups=mesh['col_0'=4,'col_1'=4,'row_0'=4,'row_1'=2] {'col_0','col_1','row_0'}, dimensions={0} | all-to-all | bytes 2097152 | tf_op jit(solution)/shard_map/all_to_all | solution.py:28
  150.3 0.7 shard_map.120
  151.0 2.3 %collective-permute-start.14 = (f32[128,512]{1,0:T(8,128)S(1)}, f32[128,512]{1,0:T(8,128)S(1)}, u32[]{:S(2)}, u32[]{:S(2)}) collective-permute-start(f32[128,512]{1,0:T(8,128)S(1)} %get-tuple-element.93.total_ref), channel_id=1, source_target_pairs={{0,1},{1,0},{2,3},{3,2},{4,5},{5,4},{6,7},{7,6},{8,9},{9,8},{10,11... | collective-permute-start | bytes 786440 | tf_op jit(solution)/shard_map/ppermute | solution.py:24
  153.4 0.7 shard_map.121.total_ref
  154.5 1.0 shard_map.122.part_ref
  155.7 1.4 shard_map.123
  157.1 21.4 %all_to_all.38.coefficient_ref = bf16[64,64,128]{2,1,0:T(8,128)(2,1)S(1)} all-to-all(bf16[64,64,128]{2,1,0:T(8,128)(2,1)S(1)} %get-tuple-element.100), channel_id=1, replica_groups=mesh['col_0'=4,'col_1'=4,'row_0'=4,'row_1'=2] {'col_0','col_1','row_0'}, dimensions={0} | all-to-all | bytes 2097152 | tf_op jit(solution)/shard_map/all_to_all | solution.py:28
  178.5 0.7 shard_map.124
  179.3 2.7 %collective-permute-start.16 = (f32[128,512]{1,0:T(8,128)S(1)}, f32[128,512]{1,0:T(8,128)S(1)}, u32[]{:S(2)}, u32[]{:S(2)}) collective-permute-start(f32[128,512]{1,0:T(8,128)S(1)} %get-tuple-element.101.total_ref), channel_id=1, source_target_pairs={{0,1},{1,0},{2,3},{3,2},{4,5},{5,4},{6,7},{7,6},{8,9},{9,8},{10,11... | collective-permute-start | bytes 786440 | tf_op jit(solution)/shard_map/ppermute | solution.py:24
  181.9 0.7 shard_map.125.total_ref
  183.1 0.9 shard_map.126.part_ref
  184.3 1.2 shard_map.127
  185.5 21.5 %all_to_all.39.coefficient_ref = bf16[64,64,128]{2,1,0:T(8,128)(2,1)S(1)} all-to-all(bf16[64,64,128]{2,1,0:T(8,128)(2,1)S(1)} %get-tuple-element.103), channel_id=1, replica_groups=mesh['col_0'=4,'col_1'=4,'row_0'=4,'row_1'=2] {'col_0','col_1','row_0'}, dimensions={0} | all-to-all | bytes 2097152 | tf_op jit(solution)/shard_map/all_to_all | solution.py:28
  207.0 0.7 shard_map.128
  207.8 2.3 %collective-permute-start.17 = (f32[128,512]{1,0:T(8,128)S(1)}, f32[128,512]{1,0:T(8,128)S(1)}, u32[]{:S(2)}, u32[]{:S(2)}) collective-permute-start(f32[128,512]{1,0:T(8,128)S(1)} %get-tuple-element.105), channel_id=1, source_target_pairs={{0,1},{1,0},{2,3},{3,2},{4,5},{5,4},{6,7},{7,6},{8,9},{9,8},{10,11... | collective-permute-start | bytes 786440 | tf_op jit(solution)/shard_map/ppermute | solution.py:24
  210.1 0.7 shard_map.129.total_ref
  211.3 0.9 shard_map.130
  212.2 12.7 %all_to_all.40 = f32[64,1,128]{2,1,0:T(1,128)S(1)} all-to-all(f32[64,1,128]{2,1,0:T(1,128)S(1)} %get-tuple-element.110), channel_id=1, replica_groups=mesh['col_0'=4,'col_1'=4,'row_0'=4,'row_1'=2] {'col_0','col_1','row_0'}, dimensions={0} | all-to-all | bytes 65536 | tf_op jit(solution)/shard_map/all_to_all | solution.py:28
  225.0 1.9 collective-permute-start.18
  226.9 0.8 collective-permute-done.18
  227.7 0.5 add.43
  (59 shorter events, 6.5 us)
Async XLA Ops:
  0.6 46.3 %collective-permute-start.5 = (bf16[512,64,128]{2,1,0:T(8,128)(2,1)}, bf16[512,64,128]{2,1,0:T(8,128)(2,1)}, u32[]{:S(2)}, u32[]{:S(2)}) collective-permute-start(bf16[512,64,128]{2,1,0:T(8,128)(2,1)} %param.10), channel_id=1, source_target_pairs={{0,1},{1,0},{2,3},{3,2},{4,5},{5,4},{6,7},{7,6},{8,9},{9,8},{10,11... | collective-permute-start | bytes 25165832 | tf_op jit(solution)/shard_map/ppermute | solution.py:24
  2.2 27.3 %copy-start = (f32[128,512]{1,0:T(8,128)S(1)}, f32[128,512]{1,0:T(8,128)}, u32[]{:S(2)}) copy-start(f32[128,512]{1,0:T(8,128)} %start_z_ref) | copy-start | bytes 786436
  2.2 27.8 %copy-start.5 = (s32[512]{0:T(512)S(1)}, s32[512]{0:T(512)}, u32[]{:S(2)}) copy-start(s32[512]{0:T(512)} %param.14) | copy-start | bytes 6148
  2.2 28.0 %copy-start.1 = (f32[128,512]{1,0:T(8,128)S(1)}, f32[128,512]{1,0:T(8,128)}, u32[]{:S(2)}) copy-start(f32[128,512]{1,0:T(8,128)} %start_m_ref) | copy-start | bytes 786436
  2.2 28.4 %copy-start.4 = (s32[64,64]{1,0:T(8,128)S(1)}, s32[64,64]{1,0:T(8,128)}, u32[]{:S(2)}) copy-start(s32[64,64]{1,0:T(8,128)} %ranks_ref.1) | copy-start | bytes 49156
  2.2 29.1 %copy-start.3 = (f32[512]{0:T(512)S(1)}, f32[512]{0:T(512)}, u32[]{:S(2)}) copy-start(f32[512]{0:T(512)} %param.13) | copy-start | bytes 6148
  2.2 44.6 %copy-start.6 = (f32[128]{0:T(128)S(1)}, f32[128]{0:T(128)}, u32[]{:S(2)}) copy-start(f32[128]{0:T(128)} %param.15) | copy-start | bytes 1540
  12.2 4.4 %collective-permute-start = (bf16[64,64,128]{2,1,0:T(8,128)(2,1)S(1)}, bf16[64,64,128]{2,1,0:T(8,128)(2,1)S(1)}, u32[]{:S(2)}, u32[]{:S(2)}) collective-permute-start(bf16[64,64,128]{2,1,0:T(8,128)(2,1)S(1)} %get-tuple-element.58), channel_id=1, source_target_pairs={{0,1},{1,0},{2,3},{3,2},{4,5},{5,4},{6,7},{7,6},{8,9},{9,8},{10,11... | collective-permute-start | bytes 3145736 | tf_op jit(solution)/shard_map/ppermute | solution.py:24
  17.9 50.7 %collective-permute-start.8 = (bf16[16,512,256]{2,1,0:T(8,128)(2,1)}, bf16[16,512,256]{2,1,0:T(8,128)(2,1)}, u32[]{:S(2)}, u32[]{:S(2)}) collective-permute-start(bf16[16,512,256]{2,1,0:T(8,128)(2,1)} %get-tuple-element.76), channel_id=1, source_target_pairs={{0,1},{1,0},{2,3},{3,2},{4,5},{5,4},{6,7},{7,6},{8,9},{9,8},{10,11... | collective-permute-start | bytes 12582920 | tf_op jit(solution)/shard_map/ppermute | solution.py:24
  18.2 28.5 %all-to-all-start = ((bf16[64,64,128]{2,1,0:T(8,128)(2,1)}), bf16[64,64,128]{2,1,0:T(8,128)(2,1)S(1)}, u32[]{:S(2)}, u32[]{:S(2)}) async-start(bf16[64,64,128]{2,1,0:T(8,128)(2,1)} %shard_map.104), calls=%async_computation | async-start | bytes 2097152 | tf_op jit(solution)/shard_map/all_to_all | solution.py:28
  29.5 3.0 %collective-permute-start.1 = (f32[128,512]{1,0:T(8,128)S(1)}, f32[128,512]{1,0:T(8,128)S(1)}, u32[]{:S(2)}, u32[]{:S(2)}) collective-permute-start(f32[128,512]{1,0:T(8,128)S(1)} %copy-done), channel_id=1, source_target_pairs={{0,1},{1,0},{2,3},{3,2},{4,5},{5,4},{6,7},{7,6},{8,9},{9,8},{10,11... | collective-permute-start | bytes 786440 | tf_op jit(solution)/shard_map/ppermute | solution.py:24
  30.0 1.3 collective-permute-start.4
  30.1 2.4 %collective-permute-start.2 = (f32[128,512]{1,0:T(8,128)S(1)}, f32[128,512]{1,0:T(8,128)S(1)}, u32[]{:S(2)}, u32[]{:S(2)}) collective-permute-start(f32[128,512]{1,0:T(8,128)S(1)} %copy-done.1), channel_id=1, source_target_pairs={{0,1},{1,0},{2,3},{3,2},{4,5},{5,4},{6,7},{7,6},{8,9},{9,8},{10,11... | collective-permute-start | bytes 786440 | tf_op jit(solution)/shard_map/ppermute | solution.py:24
  31.3 1.2 collective-permute-start.3
  62.6 3.5 %collective-permute-start.7 = (f32[128,512]{1,0:T(8,128)S(1)}, f32[128,512]{1,0:T(8,128)S(1)}, u32[]{:S(2)}, u32[]{:S(2)}) collective-permute-start(f32[128,512]{1,0:T(8,128)S(1)} %get-tuple-element.68.total_ref), channel_id=1, source_target_pairs={{0,1},{1,0},{2,3},{3,2},{4,5},{5,4},{6,7},{7,6},{8,9},{9,8},{10,11... | collective-permute-start | bytes 786440 | tf_op jit(solution)/shard_map/ppermute | solution.py:24
  65.7 1.6 collective-permute-start.6
  94.8 3.5 %collective-permute-start.10 = (f32[128,512]{1,0:T(8,128)S(1)}, f32[128,512]{1,0:T(8,128)S(1)}, u32[]{:S(2)}, u32[]{:S(2)}) collective-permute-start(f32[128,512]{1,0:T(8,128)S(1)} %get-tuple-element.81.total_ref), channel_id=1, source_target_pairs={{0,1},{1,0},{2,3},{3,2},{4,5},{5,4},{6,7},{7,6},{8,9},{9,8},{10,11... | collective-permute-start | bytes 786440 | tf_op jit(solution)/shard_map/ppermute | solution.py:24
  97.8 1.6 collective-permute-start.9
  122.8 3.6 %collective-permute-start.12 = (f32[128,512]{1,0:T(8,128)S(1)}, f32[128,512]{1,0:T(8,128)S(1)}, u32[]{:S(2)}, u32[]{:S(2)}) collective-permute-start(f32[128,512]{1,0:T(8,128)S(1)} %get-tuple-element.91.total_ref), channel_id=1, source_target_pairs={{0,1},{1,0},{2,3},{3,2},{4,5},{5,4},{6,7},{7,6},{8,9},{9,8},{10,11... | collective-permute-start | bytes 786440 | tf_op jit(solution)/shard_map/ppermute | solution.py:24
  126.0 1.6 collective-permute-start.11
  151.0 3.5 %collective-permute-start.14 = (f32[128,512]{1,0:T(8,128)S(1)}, f32[128,512]{1,0:T(8,128)S(1)}, u32[]{:S(2)}, u32[]{:S(2)}) collective-permute-start(f32[128,512]{1,0:T(8,128)S(1)} %get-tuple-element.93.total_ref), channel_id=1, source_target_pairs={{0,1},{1,0},{2,3},{3,2},{4,5},{5,4},{6,7},{7,6},{8,9},{9,8},{10,11... | collective-permute-start | bytes 786440 | tf_op jit(solution)/shard_map/ppermute | solution.py:24
  154.1 1.6 collective-permute-start.13
  179.3 3.8 %collective-permute-start.16 = (f32[128,512]{1,0:T(8,128)S(1)}, f32[128,512]{1,0:T(8,128)S(1)}, u32[]{:S(2)}, u32[]{:S(2)}) collective-permute-start(f32[128,512]{1,0:T(8,128)S(1)} %get-tuple-element.101.total_ref), channel_id=1, source_target_pairs={{0,1},{1,0},{2,3},{3,2},{4,5},{5,4},{6,7},{7,6},{8,9},{9,8},{10,11... | collective-permute-start | bytes 786440 | tf_op jit(solution)/shard_map/ppermute | solution.py:24
  182.6 1.6 collective-permute-start.15
  207.0 4.3 %copy-start.2 = (f32[128,512]{1,0:T(8,128)S(1)}, f32[128,512]{1,0:T(8,128)}, u32[]{:S(2)}) copy-start(f32[128,512]{1,0:T(8,128)} %get-tuple-element.54.z_ref) | copy-start | bytes 786436
  207.8 3.5 %collective-permute-start.17 = (f32[128,512]{1,0:T(8,128)S(1)}, f32[128,512]{1,0:T(8,128)S(1)}, u32[]{:S(2)}, u32[]{:S(2)}) collective-permute-start(f32[128,512]{1,0:T(8,128)S(1)} %get-tuple-element.105), channel_id=1, source_target_pairs={{0,1},{1,0},{2,3},{3,2},{4,5},{5,4},{6,7},{7,6},{8,9},{9,8},{10,11... | collective-permute-start | bytes 786440 | tf_op jit(solution)/shard_map/ppermute | solution.py:24
  225.0 2.7 %collective-permute-start.18 = (f32[128]{0:T(128)S(1)}, f32[128]{0:T(128)S(1)}, u32[]{:S(2)}, u32[]{:S(2)}) collective-permute-start(f32[128]{0:T(128)S(1)} %reduce_sum.9), channel_id=1, source_target_pairs={{0,1},{1,0},{2,3},{3,2},{4,5},{5,4},{6,7},{7,6},{8,9},{9,8},{10,11... | collective-permute-start | bytes 1544 | tf_op jit(solution)/shard_map/ppermute | solution.py:24

commit v6 on v5

--- a/solution.py
+++ b/solution.py
@@ -158,7 +158,7 @@
 def col_setup(factors, place, tile_ranks, z, coefficients):
     cells, tiles, ranked = factors.shape
     shape = (tiles // 4, cells, 2 * ranked)
-    parts = 8
+    parts = 16
     return pl.pallas_call(
         col_setup_kernel,
         in_specs=[SMEM, ANY, ANY, ANY],
@@ -246,7 +246,7 @@
 def row_setup(own, other, place):
     cells, tiles, ranked = own.shape
     shape = (2, tiles // 4, cells, 2 * ranked)
-    parts = 8
+    parts = 16
     rows = (cells * tiles, ranked)
     return pl.pallas_call(
         row_setup_kernel,
@@ -315,7 +315,7 @@
             jax.ShapeDtypeStruct((2, quads, cells, lanes), BF16),
             jax.ShapeDtypeStruct((2, quads, lanes, cells), BF16),
         ],
-        scratch_shapes=[pltpu.SemaphoreType.DMA((2, 8))],
+        scratch_shapes=[pltpu.SemaphoreType.DMA((2, 16))],
         compiler_params=pltpu.CompilerParams(vmem_limit_bytes=4 << 20),
         cost_estimate=pl.CostEstimate(
             flops=4_000_000_000, bytes_accessed=1 << 24, transcendentals=0

time: 229 us -> 233 us (1.017)
  Pallas kernels: 50.8 us -> 56.2 us
    pallas_call x1, Pallas kernels: 11 us -> 14 us  [row_setup(): pl.pallas_call(row_setup_kernel, in_specs=[SMEM, ANY, ANY], out_specs=ANY...]
  transfers between devices with their start and end apart: 20 -> 20, of which waited for: 15 -> 15; matrix products, arithmetic and copies ran while one was open for 0% -> 0% of each run, Pallas kernels for 16% -> 18%
where the time goes in v6:
time: 233 us; the launch traced here: 232 us
  blocking collectives  121 us (52%)
  Pallas kernels  56.2 us (24%)
  starting transfers between devices  31.3 us (13%)
  waiting for transfers between devices  21.8 us (9%)
    all_to_all x6, blocking collectives, spread(): return lax.all_to_all(value, CHIPS, split_axis=0, concat_axis=0, tiled=True)  121 us
    pallas_call x24, Pallas kernels, call(): pl.pallas_call(kernel, in_specs=specs, out_specs=[VMEM] * len(outs), out_...  21.9 us
    ppermute x19, starting transfers between devices, swap(): return lax.ppermute(value, CORE, [(0, 1), (1, 0)])  20.1 us
    all_to_all x1, waiting for transfers between devices, spread(): return lax.all_to_all(value, CHIPS, split_axis=0, concat_axis=0, tiled=True)  14.3 us
    pallas_call x1, Pallas kernels, row_setup(): pl.pallas_call(row_setup_kernel, in_specs=[SMEM, ANY, ANY], out_specs=ANY...  14 us
    pallas_call x1, Pallas kernels, col_setup(): pl.pallas_call(col_setup_kernel, in_specs=[SMEM, ANY, ANY, ANY], out_spec...  11.6 us
    all_to_all x1, starting transfers between devices, spread(): return lax.all_to_all(value, CHIPS, split_axis=0, concat_axis=0, tiled=True)  11.2 us
    pallas_call x2, Pallas kernels, merge(): pl.pallas_call(merge_kernel, in_specs=[ANY] * (1 + len(parts)), out_specs...  8.77 us
  transfers between devices with their start and end apart: 20, of which 15 were waited for; matrix products, arithmetic and copies ran while one was open for 0% of the time, Pallas kernels for 18%

profile of v6, /device:TPU:1, one launch (start us, length us, event | category | flops | bytes accessed | tf_op | source)
XLA Modules:
  0.0 232.5 jit_solution(17943807743758185142)
XLA Ops:
  0.6 1.5 collective-permute-start.5
  2.2 11.6 %shard_map.103 = (bf16[16,512,256]{2,1,0:T(8,128)(2,1)}, bf16[16,512,256]{2,1,0:T(8,128)(2,1)}, bf16[64,64,128]{2,1,0:T(8,128)(2,1)S(1)}, bf16[64,64,128]{2,1,0:T(8,128)(2,1)S(1)}) custom-call(s32[2]{0:T(128)S(1)} %pad_add_fusion.place_ref, bf16[32768,128]{1,0:T(8,128)(2,1)} %bitcast.21, s32[64,64]{1,0:T(8,128)} %ranks_ref.1, f32[128,512]{1,0:T(8,128)} %start_z_ref), custom_call_target="tpu_custom_call" | custom-call | flops 8000000000 | bytes 16777216 | tf_op jit(solution)/shard_map/pallas_call | solution.py:162
  13.9 2.7 %collective-permute-done.arrived_ref = bf16[64,64,128]{2,1,0:T(8,128)(2,1)S(1)} collective-permute-done((bf16[64,64,128]{2,1,0:T(8,128)(2,1)S(1)}, bf16[64,64,128]{2,1,0:T(8,128)(2,1)S(1)}, u32[]{:S(2)}, u32[]{:S(2)}) %collective-permute-start) | collective-permute-done | bytes 1048608 | tf_op jit(solution)/shard_map/ppermute | solution.py:24
  16.6 1.3 shard_map.104
  18.2 11.2 %all-to-all-start = ((bf16[64,64,128]{2,1,0:T(8,128)(2,1)}), bf16[64,64,128]{2,1,0:T(8,128)(2,1)S(1)}, u32[]{:S(2)}, u32[]{:S(2)}) async-start(bf16[64,64,128]{2,1,0:T(8,128)(2,1)} %shard_map.104), calls=%async_computation | async-start | bytes 2097152 | tf_op jit(solution)/shard_map/all_to_all | solution.py:28
  31.6 0.8 collective-permute-done.3
  32.5 14.3 %all-to-all-done.after_ref.coefficient_ref = bf16[64,64,128]{2,1,0:T(8,128)(2,1)S(1)} async-done(((bf16[64,64,128]{2,1,0:T(8,128)(2,1)}), bf16[64,64,128]{2,1,0:T(8,128)(2,1)S(1)}, u32[]{:S(2)}, u32[]{:S(2)}) %all-to-all-start) | async-done | bytes 1048608 | tf_op jit(solution)/shard_map/all_to_all | solution.py:28
  46.9 14.0 %shard_map.105.refs_0_ = bf16[2,16,512,256]{3,2,1,0:T(8,128)(2,1)} custom-call(s32[2]{0:T(128)S(1)} %pad_add_fusion.place_ref, bf16[32768,128]{1,0:T(8,128)(2,1)} %bitcast.22, bf16[32768,128]{1,0:T(8,128)(2,1)} %bitcast.8.other_raw_ref), custom_call_target="tpu_custom_call" | custom-call | flops 8000000000 | bytes 16777216 | tf_op jit(solution)/shard_map/pallas_call | solution.py:251
  60.9 4.4 %shard_map.106 = (bf16[2,16,512,256]{3,2,1,0:T(8,128)(2,1)S(1)}, bf16[2,16,256,512]{3,2,1,0:T(8,128)(2,1)S(1)}) custom-call(bf16[64,64,128]{2,1,0:T(8,128)(2,1)S(1)} %all-to-all-done.after_ref.coefficient_ref, bf16[2,16,512,256]{3,2,1,0:T(8,128)(2,1)} %shard_map.105.refs_0_), custom_call_target="tpu_custom_call" | custom-call | flops 4000000000 | bytes 16777216 | tf_op jit(solution)/shard_map/pallas_call | solution.py:310
  65.3 0.7 shard_map.107
  66.1 2.6 %collective-permute-start.7 = (f32[128,512]{1,0:T(8,128)S(1)}, f32[128,512]{1,0:T(8,128)S(1)}, u32[]{:S(2)}, u32[]{:S(2)}) collective-permute-start(f32[128,512]{1,0:T(8,128)S(1)} %get-tuple-element.68.total_ref), channel_id=1, source_target_pairs={{0,1},{1,0},{2,3},{3,2},{4,5},{5,4},{6,7},{7,6},{8,9},{9,8},{10,11... | collective-permute-start | bytes 786440 | tf_op jit(solution)/shard_map/ppermute | solution.py:24
  68.7 0.7 shard_map.108.total_ref
  69.8 0.9 shard_map.109.part_ref
  71.0 1.2 shard_map.110
  72.2 21.5 %all_to_all.35.after_ref.coefficient_ref = bf16[64,64,128]{2,1,0:T(8,128)(2,1)S(1)} all-to-all(bf16[64,64,128]{2,1,0:T(8,128)(2,1)S(1)} %get-tuple-element.77), channel_id=1, replica_groups=mesh['col_0'=4,'col_1'=4,'row_0'=4,'row_1'=2] {'col_0','col_1','row_0'}, dimensions={0} | all-to-all | bytes 2097152 | tf_op jit(solution)/shard_map/all_to_all | solution.py:28
  93.7 4.4 %shard_map.111 = (bf16[2,16,512,256]{3,2,1,0:T(8,128)(2,1)S(1)}, bf16[2,16,256,512]{3,2,1,0:T(8,128)(2,1)S(1)}) custom-call(bf16[64,64,128]{2,1,0:T(8,128)(2,1)S(1)} %all_to_all.35.after_ref.coefficient_ref, bf16[16,512,256]{2,1,0:T(8,128)(2,1)} %get-tuple-element.78.refs_0_, bf16[16,512,256]{2,1,0:T(8,128)(2,1)} %collective-permute-done.8.refs_1_), custom_call_target="tpu_custom_call" | custom-call | flops 4000000000 | bytes 16777216 | tf_op jit(solution)/shard_map/pallas_call | solution.py:310
  98.1 0.8 shard_map.112
  98.9 2.3 %collective-permute-start.10 = (f32[128,512]{1,0:T(8,128)S(1)}, f32[128,512]{1,0:T(8,128)S(1)}, u32[]{:S(2)}, u32[]{:S(2)}) collective-permute-start(f32[128,512]{1,0:T(8,128)S(1)} %get-tuple-element.81.total_ref), channel_id=1, source_target_pairs={{0,1},{1,0},{2,3},{3,2},{4,5},{5,4},{6,7},{7,6},{8,9},{9,8},{10,11... | collective-permute-start | bytes 786440 | tf_op jit(solution)/shard_map/ppermute | solution.py:24
  101.2 0.7 shard_map.113.total_ref
  102.4 1.0 shard_map.114
  103.7 1.2 shard_map.115
  104.9 21.6 %all_to_all.36.coefficient_ref = bf16[64,64,128]{2,1,0:T(8,128)(2,1)S(1)} all-to-all(bf16[64,64,128]{2,1,0:T(8,128)(2,1)S(1)} %get-tuple-element.90), channel_id=1, replica_groups=mesh['col_0'=4,'col_1'=4,'row_0'=4,'row_1'=2] {'col_0','col_1','row_0'}, dimensions={0} | all-to-all | bytes 2097152 | tf_op jit(solution)/shard_map/all_to_all | solution.py:28
  126.5 0.7 shard_map.116
  127.3 2.3 collective-permute-start.12
  129.6 0.7 shard_map.117.total_ref
  130.7 0.9 shard_map.118.part_ref
  131.9 1.1 shard_map.119
  133.0 21.5 %all_to_all.37.coefficient_ref = bf16[64,64,128]{2,1,0:T(8,128)(2,1)S(1)} all-to-all(bf16[64,64,128]{2,1,0:T(8,128)(2,1)S(1)} %shard_map.119), channel_id=1, replica_groups=mesh['col_0'=4,'col_1'=4,'row_0'=4,'row_1'=2] {'col_0','col_1','row_0'}, dimensions={0} | all-to-all | bytes 2097152 | tf_op jit(solution)/shard_map/all_to_all | solution.py:28
  154.5 0.7 shard_map.120
  155.3 2.3 %collective-permute-start.14 = (f32[128,512]{1,0:T(8,128)S(1)}, f32[128,512]{1,0:T(8,128)S(1)}, u32[]{:S(2)}, u32[]{:S(2)}) collective-permute-start(f32[128,512]{1,0:T(8,128)S(1)} %get-tuple-element.93.total_ref), channel_id=1, source_target_pairs={{0,1},{1,0},{2,3},{3,2},{4,5},{5,4},{6,7},{7,6},{8,9},{9,8},{10,11... | collective-permute-start | bytes 786440 | tf_op jit(solution)/shard_map/ppermute | solution.py:24
  157.6 0.7 shard_map.121.total_ref
  158.8 1.0 shard_map.122.part_ref
  160.0 1.4 shard_map.123
  161.3 21.4 %all_to_all.38.coefficient_ref = bf16[64,64,128]{2,1,0:T(8,128)(2,1)S(1)} all-to-all(bf16[64,64,128]{2,1,0:T(8,128)(2,1)S(1)} %get-tuple-element.100), channel_id=1, replica_groups=mesh['col_0'=4,'col_1'=4,'row_0'=4,'row_1'=2] {'col_0','col_1','row_0'}, dimensions={0} | all-to-all | bytes 2097152 | tf_op jit(solution)/shard_map/all_to_all | solution.py:28
  182.8 0.7 shard_map.124
  183.5 2.4 %collective-permute-start.16 = (f32[128,512]{1,0:T(8,128)S(1)}, f32[128,512]{1,0:T(8,128)S(1)}, u32[]{:S(2)}, u32[]{:S(2)}) collective-permute-start(f32[128,512]{1,0:T(8,128)S(1)} %get-tuple-element.101.total_ref), channel_id=1, source_target_pairs={{0,1},{1,0},{2,3},{3,2},{4,5},{5,4},{6,7},{7,6},{8,9},{9,8},{10,11... | collective-permute-start | bytes 786440 | tf_op jit(solution)/shard_map/ppermute | solution.py:24
  186.0 0.7 shard_map.125.total_ref
  187.1 0.9 shard_map.126.part_ref
  188.3 1.2 shard_map.127
  189.5 21.8 %all_to_all.39.coefficient_ref = bf16[64,64,128]{2,1,0:T(8,128)(2,1)S(1)} all-to-all(bf16[64,64,128]{2,1,0:T(8,128)(2,1)S(1)} %get-tuple-element.103), channel_id=1, replica_groups=mesh['col_0'=4,'col_1'=4,'row_0'=4,'row_1'=2] {'col_0','col_1','row_0'}, dimensions={0} | all-to-all | bytes 2097152 | tf_op jit(solution)/shard_map/all_to_all | solution.py:28
  211.3 0.8 shard_map.128
  212.0 2.3 %collective-permute-start.17 = (f32[128,512]{1,0:T(8,128)S(1)}, f32[128,512]{1,0:T(8,128)S(1)}, u32[]{:S(2)}, u32[]{:S(2)}) collective-permute-start(f32[128,512]{1,0:T(8,128)S(1)} %get-tuple-element.105), channel_id=1, source_target_pairs={{0,1},{1,0},{2,3},{3,2},{4,5},{5,4},{6,7},{7,6},{8,9},{9,8},{10,11... | collective-permute-start | bytes 786440 | tf_op jit(solution)/shard_map/ppermute | solution.py:24
  214.4 0.7 shard_map.129.total_ref
  215.5 0.9 shard_map.130
  216.5 12.7 %all_to_all.40 = f32[64,1,128]{2,1,0:T(1,128)S(1)} all-to-all(f32[64,1,128]{2,1,0:T(1,128)S(1)} %get-tuple-element.110), channel_id=1, replica_groups=mesh['col_0'=4,'col_1'=4,'row_0'=4,'row_1'=2] {'col_0','col_1','row_0'}, dimensions={0} | all-to-all | bytes 65536 | tf_op jit(solution)/shard_map/all_to_all | solution.py:28
  229.3 1.9 collective-permute-start.18
  231.1 0.8 collective-permute-done.18
  232.0 0.5 add.43
  (59 shorter events, 6.7 us)
Async XLA Ops:
  0.6 46.3 %collective-permute-start.5 = (bf16[512,64,128]{2,1,0:T(8,128)(2,1)}, bf16[512,64,128]{2,1,0:T(8,128)(2,1)}, u32[]{:S(2)}, u32[]{:S(2)}) collective-permute-start(bf16[512,64,128]{2,1,0:T(8,128)(2,1)} %param.10), channel_id=1, source_target_pairs={{0,1},{1,0},{2,3},{3,2},{4,5},{5,4},{6,7},{7,6},{8,9},{9,8},{10,11... | collective-permute-start | bytes 25165832 | tf_op jit(solution)/shard_map/ppermute | solution.py:24
  2.2 27.3 %copy-start = (f32[128,512]{1,0:T(8,128)S(1)}, f32[128,512]{1,0:T(8,128)}, u32[]{:S(2)}) copy-start(f32[128,512]{1,0:T(8,128)} %start_z_ref) | copy-start | bytes 786436
  2.2 27.8 %copy-start.5 = (s32[512]{0:T(512)S(1)}, s32[512]{0:T(512)}, u32[]{:S(2)}) copy-start(s32[512]{0:T(512)} %param.14) | copy-start | bytes 6148
  2.2 28.0 %copy-start.1 = (f32[128,512]{1,0:T(8,128)S(1)}, f32[128,512]{1,0:T(8,128)}, u32[]{:S(2)}) copy-start(f32[128,512]{1,0:T(8,128)} %start_m_ref) | copy-start | bytes 786436
  2.2 28.4 %copy-start.4 = (s32[64,64]{1,0:T(8,128)S(1)}, s32[64,64]{1,0:T(8,128)}, u32[]{:S(2)}) copy-start(s32[64,64]{1,0:T(8,128)} %ranks_ref.1) | copy-start | bytes 49156
  2.2 29.1 %copy-start.3 = (f32[512]{0:T(512)S(1)}, f32[512]{0:T(512)}, u32[]{:S(2)}) copy-start(f32[512]{0:T(512)} %param.13) | copy-start | bytes 6148
  2.2 44.6 %copy-start.6 = (f32[128]{0:T(128)S(1)}, f32[128]{0:T(128)}, u32[]{:S(2)}) copy-start(f32[128]{0:T(128)} %param.15) | copy-start | bytes 1540
  13.8 2.8 %collective-permute-start = (bf16[64,64,128]{2,1,0:T(8,128)(2,1)S(1)}, bf16[64,64,128]{2,1,0:T(8,128)(2,1)S(1)}, u32[]{:S(2)}, u32[]{:S(2)}) collective-permute-start(bf16[64,64,128]{2,1,0:T(8,128)(2,1)S(1)} %get-tuple-element.58), channel_id=1, source_target_pairs={{0,1},{1,0},{2,3},{3,2},{4,5},{5,4},{6,7},{7,6},{8,9},{9,8},{10,11... | collective-permute-start | bytes 3145736 | tf_op jit(solution)/shard_map/ppermute | solution.py:24
  17.9 54.3 %collective-permute-start.8 = (bf16[16,512,256]{2,1,0:T(8,128)(2,1)}, bf16[16,512,256]{2,1,0:T(8,128)(2,1)}, u32[]{:S(2)}, u32[]{:S(2)}) collective-permute-start(bf16[16,512,256]{2,1,0:T(8,128)(2,1)} %get-tuple-element.76), channel_id=1, source_target_pairs={{0,1},{1,0},{2,3},{3,2},{4,5},{5,4},{6,7},{7,6},{8,9},{9,8},{10,11... | collective-permute-start | bytes 12582920 | tf_op jit(solution)/shard_map/ppermute | solution.py:24
  18.2 28.5 %all-to-all-start = ((bf16[64,64,128]{2,1,0:T(8,128)(2,1)}), bf16[64,64,128]{2,1,0:T(8,128)(2,1)S(1)}, u32[]{:S(2)}, u32[]{:S(2)}) async-start(bf16[64,64,128]{2,1,0:T(8,128)(2,1)} %shard_map.104), calls=%async_computation | async-start | bytes 2097152 | tf_op jit(solution)/shard_map/all_to_all | solution.py:28
  29.5 3.0 %collective-permute-start.1 = (f32[128,512]{1,0:T(8,128)S(1)}, f32[128,512]{1,0:T(8,128)S(1)}, u32[]{:S(2)}, u32[]{:S(2)}) collective-permute-start(f32[128,512]{1,0:T(8,128)S(1)} %copy-done), channel_id=1, source_target_pairs={{0,1},{1,0},{2,3},{3,2},{4,5},{5,4},{6,7},{7,6},{8,9},{9,8},{10,11... | collective-permute-start | bytes 786440 | tf_op jit(solution)/shard_map/ppermute | solution.py:24
  30.0 1.3 collective-permute-start.4
  30.1 2.4 %collective-permute-start.2 = (f32[128,512]{1,0:T(8,128)S(1)}, f32[128,512]{1,0:T(8,128)S(1)}, u32[]{:S(2)}, u32[]{:S(2)}) collective-permute-start(f32[128,512]{1,0:T(8,128)S(1)} %copy-done.1), channel_id=1, source_target_pairs={{0,1},{1,0},{2,3},{3,2},{4,5},{5,4},{6,7},{7,6},{8,9},{9,8},{10,11... | collective-permute-start | bytes 786440 | tf_op jit(solution)/shard_map/ppermute | solution.py:24
  31.3 1.2 collective-permute-start.3
  66.1 3.7 %collective-permute-start.7 = (f32[128,512]{1,0:T(8,128)S(1)}, f32[128,512]{1,0:T(8,128)S(1)}, u32[]{:S(2)}, u32[]{:S(2)}) collective-permute-start(f32[128,512]{1,0:T(8,128)S(1)} %get-tuple-element.68.total_ref), channel_id=1, source_target_pairs={{0,1},{1,0},{2,3},{3,2},{4,5},{5,4},{6,7},{7,6},{8,9},{9,8},{10,11... | collective-permute-start | bytes 786440 | tf_op jit(solution)/shard_map/ppermute | solution.py:24
  69.4 1.6 collective-permute-start.6
  98.9 3.5 %collective-permute-start.10 = (f32[128,512]{1,0:T(8,128)S(1)}, f32[128,512]{1,0:T(8,128)S(1)}, u32[]{:S(2)}, u32[]{:S(2)}) collective-permute-start(f32[128,512]{1,0:T(8,128)S(1)} %get-tuple-element.81.total_ref), channel_id=1, source_target_pairs={{0,1},{1,0},{2,3},{3,2},{4,5},{5,4},{6,7},{7,6},{8,9},{9,8},{10,11... | collective-permute-start | bytes 786440 | tf_op jit(solution)/shard_map/ppermute | solution.py:24
  101.9 1.8 collective-permute-start.9
  127.3 3.5 %collective-permute-start.12 = (f32[128,512]{1,0:T(8,128)S(1)}, f32[128,512]{1,0:T(8,128)S(1)}, u32[]{:S(2)}, u32[]{:S(2)}) collective-permute-start(f32[128,512]{1,0:T(8,128)S(1)} %get-tuple-element.91.total_ref), channel_id=1, source_target_pairs={{0,1},{1,0},{2,3},{3,2},{4,5},{5,4},{6,7},{7,6},{8,9},{9,8},{10,11... | collective-permute-start | bytes 786440 | tf_op jit(solution)/shard_map/ppermute | solution.py:24
  130.3 1.6 collective-permute-start.11
  155.3 3.5 %collective-permute-start.14 = (f32[128,512]{1,0:T(8,128)S(1)}, f32[128,512]{1,0:T(8,128)S(1)}, u32[]{:S(2)}, u32[]{:S(2)}) collective-permute-start(f32[128,512]{1,0:T(8,128)S(1)} %get-tuple-element.93.total_ref), channel_id=1, source_target_pairs={{0,1},{1,0},{2,3},{3,2},{4,5},{5,4},{6,7},{7,6},{8,9},{9,8},{10,11... | collective-permute-start | bytes 786440 | tf_op jit(solution)/shard_map/ppermute | solution.py:24
  158.3 1.6 collective-permute-start.13
  183.5 3.6 %collective-permute-start.16 = (f32[128,512]{1,0:T(8,128)S(1)}, f32[128,512]{1,0:T(8,128)S(1)}, u32[]{:S(2)}, u32[]{:S(2)}) collective-permute-start(f32[128,512]{1,0:T(8,128)S(1)} %get-tuple-element.101.total_ref), channel_id=1, source_target_pairs={{0,1},{1,0},{2,3},{3,2},{4,5},{5,4},{6,7},{7,6},{8,9},{9,8},{10,11... | collective-permute-start | bytes 786440 | tf_op jit(solution)/shard_map/ppermute | solution.py:24
  186.7 1.6 collective-permute-start.15
  211.3 4.3 %copy-start.2 = (f32[128,512]{1,0:T(8,128)S(1)}, f32[128,512]{1,0:T(8,128)}, u32[]{:S(2)}) copy-start(f32[128,512]{1,0:T(8,128)} %get-tuple-element.54.z_ref) | copy-start | bytes 786436
  212.0 3.5 %collective-permute-start.17 = (f32[128,512]{1,0:T(8,128)S(1)}, f32[128,512]{1,0:T(8,128)S(1)}, u32[]{:S(2)}, u32[]{:S(2)}) collective-permute-start(f32[128,512]{1,0:T(8,128)S(1)} %get-tuple-element.105), channel_id=1, source_target_pairs={{0,1},{1,0},{2,3},{3,2},{4,5},{5,4},{6,7},{7,6},{8,9},{9,8},{10,11... | collective-permute-start | bytes 786440 | tf_op jit(solution)/shard_map/ppermute | solution.py:24
  229.3 2.7 %collective-permute-start.18 = (f32[128]{0:T(128)S(1)}, f32[128]{0:T(128)S(1)}, u32[]{:S(2)}, u32[]{:S(2)}) collective-permute-start(f32[128]{0:T(128)S(1)} %reduce_sum.9), channel_id=1, source_target_pairs={{0,1},{1,0},{2,3},{3,2},{4,5},{5,4},{6,7},{7,6},{8,9},{9,8},{10,11... | collective-permute-start | bytes 1544 | tf_op jit(solution)/shard_map/ppermute | solution.py:24
